TPU v7x, 32 devices: a whole 2x2x4 slice. The times are simulated.
32 devices in a mesh: rows: 4 (over z), ty: 4 (over x, core), tx: 2 (over y).
Axes of the slice: x: 2, y: 2, z: 4, core: 2. Of those that a mesh axis runs over, the one named last changes fastest.
Arguments:
- latent: bfloat16 [12, 32, 32, 16], P('rows', 'ty', 'tx'), may hold values from -6 to 6
- skip_input: bfloat16 [12, 32, 32, 768], P('rows', 'ty', 'tx'), may hold values from -6 to 6
- segment_ids: int32 [12, 32, 32], P('rows'), may hold values from 0 to 2, as said below
- embed_weight: bfloat16 [768, 16], replicated, may hold values from -1.5 to 1.5
- embed_bias: bfloat16 [768], replicated, may hold values from -1.75 to 1.75
- skip_weight: bfloat16 [1536, 768], replicated, may hold values from -0.15625 to 0.15625
- skip_bias: bfloat16 [768], replicated, may hold values from -1.75 to 1.75
- norm1_gain: bfloat16 [768], replicated, may hold values from 0.5 to 1.5
- norm1_bias: bfloat16 [768], replicated, may hold values from -1.75 to 1.75
- qkv_weight: bfloat16 [768, 2304], replicated, may hold values from -0.21875 to 0.21875
- proj_weight: bfloat16 [768, 768], replicated, may hold values from -0.875 to 0.875
- proj_bias: bfloat16 [768], replicated, may hold values from -1.75 to 1.75
- norm2_gain: bfloat16 [768], replicated, may hold values from 0.5 to 1.5
- norm2_bias: bfloat16 [768], replicated, may hold values from -1.75 to 1.75
- fc1_weight: bfloat16 [768, 3072], replicated, may hold values from -0.21875 to 0.21875
- fc1_bias: bfloat16 [3072], replicated, may hold values from -1.75 to 1.75
- fc2_weight: bfloat16 [3072, 768], replicated, may hold values from -0.109375 to 0.109375
- fc2_bias: bfloat16 [768], replicated, may hold values from -1.75 to 1.75
- conv_weight: bfloat16 [768, 144], replicated, may hold values from -0.125 to 0.125
- cotangent: bfloat16 [12, 32, 32, 16], P('rows', 'ty', 'tx'), may hold values from -6 to 6
Outputs:
- output: bfloat16 [12, 32, 32, 16], P('rows', 'ty', 'tx')
- skip_input_grad: bfloat16 [12, 32, 32, 768], P('rows', 'ty', 'tx')
- embed_weight_grad: float32 [768, 16], P('rows')
- embed_bias_grad: float32 [768], P('rows')
- skip_weight_grad: float32 [1536, 768], P('rows')
- skip_bias_grad: float32 [768], P('rows')
- norm1_gain_grad: float32 [768], P('rows')
- norm1_bias_grad: float32 [768], P('rows')
- qkv_weight_grad: float32 [768, 2304], P('rows')
- proj_weight_grad: float32 [768, 768], P('rows')
- proj_bias_grad: float32 [768], P('rows')
- norm2_gain_grad: float32 [768], P('rows')
- norm2_bias_grad: float32 [768], P('rows')
- fc1_weight_grad: float32 [768, 3072], P('rows')
- fc1_bias_grad: float32 [3072], P('rows')
- fc2_weight_grad: float32 [3072, 768], P('rows')
- fc2_bias_grad: float32 [768], P('rows')
- conv_weight_grad: float32 [768, 144], P('rows')
Inputs may be any that keep to these rules, and one draw needn't show every extreme that they name: `segment_ids`: each row's 32 x 32 grid is cut into three rectangular images: id 0 fills every grid row up to a left width, ids 1 and 2 fill the remaining columns above and below a top height; the width and the height are drawn for each row among the multiples of 4 from 8 to 24.
All inputs are finite; a program needn't handle non-finite values.
Results may differ from a plain program's by a relative error of at most 0.014.
Values may be sent and summed in bfloat16 or wider, within the bound.
A program may use at most 256 MiB of HBM per device.

v0:
```python
import jax
import jax.numpy as jnp
from jax import lax
from jax.sharding import PartitionSpec as P

HEADS = 12


norm_eps = 1e-05
masked_score = -1e30


def with_halo(x, sides, width):
    for axis, dim in sides:
        peers, length = (lax.axis_size(axis), x.shape[dim])
        up = [(i, (i + 1) % peers) for i in range(peers - 1)]
        down = [(j, i) for i, j in up]
        last = lax.slice_in_dim(x, length - width, length, axis=dim)
        first = lax.slice_in_dim(x, 0, width, axis=dim)
        before = lax.ppermute(last, axis, up)
        after = lax.ppermute(first, axis, down)
        x = jnp.concatenate([before, x, after], axis=dim)
    return x


def layer_norm(values, norm_gain, norm_bias):
    average = jnp.mean(values, axis=-1, keepdims=True)
    centred = values - average
    variance = jnp.mean(centred * centred, axis=-1, keepdims=True)
    return centred * lax.rsqrt(variance + norm_eps) * norm_gain + norm_bias


def gelu_exact(values):
    return jax.nn.gelu(values, approximate=False)


def product(former, latter, pattern):
    return jnp.einsum(pattern, former, latter, preferred_element_type=jnp.float32)


def shards(
    latent,
    skip_input,
    segment_ids,
    embed_weight,
    embed_bias,
    skip_weight,
    skip_bias,
    norm1_gain,
    norm1_bias,
    qkv_weight,
    proj_weight,
    proj_bias,
    norm2_gain,
    norm2_bias,
    fc1_weight,
    fc1_bias,
    fc2_weight,
    fc2_bias,
    conv_weight,
    cotangent,
):
    row_count, tile_height, tile_width, model_width = skip_input.shape
    patch_width = latent.shape[3]
    grid_side = segment_ids.shape[1]
    tile_tokens = tile_height * tile_width
    token_count = row_count * tile_tokens
    row_tokens = grid_side * grid_side
    head_count = HEADS
    head_size = model_width // head_count
    score_scale = head_size ** (-0.5)
    band_count = lax.axis_size("ty")
    column_count = lax.axis_size("tx")
    band_index = lax.axis_index("ty")
    column_index = lax.axis_index("tx")
    padded_ids = jnp.pad(segment_ids, ((0, 0), (1, 1), (1, 1)), constant_values=-1)
    window_ids = lax.dynamic_slice(
        padded_ids,
        (jnp.int32(0), band_index * tile_height, column_index * tile_width),
        (row_count, tile_height + 2, tile_width + 2),
    )
    own_ids = window_ids[:, 1:-1, 1:-1]
    shifts = [(down_step, side_step) for down_step in (-1, 0, 1) for side_step in (-1, 0, 1)]
    same_place = jnp.stack(
        [
            window_ids[
                :,
                1 + down_step : 1 + down_step + tile_height,
                1 + side_step : 1 + side_step + tile_width,
            ]
            == own_ids
            for down_step, side_step in shifts
        ],
        axis=-1,
    )
    key_ids = segment_ids.reshape(row_count, band_count, tile_height, column_count, tile_width)
    key_ids = key_ids.transpose(0, 1, 3, 2, 4).reshape(row_count, row_tokens)
    own_flat = own_ids.reshape(row_count, tile_tokens)
    allowed = own_flat[:, None, :, None] == key_ids[:, None, None, :]
    flat_latent = latent.reshape(token_count, patch_width)
    flat_skip = skip_input.reshape(token_count, model_width)
    embedded = product(flat_latent, embed_weight, "tc,dc->td") + embed_bias.astype(jnp.float32)
    joined = jnp.concatenate([embedded.astype(jnp.bfloat16), flat_skip], axis=1)
    stream = product(joined, skip_weight, "tj,jd->td") + skip_bias.astype(jnp.float32)
    normed, norm1_back = jax.vjp(
        layer_norm, stream, norm1_gain.astype(jnp.float32), norm1_bias.astype(jnp.float32)
    )
    normed_low = normed.astype(jnp.bfloat16)
    projected = product(normed_low, qkv_weight, "td,de->te").astype(jnp.bfloat16)
    queries = projected[:, :model_width].reshape(row_count, tile_tokens, head_count, head_size)
    local_pairs = projected[:, model_width:].reshape(row_count, tile_tokens, 2 * model_width)
    row_pairs = lax.all_gather(local_pairs, ("ty", "tx"), axis=1, tiled=True)
    row_keys = row_pairs[:, :, :model_width].reshape(row_count, row_tokens, head_count, head_size)
    values = row_pairs[:, :, model_width:].reshape(row_count, row_tokens, head_count, head_size)

    def masked_scores():
        raw_scores = product(queries, row_keys, "rqhd,rkhd->rhqk") * score_scale
        return jnp.where(allowed, raw_scores, masked_score)

    scores = masked_scores()
    row_peak = jnp.max(scores, axis=-1, keepdims=True)
    exponents = jnp.exp(scores - row_peak)
    row_total = jnp.sum(exponents, axis=-1, keepdims=True)
    attention_weights = exponents / row_total
    log_total = row_peak + jnp.log(row_total)
    attended = product(attention_weights.astype(jnp.bfloat16), values, "rhqk,rkhd->rqhd")
    attended = attended.astype(jnp.bfloat16).reshape(token_count, model_width)
    stream_mid = (
        stream + product(attended, proj_weight, "td,de->te") + proj_bias.astype(jnp.float32)
    )
    normed_mid, norm2_back = jax.vjp(
        layer_norm, stream_mid, norm2_gain.astype(jnp.float32), norm2_bias.astype(jnp.float32)
    )
    normed_mid_low = normed_mid.astype(jnp.bfloat16)
    hidden = product(normed_mid_low, fc1_weight, "td,df->tf") + fc1_bias.astype(jnp.float32)
    activated, gelu_back = jax.vjp(gelu_exact, hidden)
    active_low = activated.astype(jnp.bfloat16)
    stream_out = (
        stream_mid + product(active_low, fc2_weight, "tf,fd->td") + fc2_bias.astype(jnp.float32)
    )
    conv_in = stream_out.astype(jnp.bfloat16).reshape(
        row_count, tile_height, tile_width, model_width
    )
    rimmed = with_halo(conv_in, (("ty", 1), ("tx", 2)), 1)
    tap_values = product(rimmed, conv_weight, "ryxc,ck->ryxk")
    conv_sum = jnp.zeros((row_count, tile_height, tile_width, patch_width), jnp.float32)
    for offset_index, (down_step, side_step) in enumerate(shifts):
        window = tap_values[
            :,
            1 + down_step : 1 + down_step + tile_height,
            1 + side_step : 1 + side_step + tile_width,
            offset_index * patch_width : (offset_index + 1) * patch_width,
        ]
        conv_sum = conv_sum + jnp.where(
            same_place[..., offset_index : offset_index + 1], window, 0.0
        )
    output = conv_sum.astype(jnp.bfloat16)
    rim_cotangent = with_halo(cotangent, (("ty", 1), ("tx", 2)), 1)
    spread_parts = []
    for offset_index, (down_step, side_step) in enumerate(shifts):
        mirror = 8 - offset_index
        window = rim_cotangent[
            :,
            1 - down_step : 1 - down_step + tile_height,
            1 - side_step : 1 - side_step + tile_width,
            :,
        ]
        spread_parts.append(jnp.where(same_place[..., mirror : mirror + 1], window, 0.0))
    spread = jnp.concatenate(spread_parts, axis=-1)
    out_grad = product(spread, conv_weight, "ryxk,ck->ryxc").reshape(token_count, model_width)
    conv_weight_grad = product(conv_in, spread, "ryxc,ryxk->ck")
    out_low = out_grad.astype(jnp.bfloat16)
    fc2_bias_grad = jnp.sum(out_grad, axis=0)
    fc2_weight_grad = product(active_low, out_low, "tf,td->fd")
    active_grad = product(out_low, fc2_weight, "td,fd->tf")
    (hidden_grad,) = gelu_back(active_grad)
    fc1_bias_grad = jnp.sum(hidden_grad, axis=0)
    hidden_low = hidden_grad.astype(jnp.bfloat16)
    fc1_weight_grad = product(normed_mid_low, hidden_low, "td,tf->df")
    normed_mid_grad = product(hidden_low, fc1_weight, "tf,df->td")
    mid_part, norm2_gain_grad, norm2_bias_grad = norm2_back(normed_mid_grad)
    mid_grad = out_grad + mid_part
    mid_low = mid_grad.astype(jnp.bfloat16)
    proj_bias_grad = jnp.sum(mid_grad, axis=0)
    proj_weight_grad = product(attended, mid_low, "td,te->de")
    attended_grad = product(mid_low, proj_weight, "te,de->td").astype(jnp.bfloat16)
    attended_grad = attended_grad.reshape(row_count, tile_tokens, head_count, head_size)
    weights_again = jnp.exp(masked_scores() - log_total)
    weights_grad = product(attended_grad, values, "rqhd,rkhd->rhqk")
    weighted_sum = jnp.sum(weights_again * weights_grad, axis=-1, keepdims=True)
    score_grad = (weights_again * (weights_grad - weighted_sum)).astype(jnp.bfloat16)
    query_grad = product(score_grad, row_keys, "rhqk,rkhd->rqhd") * score_scale
    value_grad = product(weights_again.astype(jnp.bfloat16), attended_grad, "rhqk,rqhd->rkhd")
    key_grad = product(score_grad, queries, "rhqk,rqhd->rkhd") * score_scale
    pair_terms = jnp.concatenate(
        [
            key_grad.reshape(row_count, row_tokens, model_width),
            value_grad.reshape(row_count, row_tokens, model_width),
        ],
        axis=2,
    )
    own_pairs = lax.psum_scatter(
        pair_terms.astype(jnp.bfloat16), ("ty", "tx"), scatter_dimension=1, tiled=True
    ).astype(jnp.float32)
    projected_grad = jnp.concatenate(
        [
            query_grad.reshape(token_count, model_width),
            own_pairs.reshape(token_count, 2 * model_width),
        ],
        axis=1,
    )
    projected_grad = projected_grad.astype(jnp.bfloat16)
    qkv_weight_grad = product(normed_low, projected_grad, "td,te->de")
    normed_grad = product(projected_grad, qkv_weight, "te,de->td")
    stream_part, norm1_gain_grad, norm1_bias_grad = norm1_back(normed_grad)
    stream_grad = mid_grad + stream_part
    stream_low = stream_grad.astype(jnp.bfloat16)
    skip_bias_grad = jnp.sum(stream_grad, axis=0)
    skip_weight_grad = product(joined, stream_low, "tj,td->jd")
    joined_grad = product(stream_low, skip_weight, "td,jd->tj")
    skip_input_grad = joined_grad[:, model_width:].astype(jnp.bfloat16)
    skip_input_grad = skip_input_grad.reshape(row_count, tile_height, tile_width, model_width)
    embedded_grad = joined_grad[:, :model_width]
    embed_bias_grad = jnp.sum(embedded_grad, axis=0)
    embed_weight_grad = product(embedded_grad.astype(jnp.bfloat16), flat_latent, "td,tc->dc")
    local_grads = (
        embed_weight_grad,
        embed_bias_grad,
        skip_weight_grad,
        skip_bias_grad,
        norm1_gain_grad,
        norm1_bias_grad,
        qkv_weight_grad,
        proj_weight_grad,
        proj_bias_grad,
        norm2_gain_grad,
        norm2_bias_grad,
        fc1_weight_grad,
        fc1_bias_grad,
        fc2_weight_grad,
        fc2_bias_grad,
        conv_weight_grad,
    )
    group_count = lax.axis_size("rows")
    tile_count = band_count * column_count
    table = jnp.concatenate([entry.reshape(group_count, -1) for entry in local_grads], axis=1)
    column_total = table.shape[1]
    padded_columns = -(-column_total // tile_count) * tile_count
    piece_width = padded_columns // tile_count
    table = table.reshape(group_count, tile_count, piece_width)
    shares = lax.psum_scatter(
        table.reshape(group_count * tile_count, piece_width),
        ("rows", "ty", "tx"),
        scatter_dimension=0,
        tiled=True,
    )
    summed = (
        lax.all_gather(shares.astype(jnp.bfloat16), ("ty", "tx"), axis=0, tiled=True)
        .astype(shares.dtype)
        .reshape(-1)
    )
    totals = []
    start_at = 0
    for entry in local_grads:
        length = entry.size // group_count
        shard_shape = (entry.shape[0] // group_count,) + entry.shape[1:]
        totals.append(summed[start_at : start_at + length].reshape(shard_shape))
        start_at = start_at + length
    return (output, skip_input_grad) + tuple(totals)


def solution(mesh):
    return jax.shard_map(
        shards,
        mesh=mesh,
        in_specs=(
            P("rows", "ty", "tx", None),
            P("rows", "ty", "tx", None),
            P("rows", None, None),
            P(),
            P(),
            P(),
            P(),
            P(),
            P(),
            P(),
            P(),
            P(),
            P(),
            P(),
            P(),
            P(),
            P(),
            P(),
            P(),
            P("rows", "ty", "tx", None),
        ),
        out_specs=(
            P("rows", "ty", "tx", None),
            P("rows", "ty", "tx", None),
            P("rows", None),
            P("rows"),
            P("rows", None),
            P("rows"),
            P("rows"),
            P("rows"),
            P("rows", None),
            P("rows", None),
            P("rows"),
            P("rows"),
            P("rows"),
            P("rows", None),
            P("rows"),
            P("rows", None),
            P("rows"),
            P("rows", None),
        ),
        check_vma=False,
    )
```

profile of v0, /device:TPU:0, one launch (start us, length us, event | category | flops | bytes accessed | tf_op | source)
XLA Modules:
  0.0 1438.8 jit_solution(2606226817480569863)
XLA Ops:
  12.3 3.0 fusion.103
  21.1 3.0 collective-permute-start.4
  38.1 4.9 collective-permute-start.7
  46.2 1.9 slice.244
  49.4 2.8 reshape.307
  52.2 2.9 copy.66
  57.1 2.5 fusion.71
  59.6 2.0 concatenate.51
  65.4 16.0 %all-gather.4.cloned.1.call-done = bf16[3,1024,1536]{2,1,0:T(8,128)(2,1)} async-done(((bf16[3,128,1536]{2,1,0:T(8,128)(2,1)}), bf16[3,1024,1536]{2,1,0:T(8,128)(2,1)}) %all-gather.4.cloned.1.call-update) | async-done | bytes 9437200 | tf_op jit(solution)/shard_map/all_gather | solution.py:112
  81.4 8.0 fusion.96
  89.5 6.6 copy.62
  96.1 6.6 copy.65
  102.7 13.0 fusion.104
  115.7 10.0 fusion
  127.2 10.2 fusion.21
  139.1 2.1 convolution_add_fusion
  141.3 15.0 %fusion.90 = (f32[3072]{0:T(1024)}, bf16[384,3072]{1,0:T(8,128)(2,1)S(1)}, f32[384,3072]{1,0:T(8,128)}) fusion(f32[384,3072]{1,0:T(8,128)S(1)} %convolution_add_fusion, bf16[384,768]{1,0:T(8,128)(2,1)S(1)} %copy-done.19, bf16[3072,768]{1,0:T(8,128)(2,1)S(1)} %bitcast.107), kind=kOutput, calls=%fused_computation.186 | convolution fusion | flops 1898050560 | bytes 17117184 | tf_op jit(solution)/shard_map/td,fd->tf/dot_general | solution.py:38
  156.3 2.8 multiply_reduce_fusion.1
  163.0 2.8 reshape.308
  165.8 2.6 copy.69
  168.4 12.1 fusion.12
  180.4 14.7 %multiply_reduce_fusion = (f32[3,12,128]{2,1,0:T(8,128)}, f32[3,12,128,1024]{3,2,1,0:T(8,128)}) fusion(f32[3,12,128,1024]{3,2,1,0:T(8,128)} %get-tuple-element.117, f32[3,12,128]{2,1,0:T(8,128)S(1)} %copy-done.33, bf16[3,128,12,64]{1,3,2,0:T(8,128)(2,1)S(1)} %copy-done.13, bf16[3,1024,12,64]{1,3,2,0:T(8,128)(2,1)} %bitcast.88), kind=kOutput, calls=%fused_computation.1 | convolution fusion | flops 618130944 | bytes 43094016 | tf_op jit(solution)/shard_map/rqhd,rkhd->rhqk/dot_general | solution.py:38
  195.2 6.6 copy.74
  201.8 13.0 multiply_convert_fusion
  214.8 3.5 multiply_convert_fusion.1
  219.8 6.6 copy.73
  226.4 9.0 pad_maximum_fusion
  238.2 10.3 fusion.22
  248.5 2.7 copy.83
  251.2 3.1 reshape.306
  254.3 3.7 fusion.42
  258.0 4.4 reshape.283
  266.4 8.5 fusion.23
  274.9 14.0 reshape.287
  289.5 5.2 multiply_convert_fusion.2
  296.1 5.1 fusion.106
  301.2 12.2 reshape.289
  313.4 5.4 fusion.17
  320.9 2.5 reshape.291
  323.4 4.3 multiply_reduce_fusion.2
  332.6 3.6 fusion.40
  336.2 5.5 fusion.27
  342.6 6.9 reshape.278
  349.7 9.5 reshape.282
  360.5 25.7 %dynamic-update-slice.2 = f32[4,2097408]{1,0:T(4,128)} dynamic-update-slice(f32[4,2097408]{1,0:T(4,128)} %dynamic-update-slice.1, f32[4,294912]{1,0:T(4,128)} %reshape.278, s32[]{} %constant.118, s32[]{} %constant.120) | dynamic-update-slice | bytes 9437188
  390.4 6.5 constant_dynamic-update-slice_fusion.5
  402.6 49.6 %dynamic-update-slice.11 = f32[4,2097408]{1,0:T(4,128)} dynamic-update-slice(f32[4,2097408]{1,0:T(4,128)} %dynamic-update-slice.10, f32[4,589824]{1,0:T(4,128)} %reshape.287, s32[]{} %constant.118, s32[]{} %constant.129) | dynamic-update-slice | bytes 18874372
  453.7 49.6 %dynamic-update-slice.13 = f32[4,2097408]{1,0:T(4,128)} dynamic-update-slice(f32[4,2097408]{1,0:T(4,128)} %dynamic-update-slice.12, f32[4,589824]{1,0:T(4,128)} %reshape.289, s32[]{} %constant.118, s32[]{} %constant.131) | dynamic-update-slice | bytes 18874372
  505.7 94.5 %reshape.312 = f32[8389632]{0:T(1024)} reshape(f32[4,2097408]{1,0:T(4,128)} %constant_dynamic-update-slice_fusion.3) | data formatting | bytes 67117056
  600.3 42.8 %reshape_reshape.3 = f32[32,262176]{1,0:T(8,128)} reshape(f32[8389632]{0:T(1024)} %reshape.312) | data formatting | bytes 67117056 | tf_op jit(solution)/shard_map/reshape;reshape | solution.py:252
  643.1 551.0 %all-reduce.3 = bf16[32,262176]{1,0:T(8,128)(2,1)} all-reduce(f32[32,262176]{1,0:T(8,128)} %reshape_reshape.3), channel_id=3, replica_groups=mesh['rows'=4,'ty'=4,'tx'=2] {'rows','ty','tx'}, use_global_device_ids=true, to_apply=%region_21.22.clone | all-reduce | flops 8389632 | bytes 50337792
  1194.2 4.4 fusion.39
  1199.9 3.0 collective-permute-start
  1205.3 4.6 collective-permute-start.2
  1209.9 3.4 collective-permute-done.3
  1217.4 2.1 slice.362
  1219.6 34.3 %all-gather.6.cloned.1.call-done = bf16[8,1,262176]{2,1,0:T(2,128)(2,1)} async-done(((bf16[1,1,262176]{2,1,0:T(2,128)(2,1)}), bf16[8,1,262176]{2,1,0:T(2,128)(2,1)}) %all-gather.6.cloned.1.call-update) | async-done | bytes 4194832 | tf_op jit(solution)/shard_map/all_gather | solution.py:258
  1253.9 91.0 %convert_reduce_fusion = f32[8,262176]{1,0:T(8,128)} fusion(bf16[8,1,262176]{2,1,0:T(2,128)(2,1)} %all-gather.6.cloned.1.call-done), kind=kLoop, calls=%fused_computation.13 | loop fusion | flops 2097408 | bytes 12584448 | tf_op jit(solution)/shard_map/convert_element_type | solution.py:259
  1344.9 10.3 reshape.314
  1355.2 37.7 %slice.224 = f32[131088,16]{1,0:T(8,128)} reshape(f32[2097408]{0:T(1024)} %reshape.314) | data formatting | bytes 16779264 | tf_op jit(solution)/shard_map/slice | solution.py:267
  1397.5 9.7 slice.232
  1407.2 5.9 fusion.98
  1421.4 3.9 reshape.295
  1425.3 3.4 reshape.296
  (257 shorter events, 99.5 us)
Async XLA Ops:
  7.2 9.2 copy-start
  7.2 74.2 %all-gather.4.cloned.1.call-start = ((), (), s32[]{:S(2)}) async-start(), calls=%async_computation.1 | async-start | bytes 10616832 | tf_op jit(solution)/shard_map/all_gather | solution.py:112
  9.6 8.4 copy-start.39
  10.3 7.7 copy-start.35
  19.7 303.6 %reduce-scatter.2.cloned.1.call-start = ((), (), s32[]{:S(2)}) async-start(), calls=%async_computation.2 | async-start | bytes 10616832 | tf_op jit(solution)/shard_map/reduce_scatter | solution.py:202
  21.1 12.5 collective-permute-start.4
  24.1 10.2 collective-permute-start.5
  38.1 18.9 %collective-permute-start.7 = (bf16[3,10,1,16]{3,2,1,0:T(2,128)(2,1)}, bf16[3,10,1,16]{3,2,1,0:T(2,128)(2,1)}, u32[]{:S(2)}, u32[]{:S(2)}) collective-permute-start(bf16[3,10,1,16]{3,2,1,0:T(2,128)(2,1)} %get-tuple-element.100), channel_id=1, source_target_pairs={{0,1},{2,3},{4,5},{6,7},{8,9},{10,11},{12,13},{14,15},{16,17},{18,... | collective-permute-start | bytes 2888 | tf_op jit(solution)/shard_map/ppermute | solution.py:20
  43.0 14.1 collective-permute-start.6
  46.2 8.9 copy-start.66
  46.2 10.9 copy-start.46
  46.2 10.9 copy-start.50
  127.2 11.9 slice-start.1
  127.2 10.8 copy-start.6
  127.2 10.8 copy-start.17
  127.2 10.8 copy-start.63
  127.2 11.9 slice-start.2
  138.8 20.4 %copy-start.8 = (f32[384,768]{1,0:T(8,128)}, f32[384,768]{1,0:T(8,128)S(1)}, u32[]{:S(2)}) copy-start(f32[384,768]{1,0:T(8,128)S(1)} %get-tuple-element.119) | copy-start | bytes 3538948
  141.3 15.0 %copy-start.16 = (f32[384,3072]{1,0:T(8,128)}, f32[384,3072]{1,0:T(8,128)S(1)}, u32[]{:S(2)}) copy-start(f32[384,3072]{1,0:T(8,128)S(1)} %convolution_add_fusion) | copy-start | bytes 14155780
  156.3 3.4 copy-start.10
  168.3 12.1 copy-start.13
  168.4 12.1 copy-start.33
  201.8 13.0 copy-start.14
  214.8 5.0 copy-start.2
  235.5 1018.4 %all-gather.6.cloned.1.call-start = ((), (), s32[]{:S(2)}) async-start(), calls=%async_computation.3 | async-start | bytes 9441792 | tf_op jit(solution)/shard_map/all_gather | solution.py:258
  274.9 14.0 copy-start.64
  289.5 6.6 copy-start.20
  301.2 12.2 copy-start.67
  313.4 6.2 copy-start.31
  319.6 3.8 copy-start.36
  319.6 3.8 copy-start.42
  319.6 3.8 copy-start.44
  323.3 4.3 copy-start.57
  323.3 4.3 copy-start.7
  323.4 4.8 copy-start.4
  330.5 5.7 copy-start.18
  332.6 3.6 copy-start.24
  332.6 3.6 copy-start.28
  332.6 3.6 copy-start.40
  336.2 5.5 copy-start.27
  336.2 6.3 copy-start.58
  342.6 7.0 copy-start.69
  342.6 7.0 copy-start.68
  390.4 6.5 copy-start.12
  396.9 4.3 copy-start.60
  402.5 49.6 %copy-start.45 = (f32[4,768]{1,0:T(4,128)S(1)}, f32[4,768]{1,0:T(4,128)}, u32[]{:S(2)}) copy-start(f32[4,768]{1,0:T(4,128)} %reshape.288) | copy-start | bytes 36868
  453.7 49.6 %copy-start.59 = (f32[4,192]{1,0:T(4,128)S(1)}, f32[4,192]{1,0:T(4,128)}, u32[]{:S(2)}) copy-start(f32[4,192]{1,0:T(4,128)} %reshape.290) | copy-start | bytes 9220
  453.7 51.2 %copy-start.25 = (f32[4,27648]{1,0:T(4,128)S(1)}, f32[4,27648]{1,0:T(4,128)}, u32[]{:S(2)}) copy-start(f32[4,27648]{1,0:T(4,128)} %reshape.291) | copy-start | bytes 1327108
  643.1 555.5 %copy-start.30 = (bf16[384,768]{1,0:T(8,128)(2,1)S(1)}, bf16[384,768]{1,0:T(8,128)(2,1)}, u32[]{:S(2)}) copy-start(bf16[384,768]{1,0:T(8,128)(2,1)} %copy-done.29) | copy-start | bytes 1769476
  643.1 571.8 %copy-start.38 = (bf16[768,144]{0,1:T(8,128)(2,1)S(1)}, bf16[768,144]{0,1:T(8,128)(2,1)}, u32[]{:S(2)}) copy-start(bf16[768,144]{0,1:T(8,128)(2,1)} %param.38) | copy-start | bytes 663556
  1194.1 21.5 %copy-start.47 = (pred[3,8,16]{2,1,0:T(8,128)(4,1)S(1)}, pred[3,8,16]{2,1,0:T(8,128)(4,1)}, u32[]{:S(2)}) copy-start(pred[3,8,16]{2,1,0:T(8,128)(4,1)} %get-tuple-element.71) | copy-start | bytes 1156
  1194.1 21.5 %copy-start.48 = (pred[3,8,16]{2,1,0:T(8,128)(4,1)S(1)}, pred[3,8,16]{2,1,0:T(8,128)(4,1)}, u32[]{:S(2)}) copy-start(pred[3,8,16]{2,1,0:T(8,128)(4,1)} %get-tuple-element.107) | copy-start | bytes 1156
  1194.1 21.5 %copy-start.49 = (pred[3,8,16]{2,1,0:T(8,128)(4,1)S(1)}, pred[3,8,16]{2,1,0:T(8,128)(4,1)}, u32[]{:S(2)}) copy-start(pred[3,8,16]{2,1,0:T(8,128)(4,1)} %get-tuple-element.108) | copy-start | bytes 1156
  1194.1 21.5 %copy-start.51 = (pred[3,8,16]{2,1,0:T(8,128)(4,1)S(1)}, pred[3,8,16]{2,1,0:T(8,128)(4,1)}, u32[]{:S(2)}) copy-start(pred[3,8,16]{2,1,0:T(8,128)(4,1)} %get-tuple-element.109) | copy-start | bytes 1156
  1194.1 21.5 %copy-start.52 = (pred[3,8,16]{2,1,0:T(8,128)(4,1)S(1)}, pred[3,8,16]{2,1,0:T(8,128)(4,1)}, u32[]{:S(2)}) copy-start(pred[3,8,16]{2,1,0:T(8,128)(4,1)} %get-tuple-element.110) | copy-start | bytes 1156
  1194.1 21.5 %copy-start.53 = (pred[3,8,16]{2,1,0:T(8,128)(4,1)S(1)}, pred[3,8,16]{2,1,0:T(8,128)(4,1)}, u32[]{:S(2)}) copy-start(pred[3,8,16]{2,1,0:T(8,128)(4,1)} %get-tuple-element.111) | copy-start | bytes 1156
  1194.1 21.5 %copy-start.54 = (pred[3,8,16]{2,1,0:T(8,128)(4,1)S(1)}, pred[3,8,16]{2,1,0:T(8,128)(4,1)}, u32[]{:S(2)}) copy-start(pred[3,8,16]{2,1,0:T(8,128)(4,1)} %get-tuple-element.112) | copy-start | bytes 1156
  1194.1 21.5 %copy-start.55 = (pred[3,8,16]{2,1,0:T(8,128)(4,1)S(1)}, pred[3,8,16]{2,1,0:T(8,128)(4,1)}, u32[]{:S(2)}) copy-start(pred[3,8,16]{2,1,0:T(8,128)(4,1)} %get-tuple-element.113) | copy-start | bytes 1156
  1198.6 4.3 collective-permute-start.1
  1199.9 3.9 collective-permute-start
  1204.0 9.2 collective-permute-start.3
  1205.3 9.5 collective-permute-start.2
  1407.2 8.8 slice-start
  1421.4 10.7 copy-start.1
  (23 other events, 43.1 us)
Sparse Core Ops, SparseCore 0:
  19.8 61.5 all-gather.3
  235.6 76.6 reduce-scatter.1
  1198.7 55.0 all-gather.5
where the time goes:
time: 1450 us; the launch traced here: 1440 us
  blocking collectives  551 us (38%)
  local copies, waits for them, and re-layouts  509 us (35%)
  other arithmetic  153 us (11%)
  matrix products  134 us (9%)
  waiting for transfers between devices  56.2 us (4%)
  starting transfers between devices  20.9 us (1%)
  between operations  14.8 us (1%)
    unnamed x1, blocking collectives  551 us
    unnamed x171, local copies, waits for them, and re-layouts  268 us
    dot_general x26, matrix products, product(): jnp.einsum(pattern, former, latter, preferred_element_type=jnp.float32)  134 us
    convert_element_type x1, other arithmetic, shards(): summed = lax.all_gather(shares.astype(jnp.bfloat16), ('ty', 'tx'), axis=0...  91 us
    slice x11, local copies, waits for them, and re-layouts, shards(): totals.append(summed[start_at:start_at + length].reshape(shard_shape))  62.8 us
    reshape x16, local copies, waits for them, and re-layouts, shards(): entry.reshape(group_count, -1)  55.8 us
    another operation x1, local copies, waits for them, and re-layouts, shards(): table.reshape(group_count * tile_count, piece_width)  42.8 us
    all_gather x1, waiting for transfers between devices, shards(): lax.all_gather(shares.astype(jnp.bfloat16), ('ty', 'tx'), axis=0, tiled=T...  34.3 us
  transfers between devices with their start and end apart: 11, of which 5 were waited for; matrix products, arithmetic and copies ran while one was open for 9% of the time, Pallas kernels for 0%

commit v1 on v0

--- a/solution.py
+++ b/solution.py
@@ -1,9 +1,14 @@
+import functools
+
 import jax
 import jax.numpy as jnp
 from jax import lax
+from jax.experimental import pallas as pl
+from jax.experimental.pallas import tpu as pltpu
 from jax.sharding import PartitionSpec as P
 
 HEADS = 12
+MESH = pl.DeviceIdType.MESH
 
 
 norm_eps = 1e-05
@@ -36,6 +41,248 @@
 
 def product(former, latter, pattern):
     return jnp.einsum(pattern, former, latter, preferred_element_type=jnp.float32)
+
+
+def add_rows(target, first, second, rows):
+    step = 16
+
+    def body(i, carry):
+        at = pl.ds(pl.multiple_of(i * step, step), step)
+        target[at, :] = first[at, :] + second[at, :]
+        return carry
+
+    lax.fori_loop(0, rows // step, body, 0)
+
+
+def grad_reduce_kernel(shapes, *refs):
+    count = len(shapes)
+    grads = refs[:count]
+    outs = refs[count : 2 * count]
+    rest = refs[2 * count :]
+    own, got, half, quarter, final = [rest[i * count : (i + 1) * count] for i in range(5)]
+    local_sem, send_sem, recv_sem = rest[5 * count :]
+    z, ty, y = lax.axis_index("rows"), lax.axis_index("ty"), lax.axis_index("tx")
+    core, x = lax.rem(ty, 2), ty // 2
+    peer_core = (z, x * 2 + 1 - core, y)
+    peer_x = (z, (1 - x) * 2 + core, y)
+    peer_y = (z, ty, 1 - y)
+    peer_xy = (z, (1 - x) * 2 + core, 1 - y)
+    peers_z = [(lax.rem(z + k, 4), ty, y) for k in (1, 2, 3)]
+    barrier = pltpu.get_barrier_semaphore()
+    everyone = [peer_core, peer_x, peer_y, peer_xy] + peers_z
+    for peer in everyone:
+        pl.semaphore_signal(barrier, inc=1, device_id=peer, device_id_type=MESH)
+    pl.semaphore_wait(barrier, len(everyone))
+
+    def send(w, slot, source, target, peer):
+        return pltpu.make_async_remote_copy(
+            src_ref=source,
+            dst_ref=target,
+            send_sem=send_sem.at[w, slot],
+            recv_sem=recv_sem.at[w, slot],
+            device_id=peer,
+            device_id_type=MESH,
+        )
+
+    def columns(w, which):
+        width = shapes[w][2] // 2
+        return pl.ds(pl.multiple_of(which * width, 128), width)
+
+    def rows(start, size):
+        return pl.ds(pl.multiple_of(start, 16), size)
+
+    def place(w, block):
+        depth = shapes[w][1]
+        later = block // 2
+        major = x + later * (y - x)
+        minor = y + later * (x - y)
+        return rows(major * (depth // 2) + minor * (depth // 4), depth // 4)
+
+    pending = [{} for _ in shapes]
+
+    def begin(w):
+        swap = send(w, 0, grads[w].at[:, :, columns(w, 1 - core)], got[w], peer_core)
+        swap.start()
+        mine = pltpu.make_async_copy(grads[w].at[:, :, columns(w, core)], own[w], local_sem.at[w, 0])
+        mine.start()
+        pending[w].update(swap=swap, mine=mine)
+
+    def stage_core(w):
+        depth = shapes[w][1]
+        pending[w]["mine"].wait()
+        pending[w]["swap"].wait()
+        for block in range(4):
+            add_rows(own[w].at[block], own[w].at[block], got[w].at[block], depth)
+        first = send(w, 1, own[w].at[0:2, rows((1 - x) * (depth // 2), depth // 2)], half[w].at[0:2], peer_x)
+        second = send(w, 2, own[w].at[2:4, rows((1 - y) * (depth // 2), depth // 2)], half[w].at[2:4], peer_y)
+        first.start()
+        second.start()
+        pending[w].update(half=(first, second))
+
+    def stage_half(w):
+        depth = shapes[w][1]
+        for copy in pending[w]["half"]:
+            copy.wait()
+        for block in range(4):
+            side = x if block < 2 else y
+            kept = own[w].at[block, rows(side * (depth // 2), depth // 2)]
+            add_rows(kept, kept, half[w].at[block], depth // 2)
+        first = send(w, 3, own[w].at[0:2, rows(x * (depth // 2) + (1 - y) * (depth // 4), depth // 4)], quarter[w].at[0:2], peer_y)
+        second = send(w, 4, own[w].at[2:4, rows(y * (depth // 2) + (1 - x) * (depth // 4), depth // 4)], quarter[w].at[2:4], peer_x)
+        first.start()
+        second.start()
+        pending[w].update(quarter=(first, second))
+
+    def stage_quarter(w):
+        depth = shapes[w][1]
+        for copy in pending[w]["quarter"]:
+            copy.wait()
+        for block in range(4):
+            kept = own[w].at[block, place(w, block // 2 * 2)]
+            add_rows(kept, kept, quarter[w].at[block], depth // 4)
+        copies = []
+        for k, peer in enumerate(peers_z):
+            block = peer[0]
+            copy = send(w, 5 + k, own[w].at[block, place(w, block)], final[w].at[k], peer)
+            copy.start()
+            copies.append(copy)
+        pending[w].update(final=copies)
+
+    def stage_final(w):
+        depth = shapes[w][1]
+        for copy in pending[w]["final"]:
+            copy.wait()
+        kept = own[w].at[z, place(w, z)]
+        total = final[w].at[0]
+
+        def body(i, carry):
+            at = pl.ds(pl.multiple_of(i * 16, 16), 16)
+            parts = [ref[at, :].astype(jnp.float32) for ref in (kept, total, final[w].at[1], final[w].at[2])]
+            total[at, :] = (parts[0] + parts[1] + (parts[2] + parts[3])).astype(jnp.bfloat16)
+            return carry
+
+        lax.fori_loop(0, depth // 64, body, 0)
+        target = outs[w].at[place(w, z), columns(w, core)]
+        copies = []
+        for k, peer in enumerate((peer_x, peer_y, peer_xy)):
+            copy = send(w, 8 + k, total, target, peer)
+            copy.start()
+            copies.append(copy)
+        keep = pltpu.make_async_copy(total, target, local_sem.at[w, 1])
+        keep.start()
+        pending[w].update(gather=copies, keep=keep)
+
+    def stage_gather(w):
+        for copy in pending[w]["gather"]:
+            copy.wait()
+        pending[w]["keep"].wait()
+        strip = outs[w].at[:, columns(w, core)]
+        copy = send(w, 11, strip, strip, peer_core)
+        copy.start()
+        pending[w].update(strip=copy)
+
+    def stage_strip(w):
+        pending[w]["strip"].wait()
+
+    for w in range(count):
+        begin(w)
+    stages = [stage_core, stage_half, stage_quarter, stage_final, stage_gather, stage_strip]
+    for tick in range(count + len(stages) - 1):
+        for depth_index in reversed(range(len(stages))):
+            w = tick - depth_index
+            if 0 <= w < count:
+                stages[depth_index](w)
+
+
+def grad_reduce(grads):
+    shapes = tuple(entry.shape for entry in grads)
+    count = len(shapes)
+    low = jnp.bfloat16
+    scratch = (
+        [pltpu.VMEM((s[0], s[1], s[2] // 2), low) for s in shapes]
+        + [pltpu.VMEM((s[0], s[1], s[2] // 2), low) for s in shapes]
+        + [pltpu.VMEM((s[0], s[1] // 2, s[2] // 2), low) for s in shapes]
+        + [pltpu.VMEM((s[0], s[1] // 4, s[2] // 2), low) for s in shapes]
+        + [pltpu.VMEM((3, s[1] // 4, s[2] // 2), low) for s in shapes]
+        + [
+            pltpu.SemaphoreType.DMA((count, 2)),
+            pltpu.SemaphoreType.DMA((count, 12)),
+            pltpu.SemaphoreType.DMA((count, 12)),
+        ]
+    )
+    return pl.pallas_call(
+        functools.partial(grad_reduce_kernel, shapes),
+        out_shape=[jax.ShapeDtypeStruct(s[1:], low) for s in shapes],
+        in_specs=[pl.BlockSpec(memory_space=pl.ANY)] * count,
+        out_specs=[pl.BlockSpec(memory_space=pl.ANY)] * count,
+        scratch_shapes=scratch,
+        compiler_params=pltpu.CompilerParams(collective_id=3, has_side_effects=True, vmem_limit_bytes=56 * 1024 * 1024),
+        name="grad_reduce",
+    )(*grads)
+
+
+def sum_by_table(local_grads):
+    band_count, column_count = lax.axis_size("ty"), lax.axis_size("tx")
+    group_count = lax.axis_size("rows")
+    tile_count = band_count * column_count
+    table = jnp.concatenate([entry.reshape(group_count, -1) for entry in local_grads], axis=1)
+    column_total = table.shape[1]
+    padded_columns = -(-column_total // tile_count) * tile_count
+    piece_width = padded_columns // tile_count
+    table = table.reshape(group_count, tile_count, piece_width)
+    shares = lax.psum_scatter(
+        table.reshape(group_count * tile_count, piece_width),
+        ("rows", "ty", "tx"),
+        scatter_dimension=0,
+        tiled=True,
+    )
+    summed = (
+        lax.all_gather(shares.astype(jnp.bfloat16), ("ty", "tx"), axis=0, tiled=True)
+        .astype(shares.dtype)
+        .reshape(-1)
+    )
+    totals = []
+    start_at = 0
+    for entry in local_grads:
+        length = entry.size // group_count
+        shard_shape = (entry.shape[0] // group_count,) + entry.shape[1:]
+        totals.append(summed[start_at : start_at + length].reshape(shard_shape))
+        start_at = start_at + length
+    return tuple(totals)
+
+
+def sum_grads(local_grads):
+    if (lax.axis_size("rows"), lax.axis_size("ty"), lax.axis_size("tx")) != (4, 4, 2):
+        return sum_by_table(local_grads)
+    low = jnp.bfloat16
+    groups = 4
+    blocks = [entry.reshape((groups, -1) + entry.shape[1:]) for entry in local_grads]
+    wide = [k for k, entry in enumerate(local_grads) if entry.ndim == 2 and entry.shape[1] % 256 == 0]
+    thin = [k for k, entry in enumerate(local_grads) if entry.ndim == 2 and k not in wide]
+    flat = [k for k, entry in enumerate(local_grads) if entry.ndim == 1]
+    thin_part = jnp.concatenate([blocks[k].astype(low) for k in thin], axis=2)
+    thin_width = thin_part.shape[2]
+    thin_part = jnp.pad(thin_part, ((0, 0), (0, 0), (0, -thin_width % 256)))
+    flat_part = jnp.concatenate([blocks[k].astype(low) for k in flat], axis=1)
+    flat_size = flat_part.shape[1]
+    flat_part = jnp.pad(flat_part, ((0, 0), (0, -flat_size % (64 * 256))))
+    flat_part = flat_part.reshape(groups, -1, 256)
+    order = sorted(wide, key=lambda k: local_grads[k].size)
+    order = order[:1] + order[1:][::-1]
+    summed = grad_reduce([blocks[k].astype(low) for k in order] + [thin_part, flat_part])
+    totals = {k: part.astype(jnp.float32) for k, part in zip(order, summed)}
+    start_at = 0
+    for k in thin:
+        width = local_grads[k].shape[1]
+        totals[k] = summed[-2][:, start_at : start_at + width].astype(jnp.float32)
+        start_at = start_at + width
+    line = summed[-1].reshape(-1)
+    start_at = 0
+    for k in flat:
+        length = blocks[k].shape[1]
+        totals[k] = line[start_at : start_at + length].astype(jnp.float32)
+        start_at = start_at + length
+    return tuple(totals[k] for k in range(len(local_grads)))
 
 
 def shards(
@@ -241,32 +488,7 @@
         fc2_bias_grad,
         conv_weight_grad,
     )
-    group_count = lax.axis_size("rows")
-    tile_count = band_count * column_count
-    table = jnp.concatenate([entry.reshape(group_count, -1) for entry in local_grads], axis=1)
-    column_total = table.shape[1]
-    padded_columns = -(-column_total // tile_count) * tile_count
-    piece_width = padded_columns // tile_count
-    table = table.reshape(group_count, tile_count, piece_width)
-    shares = lax.psum_scatter(
-        table.reshape(group_count * tile_count, piece_width),
-        ("rows", "ty", "tx"),
-        scatter_dimension=0,
-        tiled=True,
-    )
-    summed = (
-        lax.all_gather(shares.astype(jnp.bfloat16), ("ty", "tx"), axis=0, tiled=True)
-        .astype(shares.dtype)
-        .reshape(-1)
-    )
-    totals = []
-    start_at = 0
-    for entry in local_grads:
-        length = entry.size // group_count
-        shard_shape = (entry.shape[0] // group_count,) + entry.shape[1:]
-        totals.append(summed[start_at : start_at + length].reshape(shard_shape))
-        start_at = start_at + length
-    return (output, skip_input_grad) + tuple(totals)
+    return (output, skip_input_grad) + sum_grads(local_grads)
 
 
 def solution(mesh):

time: 1450 us -> 503 us (0.35)
  blocking collectives: 551 us -> 0 us
  local copies, waits for them, and re-layouts: 509 us -> 104 us
  Pallas kernels: 0 us -> 116 us
  other arithmetic: 153 us -> 78.1 us
  waiting for transfers between devices: 56.2 us -> 19.9 us
    unnamed x1 -> x0, blocking collectives: 551 us -> none
    unnamed x171 -> x138, local copies, waits for them, and re-layouts: 268 us -> 12.1 us
    pallas_call x0 -> x1, Pallas kernels: none -> 116 us  [grad_reduce(): pl.pallas_call(functools.partial(grad_reduce_kernel, shapes), out_shape=[...]
    convert_element_type x2 -> x9, other arithmetic: 96.2 us -> 14.3 us  [the longest x5 9.84 us: sum_grads(): totals = {k: part.astype(jnp.float32) for k, part in zip(order, summed)}]
    reshape x21 -> x0, local copies, waits for them, and re-layouts: 67.5 us -> none  [the longest x16 55.8 us: shards(): entry.reshape(group_count, -1)]
    slice x12 -> x0, local copies, waits for them, and re-layouts: 64.9 us -> none  [the longest x11 62.8 us: shards(): totals.append(summed[start_at:start_at + length].reshape(shard_shape))]
    another operation x1 -> x0, local copies, waits for them, and re-layouts: 42.8 us -> none  [shards(): table.reshape(group_count * tile_count, piece_width)]
    all_gather x1 -> x0, waiting for transfers between devices: 34.3 us -> none  [shards(): lax.all_gather(shares.astype(jnp.bfloat16), ('ty', 'tx'), axis=0, tiled=T...]
  transfers between devices with their start and end apart: 11 -> 10, of which waited for: 5 -> 2; matrix products, arithmetic and copies ran while one was open for 9% -> 19% of each run, Pallas kernels for 0% -> 0%
where the time goes in v1:
time: 503 us; the launch traced here: 496 us
  matrix products  141 us (28%)
  Pallas kernels  116 us (23%)
  local copies, waits for them, and re-layouts  104 us (21%)
  other arithmetic  78.1 us (16%)
  starting transfers between devices  22.5 us (4%)
  waiting for transfers between devices  19.9 us (4%)
  between operations  15.3 us (3%)
    dot_general x26, matrix products, product(): jnp.einsum(pattern, former, latter, preferred_element_type=jnp.float32)  141 us
    pallas_call x1, Pallas kernels, grad_reduce(): pl.pallas_call(functools.partial(grad_reduce_kernel, shapes), out_shape=[...  116 us
    ppermute x4, starting transfers between devices, with_halo(): before = lax.ppermute(last, axis, up)  17.3 us
    slice x2, local copies, waits for them, and re-layouts, shards(): row_pairs[:, :, :model_width]  14.7 us
    all_gather x1, waiting for transfers between devices, shards(): row_pairs = lax.all_gather(local_pairs, ('ty', 'tx'), axis=1, tiled=True)  13.8 us
    convert_element_type x1, other arithmetic, shards(): (weights_again * (weights_grad - weighted_sum)).astype(jnp.bfloat16)  13 us
    unnamed x138, local copies, waits for them, and re-layouts  12.1 us
    dot_general x4, local copies, waits for them, and re-layouts, product(): jnp.einsum(pattern, former, latter, preferred_element_type=jnp.float32)  10.5 us
  transfers between devices with their start and end apart: 10, of which 2 were waited for; matrix products, arithmetic and copies ran while one was open for 19% of the time, Pallas kernels for 0%

profile of v1, /device:TPU:0, one launch (start us, length us, event | category | flops | bytes accessed | tf_op | source)
XLA Modules:
  0.0 496.3 jit_solution(10886245570822483584)
XLA Ops:
  11.5 3.2 fusion.122
  15.7 1.7 convolution_convert_fusion.2
  20.5 3.0 collective-permute-start.4
  26.3 1.8 fusion.96
  33.6 1.9 fusion.91
  37.5 4.9 collective-permute-start.7
  43.6 1.7 broadcast_compare_fusion
  45.3 1.9 slice.216
  48.5 3.0 reshape.252
  51.5 2.9 copy.78
  58.3 2.6 fusion.90
  60.9 2.0 concatenate.54
  65.2 1.7 fusion.118
  67.0 13.8 %all-gather.2.cloned.1.call-done = bf16[3,1024,1536]{2,1,0:T(8,128)(2,1)} async-done(((bf16[3,128,1536]{2,1,0:T(8,128)(2,1)}), bf16[3,1024,1536]{2,1,0:T(8,128)(2,1)}) %all-gather.2.cloned.1.call-update) | async-done | bytes 9437200 | tf_op jit(solution)/shard_map/all_gather | solution.py:359
  80.8 8.0 %fusion.117 = (bf16[3,1024,768]{2,1,0:T(8,128)(2,1)}, bf16[3,1024,768]{2,1,0:T(8,128)(2,1)}) fusion(bf16[3,1024,1536]{2,1,0:T(8,128)(2,1)} %all-gather.2.cloned.1.call-done), kind=kLoop, calls=%fused_computation.230 | loop fusion | bytes 18874368 | tf_op jit(solution)/shard_map/slice | solution.py:360
  88.8 6.7 %copy.74 = bf16[3,1024,768]{1,2,0:T(8,128)(2,1)} copy(bf16[3,1024,768]{2,1,0:T(8,128)(2,1)} %get-tuple-element.106) | data formatting | bytes 9437184 | tf_op jit(solution)/shard_map/slice | solution.py:361
  95.5 6.7 %copy.77 = bf16[3,1024,768]{1,2,0:T(8,128)(2,1)} copy(bf16[3,1024,768]{2,1,0:T(8,128)(2,1)} %get-tuple-element.105) | data formatting | bytes 9437184 | tf_op jit(solution)/shard_map/slice | solution.py:360
  102.1 13.0 %fusion.123 = (f32[3,12,128]{2,1,0:T(8,128)}, f32[3,12,128,1024]{3,2,1,0:T(8,128)}) fusion(bf16[3,128,12,64]{1,3,2,0:T(8,128)(2,1)} %copy.78, bf16[3,1024,12,64]{1,3,2,0:T(8,128)(2,1)} %bitcast.175, pred[3,128,1024]{2,1,0:T(8,128)(4,1)} %broadcast_compare_fusion), kind=kOutput, calls=%fused_computation.236 | convolution fusion | flops 618130944 | bytes 24594432 | tf_op jit(solution)/shard_map/rqhd,rkhd->rhqk/dot_general | solution.py:43
  115.2 10.0 %fusion = f32[3,12,128]{2,1,0:T(8,128)} fusion(f32[3,12,128,1024]{3,2,1,0:T(8,128)} %get-tuple-element.150, f32[3,12,128]{2,1,0:T(8,128)} %get-tuple-element.149), kind=kLoop, calls=%fused_computation.6 | loop fusion | flops 9432576 | bytes 18911232 | tf_op jit(solution)/shard_map/reduce_sum | solution.py:370
  126.6 10.4 %fusion.42 = bf16[3,128,12,64]{1,3,2,0:T(8,128)(2,1)S(1)} fusion(bf16[3,1024,12,64]{1,3,2,0:T(8,128)(2,1)} %bitcast.179, f32[3,12,128,1024]{3,2,1,0:T(8,128)} %get-tuple-element.150, f32[3,12,128]{2,1,0:T(8,128)} %fusion, f32[3,12,128]{2,1,0:T(8,128)} %get-tuple-element.149), kind=kOutput, calls=%fused_computation.79 | convolution fusion | flops 618430464 | bytes 24219648 | tf_op jit(solution)/shard_map/rhqk,rkhd->rqhd/dot_general | solution.py:43
  138.9 13.1 %fusion.9 = (bf16[3072,384]{0,1:T(8,128)(2,1)}, f32[384,3072]{1,0:T(8,128)S(1)}) fusion(f32[3072]{0:T(1024)S(1)} %copy-done.44, bf16[768,3072]{1,0:T(8,128)(2,1)S(1)} %bitcast.205, f32[384,768]{1,0:T(8,128)S(1)} %get-tuple-element.152, f32[768]{0:T(1024)S(1)} %copy-done.51, f32[768]{0:T(1024)S(1)} %copy-done.42, f32[384]{0:T(512)S(1)} %fusion.103, ...), kind=kOutput, calls=%fused_computation.20 | convolution fusion | flops 1891270656 | bytes 12997632 | tf_op jit(solution)/shard_map/td,df->tf/dot_general | solution.py:43
  152.0 15.2 %fusion.111 = (bf16[3072]{0:T(1024)(128)(2,1)}, bf16[384,3072]{1,0:T(8,128)(2,1)S(1)}, f32[384,3072]{1,0:T(8,128)}) fusion(f32[384,3072]{1,0:T(8,128)S(1)} %get-tuple-element.158, f32[3072]{0:T(1024)S(1)} %copy-done.44, bf16[384,768]{1,0:T(8,128)(2,1)S(1)} %copy-done.24, bf16[3072,768]{1,0:T(8,128)(2,1)S(1)} %bitcast.207), kind=kOutput, calls=%fused_computation.225 | convolution fusion | flops 1899230208 | bytes 17123328 | tf_op jit(solution)/shard_map/td,fd->tf/dot_general | solution.py:43
  167.2 2.8 multiply_reduce_fusion.1
  173.9 2.8 reshape.253
  176.7 2.6 copy.81
  179.3 12.1 %fusion.29 = bf16[3,12,64,1024]{3,2,1,0:T(8,128)(2,1)} fusion(bf16[3,128,12,64]{1,3,2,0:T(8,128)(2,1)} %copy.81, f32[3,12,128,1024]{3,2,1,0:T(8,128)} %get-tuple-element.150, f32[3,12,128]{2,1,0:T(8,128)} %log_add_fusion), kind=kOutput, calls=%fused_computation.57 | convolution fusion | flops 615776256 | bytes 24201216 | tf_op jit(solution)/shard_map/rhqk,rqhd->rkhd/dot_general | solution.py:43
  191.4 14.3 %multiply_reduce_fusion = (f32[3,12,128]{2,1,0:T(8,128)}, f32[3,12,128,1024]{3,2,1,0:T(8,128)}) fusion(f32[3,12,128,1024]{3,2,1,0:T(8,128)} %get-tuple-element.150, f32[3,12,128]{2,1,0:T(8,128)S(1)} %copy-done.25, bf16[3,128,12,64]{1,3,2,0:T(8,128)(2,1)S(1)} %copy-done.12, bf16[3,1024,12,64]{1,3,2,0:T(8,128)(2,1)} %bitcast.180), kind=kOutput, calls=%fused_computation.1 | convolution fusion | flops 618130944 | bytes 43094016 | tf_op jit(solution)/shard_map/rqhd,rkhd->rhqk/dot_general | solution.py:43
  205.7 6.7 %copy.86 = bf16[3,1024,768]{2,1,0:T(8,128)(2,1)} copy(bf16[3,1024,768]{1,2,0:T(8,128)(2,1)} %bitcast.177) | data formatting | bytes 9437184 | tf_op jit(solution)/shard_map/reshape | solution.py:445
  212.4 13.0 %multiply_convert_fusion = bf16[3,12,128,1024]{3,2,1,0:T(8,128)(2,1)S(1)} fusion(f32[3,12,128,1024]{3,2,1,0:T(8,128)} %get-tuple-element.155, f32[3,12,128,1024]{3,2,1,0:T(8,128)} %get-tuple-element.150, f32[3,12,128]{2,1,0:T(8,128)} %get-tuple-element.154, f32[3,12,128]{2,1,0:T(8,128)} %log_add_fusion), kind=kLoop, calls=%fused_computation | loop fusion | flops 18874368 | bytes 47222784 | tf_op jit(solution)/shard_map/convert_element_type | solution.py:438
  225.4 3.5 multiply_convert_fusion.1
  230.4 6.6 %copy.85 = bf16[3,1024,768]{2,1,0:T(8,128)(2,1)} copy(bf16[3,1024,768]{1,2,0:T(8,128)(2,1)} %bitcast.178) | data formatting | bytes 9437184 | tf_op jit(solution)/shard_map/reshape | solution.py:444
  237.0 9.2 %pad_maximum_fusion = bf16[3,1024,1536]{2,1,0:T(8,128)(2,1)} fusion(bf16[3,1024,768]{2,1,0:T(8,128)(2,1)} %copy.86, bf16[3,1024,768]{2,1,0:T(8,128)(2,1)} %copy.85), kind=kLoop, calls=%fused_computation.9 | loop fusion | flops 18874368 | bytes 18874368 | tf_op jit(solution)/shard_map/concatenate | solution.py:442
  248.2 8.3 %fusion.38 = bf16[384,768]{1,0:T(8,128)(2,1)S(1)} fusion(f32[384,768]{1,0:T(8,128)} %copy-done.10, bf16[3072,768]{1,0:T(8,128)(2,1)} %param.36, f32[384,3072]{1,0:T(8,128)} %get-tuple-element.94, f32[384,3072]{1,0:T(8,128)} %copy-done.56, f32[3072]{0:T(1024)} %convert_element_type.250, f32[768]{0:T(1024)} %convert_element_type.252), kind=kOutput, calls=%fused_computation.73 | convolution fusion | flops 1817542656 | bytes 15940608 | tf_op jit(solution)/shard_map/tf,fd->td/dot_general | solution.py:43
  259.3 3.7 collective-permute-start
  262.9 4.3 copy.100
  267.3 6.8 %convolution_convert_fusion.4.refs_1_ = bf16[4,768,768]{2,1,0:T(8,128)(2,1)} fusion(bf16[4,768,384]{2,1,0:T(8,128)(2,1)} %bitcast.191, bf16[384,768,1]{1,0,2:T(8,128)(2,1)} %bitcast.194), kind=kOutput, calls=%fused_computation.58 | convolution fusion | flops 1814298624 | bytes 7667712 | tf_op jit(solution)/shard_map/tf,td->fd/dot_general | solution.py:43
  274.1 4.7 convolution_convert_fusion.1
  278.9 6.9 %fusion.43 = bf16[3,128,12,64]{1,3,2,0:T(8,128)(2,1)} fusion(bf16[3,1024,12,64]{1,3,2,0:T(8,128)(2,1)} %bitcast.176, bf16[3,12,128,1024]{3,2,1,0:T(8,128)(2,1)S(1)} %bitcast.174), kind=kOutput, calls=%fused_computation.80 | convolution fusion | flops 604569600 | bytes 14745600 | tf_op jit(solution)/shard_map/rhqk,rkhd->rqhd/dot_general | solution.py:43
  285.8 1.8 convolution_convert_fusion.5.refs_0_
  287.5 2.9 dot_general.124
  290.5 1.9 pad_maximum_fusion.13
  293.7 5.8 %collective-permute-start.2 = (bf16[3,10,1,768]{3,2,1,0:T(2,128)(2,1)}, bf16[3,10,1,768]{3,2,1,0:T(2,128)(2,1)}, u32[]{:S(2)}, u32[]{:S(2)}) collective-permute-start(bf16[3,10,1,768]{3,2,1,0:T(2,128)(2,1)} %get-tuple-element.112), channel_id=1, source_target_pairs={{0,1},{2,3},{4,5},{6,7},{8,9},{10,11},{12,13},{14,15},{16,17},{18,... | collective-permute-start | bytes 138248 | tf_op jit(solution)/shard_map/ppermute | solution.py:25
  299.5 2.2 fusion.44
  301.7 2.9 copy.99
  304.6 2.9 reshape.251
  307.5 1.9 copy.93
  314.6 2.0 fusion.49
  316.7 2.3 fusion.74
  319.0 6.0 %reduce-scatter.2.cloned.1.call-done = bf16[3,128,1536]{2,1,0:T(8,128)(2,1)} async-done(((bf16[3,1024,1536]{2,1,0:T(8,128)(2,1)}), bf16[3,128,1536]{2,1,0:T(8,128)(2,1)}) %reduce-scatter.2.cloned.1.call-update) | async-done | bytes 1179664 | tf_op jit(solution)/shard_map/reduce_scatter | solution.py:449
  325.1 4.3 multiply_reduce_fusion.2
  329.4 4.0 convolution_convert_fusion
  336.2 2.8 convolution_convert_fusion.3
  340.3 2.1 copy.89
  342.4 2.0 convolution_convert_fusion.7
  344.4 1.6 copy.92
  353.0 2.0 fusion.64.refs_5_
  355.0 115.7 %grad_reduce.1 = (bf16[192,768]{1,0:T(8,128)(2,1)}, bf16[768,768]{1,0:T(8,128)(2,1)}, bf16[192,3072]{1,0:T(8,128)(2,1)}, bf16[192,2304]{1,0:T(8,128)(2,1)}, bf16...) custom-call(bf16[4,192,768]{2,1,0:T(8,128)(2,1)} %convolution_convert_fusion.5.refs_0_, ...), custom_call_target="tpu_custom_call" | custom-call | tf_op jit(solution)/shard_map/grad_reduce/pallas_call | solution.py:213
  474.3 1.7 slice_convert_fusion.2
  477.5 2.3 convert_element_type.296
  479.8 2.5 convert_element_type.300
  482.3 1.8 convert_element_type.301
  484.1 1.7 convert_element_type.305
  485.8 1.6 convert_element_type.307
  487.3 1.7 copy.95
  (212 shorter events, 63.1 us)
Async XLA Ops:
  7.2 8.5 %copy-start = (bf16[768,2304]{1,0:T(8,128)(2,1)S(1)}, bf16[768,2304]{1,0:T(8,128)(2,1)}, u32[]{:S(2)}) copy-start(bf16[768,2304]{1,0:T(8,128)(2,1)} %param.29) | copy-start | bytes 10616836
  7.2 73.6 %all-gather.2.cloned.1.call-start = ((), (), s32[]{:S(2)}) async-start(), calls=%async_computation.1 | async-start | bytes 10616832 | tf_op jit(solution)/shard_map/all_gather | solution.py:359
  9.6 7.8 %copy-start.49 = (f32[768]{0:T(1024)}, f32[768]{0:T(1024)S(1)}, u32[]{:S(2)}) copy-start(f32[768]{0:T(1024)S(1)} %convert_element_type.240) | copy-start | bytes 9220
  10.3 7.1 %copy-start.40 = (f32[768]{0:T(1024)}, f32[768]{0:T(1024)S(1)}, u32[]{:S(2)}) copy-start(f32[768]{0:T(1024)S(1)} %convert_element_type.239) | copy-start | bytes 9220
  11.5 3.5 copy-start.21
  14.7 2.7 copy-start.7
  14.8 2.7 copy-start.36
  19.1 306.0 %reduce-scatter.2.cloned.1.call-start = ((), (), s32[]{:S(2)}) async-start(), calls=%async_computation.2 | async-start | bytes 10616832 | tf_op jit(solution)/shard_map/reduce_scatter | solution.py:449
  20.5 12.4 %collective-permute-start.4 = (bf16[3,1,16,16]{3,2,1,0:T(8,128)(2,1)}, bf16[3,1,16,16]{3,2,1,0:T(8,128)(2,1)}, u32[]{:S(2)}, u32[]{:S(2)}) collective-permute-start(bf16[3,1,16,16]{3,2,1,0:T(8,128)(2,1)} %get-tuple-element.131), channel_id=1, source_target_pairs={{0,2},{2,4},{4,6},{1,3},{3,5},{5,7},{8,10},{10,12},{12,14},{9,11},... | collective-permute-start | bytes 4616 | tf_op jit(solution)/shard_map/ppermute | solution.py:25
  23.4 10.1 %collective-permute-start.5 = (bf16[3,1,16,16]{3,2,1,0:T(8,128)(2,1)}, bf16[3,1,16,16]{3,2,1,0:T(8,128)(2,1)}, u32[]{:S(2)}, u32[]{:S(2)}) collective-permute-start(bf16[3,1,16,16]{3,2,1,0:T(8,128)(2,1)} %get-tuple-element.130), channel_id=1, source_target_pairs={{2,0},{4,2},{6,4},{3,1},{5,3},{7,5},{10,8},{12,10},{14,12},{11,9},... | collective-permute-start | bytes 4616 | tf_op jit(solution)/shard_map/ppermute | solution.py:26
  37.5 20.8 %collective-permute-start.7 = (bf16[3,10,1,16]{3,2,1,0:T(2,128)(2,1)}, bf16[3,10,1,16]{3,2,1,0:T(2,128)(2,1)}, u32[]{:S(2)}, u32[]{:S(2)}) collective-permute-start(bf16[3,10,1,16]{3,2,1,0:T(2,128)(2,1)} %get-tuple-element.125), channel_id=1, source_target_pairs={{0,1},{2,3},{4,5},{6,7},{8,9},{10,11},{12,13},{14,15},{16,17},{18,... | collective-permute-start | bytes 2888 | tf_op jit(solution)/shard_map/ppermute | solution.py:25
  42.3 15.9 %collective-permute-start.6 = (bf16[3,10,1,16]{3,2,1,0:T(2,128)(2,1)}, bf16[3,10,1,16]{3,2,1,0:T(2,128)(2,1)}, u32[]{:S(2)}, u32[]{:S(2)}) collective-permute-start(bf16[3,10,1,16]{3,2,1,0:T(2,128)(2,1)} %get-tuple-element.126), channel_id=1, source_target_pairs={{1,0},{3,2},{5,4},{7,6},{9,8},{11,10},{13,12},{15,14},{17,16},{19,... | collective-permute-start | bytes 2888 | tf_op jit(solution)/shard_map/ppermute | solution.py:26
  45.3 12.9 %copy-start.27 = (pred[3,8,16]{2,1,0:T(8,128)(4,1)S(1)}, pred[3,8,16]{2,1,0:T(8,128)(4,1)}, u32[]{:S(2)}) copy-start(pred[3,8,16]{2,1,0:T(8,128)(4,1)} %get-tuple-element.103) | copy-start | bytes 1156
  45.3 12.9 %copy-start.31 = (pred[3,8,16]{2,1,0:T(8,128)(4,1)S(1)}, pred[3,8,16]{2,1,0:T(8,128)(4,1)}, u32[]{:S(2)}) copy-start(pred[3,8,16]{2,1,0:T(8,128)(4,1)} %get-tuple-element.134) | copy-start | bytes 1156
  45.3 12.9 %copy-start.33 = (pred[3,8,16]{2,1,0:T(8,128)(4,1)S(1)}, pred[3,8,16]{2,1,0:T(8,128)(4,1)}, u32[]{:S(2)}) copy-start(pred[3,8,16]{2,1,0:T(8,128)(4,1)} %get-tuple-element.135) | copy-start | bytes 1156
  45.3 13.0 %copy-start.34 = (pred[3,8,16]{2,1,0:T(8,128)(4,1)S(1)}, pred[3,8,16]{2,1,0:T(8,128)(4,1)}, u32[]{:S(2)}) copy-start(pred[3,8,16]{2,1,0:T(8,128)(4,1)} %get-tuple-element.136) | copy-start | bytes 1156
  126.6 12.2 %slice-start.3 = ((s8[4718592]{0:T(1024)(128)(4,1)}), s8[4194304]{0:T(1024)(128)(4,1)S(1)}, s32[]{:S(2)}) async-start(s8[4718592]{0:T(1024)(128)(4,1)} %bitcast.204), calls=%async_computation.6 | async-start | bytes 8388608
  126.6 11.1 %copy-start.8 = (f32[384,768]{1,0:T(8,128)S(1)}, f32[384,768]{1,0:T(8,128)}, u32[]{:S(2)}) copy-start(f32[384,768]{1,0:T(8,128)} %copy-done.7) | copy-start | bytes 3538948
  126.6 11.1 %copy-start.16 = (bf16[768,768]{1,0:T(8,128)(2,1)S(1)}, bf16[768,768]{1,0:T(8,128)(2,1)}, u32[]{:S(2)}) copy-start(bf16[768,768]{1,0:T(8,128)(2,1)} %param.30) | copy-start | bytes 3538948
  126.6 11.1 %copy-start.43 = (f32[768]{0:T(1024)S(1)}, f32[768]{0:T(1024)}, u32[]{:S(2)}) copy-start(f32[768]{0:T(1024)} %convert_element_type.246) | copy-start | bytes 9220
  126.6 12.2 %slice-start.4 = ((s8[4718592]{0:T(1024)(128)(4,1)}), s8[524288]{0:T(1024)(128)(4,1)S(1)}, s32[]{:S(2)}) async-start(s8[4718592]{0:T(1024)(128)(4,1)} %bitcast.204), calls=%async_computation.7 | async-start | bytes 1048576
  137.6 14.3 %copy-start.14 = (bf16[96,8,3,128]{3,1,2,0:T(8,128)(2,1)}, bf16[96,8,3,128]{3,1,2,0:T(8,128)(2,1)S(1)}, u32[]{:S(2)}) copy-start(bf16[96,8,3,128]{3,1,2,0:T(8,128)(2,1)S(1)} %copy.115) | copy-start | bytes 1769476
  137.7 14.3 %slice-start.5 = ((s8[4718592]{0:T(1024)(128)(4,1)}), s8[4194304]{0:T(1024)(128)(4,1)S(1)}, s32[]{:S(2)}) async-start(s8[4718592]{0:T(1024)(128)(4,1)} %bitcast.206), calls=%async_computation.8 | async-start | bytes 8388608
  138.5 31.6 %copy-start.10 = (f32[384,768]{1,0:T(8,128)}, f32[384,768]{1,0:T(8,128)S(1)}, u32[]{:S(2)}) copy-start(f32[384,768]{1,0:T(8,128)S(1)} %get-tuple-element.152) | copy-start | bytes 3538948
  138.8 13.1 %copy-start.24 = (bf16[384,768]{1,0:T(8,128)(2,1)S(1)}, bf16[384,768]{1,0:T(8,128)(2,1)}, u32[]{:S(2)}) copy-start(bf16[384,768]{1,0:T(8,128)(2,1)} %get-tuple-element.111) | copy-start | bytes 1769476
  138.8 13.1 %slice-start.6 = ((s8[4718592]{0:T(1024)(128)(4,1)}), s8[524288]{0:T(1024)(128)(4,1)S(1)}, s32[]{:S(2)}) async-start(s8[4718592]{0:T(1024)(128)(4,1)} %bitcast.206), calls=%async_computation.9 | async-start | bytes 1048576
  152.0 15.3 %copy-start.56 = (f32[384,3072]{1,0:T(8,128)}, f32[384,3072]{1,0:T(8,128)S(1)}, u32[]{:S(2)}) copy-start(f32[384,3072]{1,0:T(8,128)S(1)} %get-tuple-element.158) | copy-start | bytes 14155780
  167.2 2.8 copy-start.57
  167.2 3.4 copy-start.6
  179.3 12.1 %copy-start.12 = (bf16[3,128,12,64]{1,3,2,0:T(8,128)(2,1)S(1)}, bf16[3,128,12,64]{1,3,2,0:T(8,128)(2,1)}, u32[]{:S(2)}) copy-start(bf16[3,128,12,64]{1,3,2,0:T(8,128)(2,1)} %copy.81) | copy-start | bytes 1769476
  179.3 12.1 %copy-start.25 = (f32[3,12,128]{2,1,0:T(8,128)S(1)}, f32[3,12,128]{2,1,0:T(8,128)}, u32[]{:S(2)}) copy-start(f32[3,12,128]{2,1,0:T(8,128)} %log_add_fusion) | copy-start | bytes 55300
  212.4 13.0 %copy-start.13 = (bf16[3,128,12,64]{1,3,2,0:T(8,128)(2,1)S(1)}, bf16[3,128,12,64]{1,3,2,0:T(8,128)(2,1)}, u32[]{:S(2)}) copy-start(bf16[3,128,12,64]{1,3,2,0:T(8,128)(2,1)} %copy.78) | copy-start | bytes 1769476
  225.4 5.0 %copy-start.1 = (bf16[3,12,128,1024]{3,2,1,0:T(8,128)(2,1)}, bf16[3,12,128,1024]{3,2,1,0:T(8,128)(2,1)S(1)}, u32[]{:S(2)}) copy-start(bf16[3,12,128,1024]{3,2,1,0:T(8,128)(2,1)S(1)} %multiply_convert_fusion) | copy-start | bytes 28311556
  258.0 32.5 %collective-permute-start.1 = (bf16[3,1,16,768]{3,2,1,0:T(8,128)(2,1)}, bf16[3,1,16,768]{3,2,1,0:T(8,128)(2,1)}, u32[]{:S(2)}, u32[]{:S(2)}) collective-permute-start(bf16[3,1,16,768]{3,2,1,0:T(8,128)(2,1)} %get-tuple-element.115), channel_id=1, source_target_pairs={{2,0},{4,2},{6,4},{3,1},{5,3},{7,5},{10,8},{12,10},{14,12},{11,9},... | collective-permute-start | bytes 221192 | tf_op jit(solution)/shard_map/ppermute | solution.py:26
  259.3 31.2 %collective-permute-start = (bf16[3,1,16,768]{3,2,1,0:T(8,128)(2,1)}, bf16[3,1,16,768]{3,2,1,0:T(8,128)(2,1)}, u32[]{:S(2)}, u32[]{:S(2)}) collective-permute-start(bf16[3,1,16,768]{3,2,1,0:T(8,128)(2,1)} %get-tuple-element.114), channel_id=1, source_target_pairs={{0,2},{2,4},{4,6},{1,3},{3,5},{5,7},{8,10},{10,12},{12,14},{9,11},... | collective-permute-start | bytes 221192 | tf_op jit(solution)/shard_map/ppermute | solution.py:25
  267.3 6.8 %copy-start.11 = (f32[384,768]{1,0:T(8,128)S(1)}, f32[384,768]{1,0:T(8,128)}, u32[]{:S(2)}) copy-start(f32[384,768]{1,0:T(8,128)} %copy-done.10) | copy-start | bytes 3538948
  267.3 6.8 %copy-start.52 = (f32[768]{0:T(1024)S(1)}, f32[768]{0:T(1024)}, u32[]{:S(2)}) copy-start(f32[768]{0:T(1024)} %convert_element_type.248) | copy-start | bytes 9220
  267.3 6.9 %copy-start.58 = (bf16[384,3072]{1,0:T(8,128)(2,1)S(1)}, bf16[384,3072]{1,0:T(8,128)(2,1)}, u32[]{:S(2)}) copy-start(bf16[384,3072]{1,0:T(8,128)(2,1)} %copy-done.57) | copy-start | bytes 7077892
  267.3 11.6 %slice-start = ((s8[9437184]{0:T(1024)(128)(4,1)}), s8[4194304]{0:T(1024)(128)(4,1)S(1)}, s32[]{:S(2)}) async-start(s8[9437184]{0:T(1024)(128)(4,1)} %bitcast.173), calls=%async_computation.3 | async-start | bytes 8388608
  267.3 11.6 %slice-start.1 = ((s8[9437184]{0:T(1024)(128)(4,1)}), s8[4194304]{0:T(1024)(128)(4,1)S(1)}, s32[]{:S(2)}) async-start(s8[9437184]{0:T(1024)(128)(4,1)} %bitcast.173), calls=%async_computation.4 | async-start | bytes 8388608
  274.1 4.7 slice-start.2
  278.9 6.9 %copy-start.3 = (f32[384,768]{1,0:T(8,128)S(1)}, f32[384,768]{1,0:T(8,128)}, u32[]{:S(2)}) copy-start(f32[384,768]{1,0:T(8,128)} %copy-done.2) | copy-start | bytes 3538948
  278.9 6.9 %copy-start.15 = (bf16[96,8,3,128]{3,1,2,0:T(8,128)(2,1)S(1)}, bf16[96,8,3,128]{3,1,2,0:T(8,128)(2,1)}, u32[]{:S(2)}) copy-start(bf16[96,8,3,128]{3,1,2,0:T(8,128)(2,1)} %copy-done.14) | copy-start | bytes 1769476
  292.4 22.2 %collective-permute-start.3 = (bf16[3,10,1,768]{3,2,1,0:T(2,128)(2,1)}, bf16[3,10,1,768]{3,2,1,0:T(2,128)(2,1)}, u32[]{:S(2)}, u32[]{:S(2)}) collective-permute-start(bf16[3,10,1,768]{3,2,1,0:T(2,128)(2,1)} %get-tuple-element.113), channel_id=1, source_target_pairs={{1,0},{3,2},{5,4},{7,6},{9,8},{11,10},{13,12},{15,14},{17,16},{19,... | collective-permute-start | bytes 138248 | tf_op jit(solution)/shard_map/ppermute | solution.py:26
  293.7 21.0 %collective-permute-start.2 = (bf16[3,10,1,768]{3,2,1,0:T(2,128)(2,1)}, bf16[3,10,1,768]{3,2,1,0:T(2,128)(2,1)}, u32[]{:S(2)}, u32[]{:S(2)}) collective-permute-start(bf16[3,10,1,768]{3,2,1,0:T(2,128)(2,1)} %get-tuple-element.112), channel_id=1, source_target_pairs={{0,1},{2,3},{4,5},{6,7},{8,9},{10,11},{12,13},{14,15},{16,17},{18,... | collective-permute-start | bytes 138248 | tf_op jit(solution)/shard_map/ppermute | solution.py:25
  304.6 12.1 %copy-start.28 = (pred[3,8,16]{2,1,0:T(8,128)(4,1)S(1)}, pred[3,8,16]{2,1,0:T(8,128)(4,1)}, u32[]{:S(2)}) copy-start(pred[3,8,16]{2,1,0:T(8,128)(4,1)} %get-tuple-element.103) | copy-start | bytes 1156
  304.6 12.1 %copy-start.29 = (pred[3,8,16]{2,1,0:T(8,128)(4,1)S(1)}, pred[3,8,16]{2,1,0:T(8,128)(4,1)}, u32[]{:S(2)}) copy-start(pred[3,8,16]{2,1,0:T(8,128)(4,1)} %get-tuple-element.132) | copy-start | bytes 1156
  304.6 12.1 %copy-start.30 = (pred[3,8,16]{2,1,0:T(8,128)(4,1)S(1)}, pred[3,8,16]{2,1,0:T(8,128)(4,1)}, u32[]{:S(2)}) copy-start(pred[3,8,16]{2,1,0:T(8,128)(4,1)} %get-tuple-element.133) | copy-start | bytes 1156
  304.6 12.1 %copy-start.32 = (pred[3,8,16]{2,1,0:T(8,128)(4,1)S(1)}, pred[3,8,16]{2,1,0:T(8,128)(4,1)}, u32[]{:S(2)}) copy-start(pred[3,8,16]{2,1,0:T(8,128)(4,1)} %get-tuple-element.134) | copy-start | bytes 1156
  325.0 4.3 copy-start.9
  325.1 4.3 copy-start.23
  325.1 4.3 copy-start.37
  325.1 4.3 copy-start.41
  325.1 4.3 copy-start.46
  325.1 4.3 copy-start.50
  325.1 4.3 copy-start.54
  329.4 4.0 copy-start.39
  329.4 4.5 copy-start.4
  333.9 2.3 copy-start.22
  333.9 2.3 copy-start.55
  339.1 11.1 %copy-start.35 = (bf16[4,768]{1,0:T(4,128)(2,1)S(1)}, bf16[4,768]{1,0:T(4,128)(2,1)}, u32[]{:S(2)}) copy-start(bf16[4,768]{1,0:T(4,128)(2,1)} %convert_element_type.291) | copy-start | bytes 18436
  339.1 11.1 %copy-start.47 = (bf16[4,192]{1,0:T(4,128)(2,1)S(1)}, bf16[4,192]{1,0:T(4,128)(2,1)}, u32[]{:S(2)}) copy-start(bf16[4,192]{1,0:T(4,128)(2,1)} %convert_element_type.293) | copy-start | bytes 4612
  477.5 6.6 %copy-start.20 = (bf16[192,3072]{1,0:T(8,128)(2,1)S(1)}, bf16[192,3072]{1,0:T(8,128)(2,1)}, u32[]{:S(2)}) copy-start(bf16[192,3072]{1,0:T(8,128)(2,1)} %get-tuple-element.30) | copy-start | bytes 3538948
  477.5 8.3 %copy-start.19 = (bf16[768,768]{1,0:T(8,128)(2,1)S(1)}, bf16[768,768]{1,0:T(8,128)(2,1)}, u32[]{:S(2)}) copy-start(bf16[768,768]{1,0:T(8,128)(2,1)} %get-tuple-element.31) | copy-start | bytes 3538948
  (12 other events, 15.9 us)
Sparse Core Ops, SparseCore 0:
  19.2 61.5 all-gather.1
  246.4 78.5 reduce-scatter.1

commit v2 on v1

--- a/solution.py
+++ b/solution.py
@@ -219,6 +219,386 @@
         compiler_params=pltpu.CompilerParams(collective_id=3, has_side_effects=True, vmem_limit_bytes=56 * 1024 * 1024),
         name="grad_reduce",
     )(*grads)
+
+
+def plane_peers():
+    z, ty, y = lax.axis_index("rows"), lax.axis_index("ty"), lax.axis_index("tx")
+    core, x = lax.rem(ty, 2), ty // 2
+    here = x * 2 + core
+    across = (1 - x) * 2 + core
+    tiles = {
+        "own": here * 2 + y,
+        "x": across * 2 + y,
+        "y": here * 2 + 1 - y,
+        "xy": across * 2 + 1 - y,
+    }
+    peers = {
+        "core": (z, x * 2 + 1 - core, y),
+        "x": (z, across, y),
+        "y": (z, here, 1 - y),
+    }
+    return tiles, peers
+
+
+def greet(peers):
+    barrier = pltpu.get_barrier_semaphore()
+    for peer in peers:
+        pl.semaphore_signal(barrier, inc=1, device_id=peer, device_id_type=MESH)
+    pl.semaphore_wait(barrier, len(peers))
+
+
+def fill_mask(mask_ref, cuts_ref, row, tile_height, tile_width):
+    ty, tx = lax.axis_index("ty"), lax.axis_index("tx")
+    columns = lax.axis_size("tx")
+    tokens = tile_height * tile_width
+    left_width = cuts_ref[row, 0]
+    top_height = cuts_ref[row, 1]
+
+    def image_of(down, across):
+        return jnp.where(across < left_width, 0, jnp.where(down < top_height, 1, 2))
+
+    lane = lax.broadcasted_iota(jnp.int32, (tokens, tokens), 1)
+    step = lax.broadcasted_iota(jnp.int32, (tokens, tokens), 0)
+    mine = image_of(
+        ty * tile_height + lane // tile_width, tx * tile_width + lane % tile_width
+    )
+    for tile in range(mask_ref.shape[0] // tokens):
+        theirs = image_of(
+            tile // columns * tile_height + step // tile_width,
+            tile % columns * tile_width + step % tile_width,
+        )
+        mask_ref[tile * tokens : (tile + 1) * tokens, :] = jnp.where(
+            mine == theirs, 0.0, -1e30
+        )
+
+
+def two_heads(pair, scale):
+    lane = lax.broadcasted_iota(jnp.int32, pair.shape, 1)
+    wide = pair.astype(jnp.float32) * scale
+    first = jnp.where(lane < pair.shape[1] // 2, wide, 0.0)
+    return jnp.concatenate([first, wide - first], axis=0).astype(jnp.bfloat16)
+
+
+def mm(former, latter, axis_former, axis_latter):
+    return lax.dot_general(
+        former,
+        latter,
+        (((axis_former,), (axis_latter,)), ((), ())),
+        preferred_element_type=jnp.float32,
+    )
+
+
+def own_blocks(both):
+    head, tokens = both.shape[0] // 2, both.shape[1] // 2
+    return jnp.concatenate([both[:head, :tokens], both[head:, tokens:]], axis=0)
+
+
+def attend_kernel(
+    tile_height, tile_width, cuts, query, pairs, out, lse, all_out, held, scores, mask, local_sem, send_sem, recv_sem
+):
+    row_count, tokens, width = query.shape
+    tile_count = held.shape[1]
+    pair_count = width // 128
+    tiles, peers = plane_peers()
+    own = tiles["own"]
+    greet(list(peers.values()))
+
+    def send(row, slot, source, target, peer):
+        copy = pltpu.make_async_remote_copy(
+            src_ref=source,
+            dst_ref=target,
+            send_sem=send_sem.at[row, slot],
+            recv_sem=recv_sem.at[row, slot],
+            device_id=peer,
+            device_id_type=MESH,
+        )
+        copy.start()
+        return copy
+
+    flights = [{} for _ in range(row_count)]
+
+    def begin(row):
+        here = held.at[row, own]
+        source = pairs.at[row]
+        flights[row]["x"] = send(row, 0, source, here, peers["x"])
+        flights[row]["y"] = send(row, 1, source, here, peers["y"])
+        flights[row]["core"] = send(row, 2, source, here, peers["core"])
+        keep = pltpu.make_async_copy(source, here, local_sem.at[row, 0])
+        keep.start()
+        flights[row]["keep"] = keep
+
+    def forward(row):
+        flights[row]["y"].wait_recv()
+        key_half = held.at[row, tiles["y"], :, pl.ds(0, width)]
+        flights[row]["far_x"] = send(row, 3, key_half, key_half, peers["x"])
+        flights[row]["x"].wait_recv()
+        value_half = held.at[row, tiles["x"], :, pl.ds(width, width)]
+        flights[row]["far_y"] = send(row, 4, value_half, value_half, peers["y"])
+        for slot, name in ((5, "x"), (6, "y")):
+            tile = held.at[row, tiles[name]]
+            flights[row]["core_" + name] = send(row, slot, tile, tile, peers["core"])
+
+    def finish(row):
+        flights[row]["far_x"].wait_recv()
+        flights[row]["far_y"].wait_recv()
+        tile = held.at[row, tiles["xy"]]
+        last = send(row, 7, tile, tile, peers["core"])
+        flights[row]["keep"].wait()
+        for name in ("core", "core_x", "core_y"):
+            flights[row][name].wait_recv()
+        last.wait_recv()
+        for name in ("x", "y", "core", "far_x", "far_y", "core_x", "core_y"):
+            flights[row][name].wait_send()
+        last.wait_send()
+        keep = pltpu.make_async_copy(held.at[row], all_out.at[row], local_sem.at[row, 1])
+        keep.start()
+        flights[row]["out"] = keep
+
+    chunk = 2
+
+    def compute(row):
+        fill_mask(mask, cuts, row, tile_height, tile_width)
+
+        def one_pair(p, carry):
+            at = pl.ds(pl.multiple_of(p * 128, 128), 128)
+            at_value = pl.ds(pl.multiple_of(width + p * 128, 128), 128)
+            both = two_heads(query[row, :, at], 0.125)
+            peak = None
+            for c in range(tile_count // chunk):
+                span = slice(c * chunk * tokens, (c + 1) * chunk * tokens)
+                keys = held[row, c * chunk : (c + 1) * chunk, :, at].reshape(chunk * tokens, 128)
+                extra = mask[span, :]
+                part = mm(keys, both, 1, 1) + jnp.concatenate([extra, extra], axis=1)
+                scores[span, :] = part
+                top = jnp.max(part, axis=0, keepdims=True)
+                peak = top if peak is None else jnp.maximum(peak, top)
+            total = jnp.zeros_like(peak)
+            summed = jnp.zeros((128, 2 * tokens), jnp.float32)
+            for c in range(tile_count // chunk):
+                span = slice(c * chunk * tokens, (c + 1) * chunk * tokens)
+                values = held[row, c * chunk : (c + 1) * chunk, :, at_value].reshape(chunk * tokens, 128)
+                part = jnp.exp(scores[span, :] - peak)
+                total = total + jnp.sum(part, axis=0, keepdims=True)
+                summed = summed + mm(values, part.astype(jnp.bfloat16), 0, 0)
+            blocks = own_blocks(summed / total)
+            out[row, :, at] = jnp.transpose(blocks).astype(jnp.bfloat16)
+            lse[row, p] = peak + jnp.log(total)
+            return carry
+
+        lax.fori_loop(0, pair_count, one_pair, 0)
+
+    begin(0)
+    if row_count > 1:
+        begin(1)
+    forward(0)
+    for row in range(row_count):
+        if row + 2 < row_count:
+            begin(row + 2)
+        if row + 1 < row_count:
+            forward(row + 1)
+        finish(row)
+        compute(row)
+    for row in range(row_count):
+        flights[row]["out"].wait()
+
+
+def attend(cuts, query, pairs, tile_height, tile_width):
+    row_count, tokens, width = query.shape
+    tile_count = lax.axis_size("ty") * lax.axis_size("tx")
+    pair_count = width // 128
+    low = jnp.bfloat16
+    vmem = pl.BlockSpec(memory_space=pltpu.VMEM)
+    return pl.pallas_call(
+        functools.partial(attend_kernel, tile_height, tile_width),
+        out_shape=[
+            jax.ShapeDtypeStruct((row_count, tokens, width), low),
+            jax.ShapeDtypeStruct((row_count, pair_count, 1, 2 * tokens), jnp.float32),
+            jax.ShapeDtypeStruct((row_count, tile_count, tokens, 2 * width), low),
+        ],
+        in_specs=[pl.BlockSpec(memory_space=pltpu.SMEM), vmem, pl.BlockSpec(memory_space=pl.ANY)],
+        out_specs=[vmem, vmem, pl.BlockSpec(memory_space=pl.ANY)],
+        scratch_shapes=[
+            pltpu.VMEM((row_count, tile_count, tokens, 2 * width), low),
+            pltpu.VMEM((tile_count * tokens, 2 * tokens), jnp.float32),
+            pltpu.VMEM((tile_count * tokens, tokens), jnp.float32),
+            pltpu.SemaphoreType.DMA((row_count, 2)),
+            pltpu.SemaphoreType.DMA((row_count, 8)),
+            pltpu.SemaphoreType.DMA((row_count, 8)),
+        ],
+        compiler_params=pltpu.CompilerParams(
+            collective_id=1, has_side_effects=True, vmem_limit_bytes=40 * 1024 * 1024
+        ),
+        name="attend",
+    )(cuts, query, pairs)
+
+
+def attend_back_kernel(
+    tile_height, tile_width, cuts, query, attended, grad, lse, all_pairs, out,
+    held, terms, core_terms, side_terms, mask, deltas, load_sem, send_sem, recv_sem
+):
+    row_count, tokens, width = query.shape
+    tile_count = held.shape[1]
+    pair_count = width // 128
+    tiles, peers = plane_peers()
+    low = jnp.bfloat16
+    loads = []
+    for row in range(row_count):
+        load = pltpu.make_async_copy(all_pairs.at[row], held.at[row], load_sem.at[row])
+        load.start()
+        loads.append(load)
+    greet(list(peers.values()))
+    z, ty, y = lax.axis_index("rows"), lax.axis_index("ty"), lax.axis_index("tx")
+    core = lax.rem(ty, 2)
+    chunk = 2
+
+    def send(row, slot, source, target, peer):
+        copy = pltpu.make_async_remote_copy(
+            src_ref=source,
+            dst_ref=target,
+            send_sem=send_sem.at[row, slot],
+            recv_sem=recv_sem.at[row, slot],
+            device_id=peer,
+            device_id_type=MESH,
+        )
+        copy.start()
+        return copy
+
+    def compute(row):
+        loads[row].wait()
+        fill_mask(mask, cuts, row, tile_height, tile_width)
+
+        def one_pair(p, carry):
+            at = pl.ds(pl.multiple_of(p * 128, 128), 128)
+            at_value = pl.ds(pl.multiple_of(width + p * 128, 128), 128)
+            grad_pair = grad[row, :, at]
+            both = two_heads(query[row, :, at], 0.125)
+            both_grad = two_heads(grad_pair, 1.0)
+            inner = jnp.transpose(grad_pair.astype(jnp.float32) * attended[row, :, at].astype(jnp.float32))
+            half = inner.shape[0] // 2
+            delta = jnp.concatenate(
+                [jnp.sum(inner[:half], axis=0, keepdims=True), jnp.sum(inner[half:], axis=0, keepdims=True)], axis=1
+            )
+            level = lse[row, p]
+            query_part = jnp.zeros((128, 2 * tokens), jnp.float32)
+            for c in range(tile_count // chunk):
+                span = slice(c * chunk * tokens, (c + 1) * chunk * tokens)
+                some = slice(c * chunk, (c + 1) * chunk)
+                keys = held[row, some, :, at].reshape(chunk * tokens, 128)
+                values = held[row, some, :, at_value].reshape(chunk * tokens, 128)
+                extra = mask[span, :]
+                weights = jnp.exp(mm(keys, both, 1, 1) + jnp.concatenate([extra, extra], axis=1) - level)
+                score_grad = (weights * (mm(values, both_grad, 1, 1) - delta)).astype(low)
+                value_part = mm(weights.astype(low), both_grad, 1, 0)
+                key_part = mm(score_grad, both, 1, 0)
+                query_part = query_part + mm(keys, score_grad, 0, 0)
+                terms[row, some, :, at] = key_part.astype(low).reshape(chunk, tokens, 128)
+                terms[row, some, :, at_value] = value_part.astype(low).reshape(chunk, tokens, 128)
+            blocks = own_blocks(query_part) * 0.125
+            out[row, :, at] = jnp.transpose(blocks).astype(low)
+            return carry
+
+        lax.fori_loop(0, pair_count, one_pair, 0)
+
+    flights = [{} for _ in range(row_count)]
+    names = ("own", "x", "y", "xy")
+    key_at, value_at = pl.ds(0, width), pl.ds(width, width)
+
+    def begin(row):
+        copies = []
+        other = 2 - 4 * core
+        for k, name in enumerate(names):
+            copies.append(send(row, k, terms.at[row, tiles[name] + other], core_terms.at[row, k], peers["core"]))
+        flights[row]["core"] = copies
+
+    def add(target, source, row_total):
+        def body(i, carry):
+            at = pl.ds(pl.multiple_of(i * 16, 16), 16)
+            target[at, :] = target[at, :] + source[at, :]
+            return carry
+
+        lax.fori_loop(0, row_total // 16, body, 0)
+
+    def spread(row):
+        for k in (3, 1, 2, 0):
+            flights[row]["core"][k].wait()
+            add(terms.at[row, tiles[names[k]]], core_terms.at[row, k], tokens)
+            if k == 3:
+                far = terms.at[row, tiles["xy"]]
+                flights[row]["far_x"] = send(row, 4, far.at[:, key_at], side_terms.at[row, 0], peers["x"])
+                flights[row]["far_y"] = send(row, 5, far.at[:, value_at], side_terms.at[row, 1], peers["y"])
+            if k == 1:
+                near = terms.at[row, tiles["x"]]
+                flights[row]["near_x"] = send(row, 6, near.at[:, key_at], side_terms.at[row, 2], peers["x"])
+            if k == 2:
+                near = terms.at[row, tiles["y"]]
+                flights[row]["near_y"] = send(row, 7, near.at[:, value_at], side_terms.at[row, 3], peers["y"])
+
+    def pass_on(row):
+        flights[row]["far_x"].wait()
+        near = terms.at[row, tiles["y"], :, key_at]
+        add(near, side_terms.at[row, 0], tokens)
+        flights[row]["last_y"] = send(row, 8, near, side_terms.at[row, 4], peers["y"])
+        flights[row]["far_y"].wait()
+        near = terms.at[row, tiles["x"], :, value_at]
+        add(near, side_terms.at[row, 1], tokens)
+        flights[row]["last_x"] = send(row, 9, near, side_terms.at[row, 5], peers["x"])
+
+    def close(row):
+        for name in ("near_x", "near_y", "last_x", "last_y"):
+            flights[row][name].wait()
+        mine = terms.at[row, tiles["own"]]
+
+        def body(i, carry):
+            at = pl.ds(pl.multiple_of(i * 16, 16), 16)
+            for start, first, second in ((0, 2, 4), (width, 3, 5)):
+                total = mine[at, start : start + width].astype(jnp.float32)
+                total = total + side_terms[row, first, at, :].astype(jnp.float32)
+                total = total + side_terms[row, second, at, :].astype(jnp.float32)
+                out[row, at, width + start : 2 * width + start] = total.astype(low)
+            return carry
+
+        lax.fori_loop(0, tokens // 16, body, 0)
+
+    for row in range(row_count):
+        compute(row)
+        begin(row)
+        if row > 0:
+            spread(row - 1)
+        if row > 1:
+            pass_on(row - 2)
+    spread(row_count - 1)
+    for row in range(max(row_count - 2, 0), row_count):
+        pass_on(row)
+    for row in range(row_count):
+        close(row)
+
+
+def attend_back(cuts, query, attended, grad, lse, all_pairs, tile_height, tile_width):
+    row_count, tokens, width = query.shape
+    tile_count = all_pairs.shape[1]
+    low = jnp.bfloat16
+    vmem = pl.BlockSpec(memory_space=pltpu.VMEM)
+    return pl.pallas_call(
+        functools.partial(attend_back_kernel, tile_height, tile_width),
+        out_shape=jax.ShapeDtypeStruct((row_count, tokens, 3 * width), low),
+        in_specs=[pl.BlockSpec(memory_space=pltpu.SMEM)] + [vmem] * 4 + [pl.BlockSpec(memory_space=pl.ANY)],
+        out_specs=vmem,
+        scratch_shapes=[
+            pltpu.VMEM((row_count, tile_count, tokens, 2 * width), low),
+            pltpu.VMEM((row_count, tile_count, tokens, 2 * width), low),
+            pltpu.VMEM((row_count, 4, tokens, 2 * width), low),
+            pltpu.VMEM((row_count, 6, tokens, width), low),
+            pltpu.VMEM((tile_count * tokens, tokens), jnp.float32),
+            pltpu.VMEM((8, 2 * tokens), jnp.float32),
+            pltpu.SemaphoreType.DMA((row_count,)),
+            pltpu.SemaphoreType.DMA((row_count, 10)),
+            pltpu.SemaphoreType.DMA((row_count, 10)),
+        ],
+        compiler_params=pltpu.CompilerParams(
+            collective_id=2, has_side_effects=True, vmem_limit_bytes=50 * 1024 * 1024
+        ),
+        name="attend_back",
+    )(cuts, query, attended, grad, lse, all_pairs)
 
 
 def sum_by_table(local_grads):
@@ -309,15 +689,8 @@
 ):
     row_count, tile_height, tile_width, model_width = skip_input.shape
     patch_width = latent.shape[3]
-    grid_side = segment_ids.shape[1]
     tile_tokens = tile_height * tile_width
     token_count = row_count * tile_tokens
-    row_tokens = grid_side * grid_side
-    head_count = HEADS
-    head_size = model_width // head_count
-    score_scale = head_size ** (-0.5)
-    band_count = lax.axis_size("ty")
-    column_count = lax.axis_size("tx")
     band_index = lax.axis_index("ty")
     column_index = lax.axis_index("tx")
     padded_ids = jnp.pad(segment_ids, ((0, 0), (1, 1), (1, 1)), constant_values=-1)
@@ -340,10 +713,10 @@
         ],
         axis=-1,
     )
-    key_ids = segment_ids.reshape(row_count, band_count, tile_height, column_count, tile_width)
-    key_ids = key_ids.transpose(0, 1, 3, 2, 4).reshape(row_count, row_tokens)
-    own_flat = own_ids.reshape(row_count, tile_tokens)
-    allowed = own_flat[:, None, :, None] == key_ids[:, None, None, :]
+    cuts = jnp.stack(
+        [jnp.sum(segment_ids[:, 0, :] == 0, axis=1), jnp.sum(segment_ids[:, :, -1] == 1, axis=1)],
+        axis=1,
+    ).astype(jnp.int32)
     flat_latent = latent.reshape(token_count, patch_width)
     flat_skip = skip_input.reshape(token_count, model_width)
     embedded = product(flat_latent, embed_weight, "tc,dc->td") + embed_bias.astype(jnp.float32)
@@ -354,24 +727,11 @@
     )
     normed_low = normed.astype(jnp.bfloat16)
     projected = product(normed_low, qkv_weight, "td,de->te").astype(jnp.bfloat16)
-    queries = projected[:, :model_width].reshape(row_count, tile_tokens, head_count, head_size)
+    queries = projected[:, :model_width].reshape(row_count, tile_tokens, model_width)
     local_pairs = projected[:, model_width:].reshape(row_count, tile_tokens, 2 * model_width)
-    row_pairs = lax.all_gather(local_pairs, ("ty", "tx"), axis=1, tiled=True)
-    row_keys = row_pairs[:, :, :model_width].reshape(row_count, row_tokens, head_count, head_size)
-    values = row_pairs[:, :, model_width:].reshape(row_count, row_tokens, head_count, head_size)
-
-    def masked_scores():
-        raw_scores = product(queries, row_keys, "rqhd,rkhd->rhqk") * score_scale
-        return jnp.where(allowed, raw_scores, masked_score)
-
-    scores = masked_scores()
-    row_peak = jnp.max(scores, axis=-1, keepdims=True)
-    exponents = jnp.exp(scores - row_peak)
-    row_total = jnp.sum(exponents, axis=-1, keepdims=True)
-    attention_weights = exponents / row_total
-    log_total = row_peak + jnp.log(row_total)
-    attended = product(attention_weights.astype(jnp.bfloat16), values, "rhqk,rkhd->rqhd")
-    attended = attended.astype(jnp.bfloat16).reshape(token_count, model_width)
+    attended, log_total, row_pairs = attend(cuts, queries, local_pairs, tile_height, tile_width)
+    attended_tiles = attended
+    attended = attended.reshape(token_count, model_width)
     stream_mid = (
         stream + product(attended, proj_weight, "td,de->te") + proj_bias.astype(jnp.float32)
     )
@@ -431,32 +791,16 @@
     proj_bias_grad = jnp.sum(mid_grad, axis=0)
     proj_weight_grad = product(attended, mid_low, "td,te->de")
     attended_grad = product(mid_low, proj_weight, "te,de->td").astype(jnp.bfloat16)
-    attended_grad = attended_grad.reshape(row_count, tile_tokens, head_count, head_size)
-    weights_again = jnp.exp(masked_scores() - log_total)
-    weights_grad = product(attended_grad, values, "rqhd,rkhd->rhqk")
-    weighted_sum = jnp.sum(weights_again * weights_grad, axis=-1, keepdims=True)
-    score_grad = (weights_again * (weights_grad - weighted_sum)).astype(jnp.bfloat16)
-    query_grad = product(score_grad, row_keys, "rhqk,rkhd->rqhd") * score_scale
-    value_grad = product(weights_again.astype(jnp.bfloat16), attended_grad, "rhqk,rqhd->rkhd")
-    key_grad = product(score_grad, queries, "rhqk,rqhd->rkhd") * score_scale
-    pair_terms = jnp.concatenate(
-        [
-            key_grad.reshape(row_count, row_tokens, model_width),
-            value_grad.reshape(row_count, row_tokens, model_width),
-        ],
-        axis=2,
-    )
-    own_pairs = lax.psum_scatter(
-        pair_terms.astype(jnp.bfloat16), ("ty", "tx"), scatter_dimension=1, tiled=True
-    ).astype(jnp.float32)
-    projected_grad = jnp.concatenate(
-        [
-            query_grad.reshape(token_count, model_width),
-            own_pairs.reshape(token_count, 2 * model_width),
-        ],
-        axis=1,
-    )
-    projected_grad = projected_grad.astype(jnp.bfloat16)
+    projected_grad = attend_back(
+        cuts,
+        queries,
+        attended_tiles,
+        attended_grad.reshape(row_count, tile_tokens, model_width),
+        log_total,
+        row_pairs,
+        tile_height,
+        tile_width,
+    ).reshape(token_count, 3 * model_width)
     qkv_weight_grad = product(normed_low, projected_grad, "td,te->de")
     normed_grad = product(projected_grad, qkv_weight, "te,de->td")
     stream_part, norm1_gain_grad, norm1_bias_grad = norm1_back(normed_grad)

time: 503 us -> 432 us (0.86)
  Pallas kernels: 116 us -> 231 us
  matrix products: 141 us -> 84.8 us
  local copies, waits for them, and re-layouts: 104 us -> 47.9 us
  other arithmetic: 78.1 us -> 38.5 us
  waiting for transfers between devices: 19.9 us -> 0.02 us
  between operations: 15.3 us -> 1.64 us
    pallas_call x0 -> x2, Pallas kernels: none -> 115 us  [the longest x1 59.5 us: attend_back(): pl.pallas_call(functools.partial(attend_back_kernel, tile_height, tile_wi...]
    dot_general x26 -> x20, matrix products: 141 us -> 84.8 us  [product(): jnp.einsum(pattern, former, latter, preferred_element_type=jnp.float32)]
    reshape x10 -> x0, local copies, waits for them, and re-layouts: 33.4 us -> none  [the longest x1 6.69 us: shards(): value_grad.reshape(row_count, row_tokens, model_width)]
    slice x4 -> x1, local copies, waits for them, and re-layouts: 23.3 us -> 0.85 us  [shards(): projected[:, :model_width].reshape(row_count, tile_tokens, model_width)]
    all_gather x1 -> x0, waiting for transfers between devices: 13.8 us -> none  [shards(): row_pairs = lax.all_gather(local_pairs, ('ty', 'tx'), axis=1, tiled=True)]
    convert_element_type x1 -> x0, other arithmetic: 13 us -> none  [shards(): (weights_again * (weights_grad - weighted_sum)).astype(jnp.bfloat16)]
    concatenate x1 -> x0, other arithmetic: 9.24 us -> none  [shards(): jnp.concatenate([key_grad.reshape(row_count, row_tokens, model_width), va...]
    reduce_sum x1 -> x2, other arithmetic: 10 us -> 2.41 us  [the longest x1 1.38 us: shards(): jnp.sum(segment_ids[:, 0, :] == 0, axis=1)]
  transfers between devices with their start and end apart: 10 -> 8, of which waited for: 2 -> 0; matrix products, arithmetic and copies ran while one was open for 19% -> 15% of each run, Pallas kernels for 0% -> 13%
where the time goes in v2:
time: 432 us; the launch traced here: 423 us
  Pallas kernels  231 us (53%)
  matrix products  84.8 us (20%)
  local copies, waits for them, and re-layouts  47.9 us (11%)
  other arithmetic  38.5 us (9%)
  starting transfers between devices  19.7 us (5%)
    pallas_call x1, Pallas kernels, grad_reduce(): pl.pallas_call(functools.partial(grad_reduce_kernel, shapes), out_shape=[...  116 us
    dot_general x20, matrix products, product(): jnp.einsum(pattern, former, latter, preferred_element_type=jnp.float32)  84.8 us
    pallas_call x1, Pallas kernels, attend_back(): pl.pallas_call(functools.partial(attend_back_kernel, tile_height, tile_wi...  59.5 us
    pallas_call x1, Pallas kernels, attend(): pl.pallas_call(functools.partial(attend_kernel, tile_height, tile_width),...  55.5 us
    ppermute x4, starting transfers between devices, with_halo(): before = lax.ppermute(last, axis, up)  14.2 us
    dot_general x5, local copies, waits for them, and re-layouts, product(): jnp.einsum(pattern, former, latter, preferred_element_type=jnp.float32)  12.7 us
    convert_element_type x9, local copies, waits for them, and re-layouts, sum_grads(): flat_part = jnp.concatenate([blocks[k].astype(low) for k in flat], axis=1)  10.5 us
    convert_element_type x5, other arithmetic, sum_grads(): totals = {k: part.astype(jnp.float32) for k, part in zip(order, summed)}  9.84 us
  transfers between devices with their start and end apart: 8, of which 0 were waited for; matrix products, arithmetic and copies ran while one was open for 15% of the time, Pallas kernels for 13%

profile of v2, /device:TPU:0, one launch (start us, length us, event | category | flops | bytes accessed | tf_op | source)
XLA Modules:
  0.0 423.5 jit_solution(14828355684404351598)
XLA Ops:
  0.7 1.5 fusion.106
  2.2 2.4 collective-permute-start.4
  4.5 1.3 collective-permute-start.5
  6.9 1.4 fusion.90
  11.0 1.2 fusion.30
  12.2 3.2 fusion.107
  16.4 1.7 convolution_convert_fusion.2
  20.0 1.3 convert_element_type.236
  22.0 1.3 copy.62
  25.1 1.3 copy-done.6
  26.4 55.5 %attend.1 = (bf16[3,128,768]{2,1,0:T(8,128)(2,1)S(1)}, f32[3,6,1,256]{3,2,1,0:T(1,128)S(1)}, bf16[3,8,128,1536]{3,2,1,0:T(8,128)(2,1)S(1)}) custom-call(s32[3,2]{1,0:T(4,128)S(1)} %pad_add_fusion.cuts, bf16[3,128,768]{2,1,0:T(8,128)(2,1)S(1)} %bitcast.153, bf16[3,128,1536]{2,1,0:T(8,128)(2,1)S(1)} %bitcast.155), custom_call_target="tpu_custom_call" | custom-call | tf_op jit(solution)/shard_map/attend/pallas_call | solution.py:411
  82.0 4.2 fusion.108
  88.7 1.6 fusion.77
  91.6 3.0 collective-permute-start.7
  94.6 1.6 collective-permute-start.6
  96.2 15.2 %fusion.3 = (bf16[3072,384]{0,1:T(8,128)(2,1)}, f32[384,3072]{1,0:T(8,128)}) fusion(f32[3072]{0:T(1024)S(1)} %convert_element_type.240, bf16[768,3072]{1,0:T(8,128)(2,1)} %param.34, f32[384,768]{1,0:T(8,128)S(1)} %get-tuple-element.154, f32[768]{0:T(1024)S(1)} %convert_element_type.238, f32[768]{0:T(1024)S(1)} %convert_element_type.237, f32[384]{0:T(512)S(1)} %fusion.89, ...), kind=kOutput, calls=%fused_computation.7 | convolution fusion | flops 1891270656 | bytes 12997632 | tf_op jit(solution)/shard_map/td,df->tf/dot_general | solution.py:43
  112.1 2.1 copy.64
  114.2 4.3 %copy.77 = bf16[3072,384]{1,0:T(8,128)(2,1)} copy(bf16[3072,384]{0,1:T(8,128)(2,1)} %get-tuple-element.157) | data formatting | bytes 4718592 | tf_op jit(solution)/shard_map/tf,td->fd/dot_general | solution.py:43
  118.5 2.4 fusion.76
  121.0 2.0 concatenate.46
  123.0 1.5 fusion.56
  124.5 1.5 fusion.103
  126.0 16.6 %fusion.97 = (bf16[3072]{0:T(1024)(128)(2,1)}, bf16[384,3072]{1,0:T(8,128)(2,1)S(1)}, f32[384,3072]{1,0:T(8,128)}) fusion(f32[384,3072]{1,0:T(8,128)} %get-tuple-element.158, f32[3072]{0:T(1024)} %copy-done.50, bf16[384,768]{1,0:T(8,128)(2,1)S(1)} %get-tuple-element.114, bf16[3072,768]{1,0:T(8,128)(2,1)} %param.36), kind=kOutput, calls=%fused_computation.204 | convolution fusion | flops 1899230208 | bytes 17123328 | tf_op jit(solution)/shard_map/td,fd->tf/dot_general | solution.py:43
  142.6 2.8 multiply_reduce_fusion
  145.5 4.7 %convolution_convert_fusion.1 = bf16[768,3072]{1,0:T(8,128)(2,1)} fusion(bf16[384,3072]{1,0:T(8,128)(2,1)S(1)} %get-tuple-element.99, f32[384,768]{1,0:T(8,128)S(1)} %copy-done.14, f32[768]{0:T(1024)S(1)} %copy-done.59, f32[768]{0:T(1024)S(1)} %copy-done.49, f32[384]{0:T(512)S(1)} %copy-done.54, f32[384]{0:T(512)S(1)} %copy-done.39), kind=kOutput, calls=%fused_computation.3 | convolution fusion | flops 1815773184 | bytes 8266752 | tf_op jit(solution)/shard_map/td,tf->df/dot_general | solution.py:43
  152.3 59.5 %attend_back.1 = bf16[3,128,2304]{2,1,0:T(8,128)(2,1)S(1)} custom-call(s32[3,2]{1,0:T(4,128)S(1)} %pad_add_fusion.cuts, bf16[3,128,768]{2,1,0:T(8,128)(2,1)S(1)} %bitcast.154, bf16[3,128,768]{2,1,0:T(8,128)(2,1)S(1)} %copy-done.3, bf16[3,128,768]{2,1,0:T(8,128)(2,1)S(1)} %bitcast.156, f32[3,6,1,256]{3,2,1,0:T(1,128)S(1)} %copy-done.10, ...), custom_call_target="tpu_custom_call" | custom-call | tf_op jit(solution)/shard_map/attend_back/pallas_call | solution.py:581
  211.9 2.3 multiply_reduce_fusion.1
  214.3 1.3 fusion.101
  217.6 2.8 convolution_convert_fusion.3
  222.2 1.8 convolution_convert_fusion.5.refs_0_
  224.0 2.2 copy.66
  226.2 8.3 %fusion.29 = bf16[384,768]{1,0:T(8,128)(2,1)} fusion(f32[384,768]{1,0:T(8,128)} %copy-done.13, bf16[3072,768]{1,0:T(8,128)(2,1)} %param.36, f32[384,3072]{1,0:T(8,128)} %get-tuple-element.100, f32[384,3072]{1,0:T(8,128)} %get-tuple-element.158, f32[3072]{0:T(1024)} %copy-done.50, f32[768]{0:T(1024)S(1)} %copy-done.57), kind=kOutput, calls=%fused_computation.57 | convolution fusion | flops 1817542656 | bytes 15940608 | tf_op jit(solution)/shard_map/tf,fd->td/dot_general | solution.py:43
  234.5 3.1 dot_general.102
  237.6 2.2 fusion.31
  239.8 2.0 copy.71
  241.8 2.1 copy.67
  243.9 2.0 convolution_convert_fusion.7
  245.9 1.6 copy.70
  247.5 1.3 convert_element_type.265
  248.8 1.3 convert_element_type.267
  250.1 1.3 convert_element_type.269
  251.4 1.3 convert_element_type.271
  254.1 1.3 convert_element_type.277
  255.4 1.3 convert_element_type.279
  256.7 1.3 convert_element_type.281
  258.0 1.4 concatenate.48
  260.9 6.7 %convolution_convert_fusion.4.refs_1_ = bf16[4,768,768]{2,1,0:T(8,128)(2,1)} fusion(bf16[4,768,384]{2,1,0:T(8,128)(2,1)} %bitcast.164, bf16[384,768,1]{1,0,2:T(8,128)(2,1)} %bitcast.170), kind=kOutput, calls=%fused_computation.44 | convolution fusion | flops 1814298624 | bytes 7667712 | tf_op jit(solution)/shard_map/tf,td->fd/dot_general | solution.py:43
  267.6 3.8 convolution_convert_fusion.refs_3_
  272.4 115.9 %grad_reduce.1 = (bf16[192,768]{1,0:T(8,128)(2,1)}, bf16[768,768]{1,0:T(8,128)(2,1)}, bf16[192,3072]{1,0:T(8,128)(2,1)}, bf16[192,2304]{1,0:T(8,128)(2,1)}, bf16...) custom-call(bf16[4,192,768]{2,1,0:T(8,128)(2,1)} %convolution_convert_fusion.5.refs_0_, ...), custom_call_target="tpu_custom_call" | custom-call | tf_op jit(solution)/shard_map/grad_reduce/pallas_call | solution.py:213
  388.3 1.4 slice_convert_fusion.3
  389.8 1.7 slice_convert_fusion.2
  391.4 1.3 collective-permute-start.1
  392.7 3.0 collective-permute-start
  398.1 1.3 collective-permute-start.3
  399.4 5.8 %collective-permute-start.2 = (bf16[3,10,1,768]{3,2,1,0:T(2,128)(2,1)}, bf16[3,10,1,768]{3,2,1,0:T(2,128)(2,1)}, u32[]{:S(2)}, u32[]{:S(2)}) collective-permute-start(bf16[3,10,1,768]{3,2,1,0:T(2,128)(2,1)} %get-tuple-element.115), channel_id=1, source_target_pairs={{0,1},{2,3},{4,5},{6,7},{8,9},{10,11},{12,13},{14,15},{16,17},{18,... | collective-permute-start | bytes 138248 | tf_op jit(solution)/shard_map/ppermute | solution.py:25
  405.9 1.6 copy.72
  407.4 2.3 convert_element_type.284
  409.7 2.5 convert_element_type.288
  412.2 1.8 convert_element_type.289
  414.0 1.7 convert_element_type.293
  415.7 1.6 convert_element_type.295
  417.3 1.7 copy.73
  419.0 2.0 fusion.35
  421.0 2.3 fusion.60
  (182 shorter events, 26.2 us)
Async XLA Ops:
  0.7 15.7 %copy-start = (bf16[768,2304]{1,0:T(8,128)(2,1)S(1)}, bf16[768,2304]{1,0:T(8,128)(2,1)}, u32[]{:S(2)}) copy-start(bf16[768,2304]{1,0:T(8,128)(2,1)} %param.29) | copy-start | bytes 10616836
  2.2 86.5 %collective-permute-start.4 = (bf16[3,1,16,16]{3,2,1,0:T(8,128)(2,1)}, bf16[3,1,16,16]{3,2,1,0:T(8,128)(2,1)S(1)}, u32[]{:S(2)}, u32[]{:S(2)}) collective-permute-start(bf16[3,1,16,16]{3,2,1,0:T(8,128)(2,1)} %get-tuple-element.134), channel_id=1, source_target_pairs={{0,2},{2,4},{4,6},{1,3},{3,5},{5,7},{8,10},{10,12},{12,14},{9,11},... | collective-permute-start | bytes 4616 | tf_op jit(solution)/shard_map/ppermute | solution.py:25
  4.5 84.1 %collective-permute-start.5 = (bf16[3,1,16,16]{3,2,1,0:T(8,128)(2,1)}, bf16[3,1,16,16]{3,2,1,0:T(8,128)(2,1)}, u32[]{:S(2)}, u32[]{:S(2)}) collective-permute-start(bf16[3,1,16,16]{3,2,1,0:T(8,128)(2,1)} %get-tuple-element.133), channel_id=1, source_target_pairs={{2,0},{4,2},{6,4},{3,1},{5,3},{7,5},{10,8},{12,10},{14,12},{11,9},... | collective-permute-start | bytes 4616 | tf_op jit(solution)/shard_map/ppermute | solution.py:26
  10.3 7.7 %copy-start.44 = (f32[768]{0:T(1024)}, f32[768]{0:T(1024)S(1)}, u32[]{:S(2)}) copy-start(f32[768]{0:T(1024)S(1)} %convert_element_type.233) | copy-start | bytes 9220
  11.0 7.0 %copy-start.46 = (f32[768]{0:T(1024)}, f32[768]{0:T(1024)S(1)}, u32[]{:S(2)}) copy-start(f32[768]{0:T(1024)S(1)} %convert_element_type.232) | copy-start | bytes 9220
  12.2 3.5 copy-start.22
  15.4 2.6 copy-start.11
  15.4 2.6 copy-start.36
  23.3 64.0 %copy-start.56 = (bf16[3072]{0:T(1024)(128)(2,1)S(1)}, bf16[3072]{0:T(1024)(128)(2,1)}, u32[]{:S(2)}) copy-start(bf16[3072]{0:T(1024)(128)(2,1)} %param.35) | copy-start | bytes 18436
  26.4 60.0 %copy-start.27 = (s32[3,32,32]{2,1,0:T(8,128)S(1)}, s32[3,32,32]{2,1,0:T(8,128)}, u32[]{:S(2)}) copy-start(s32[3,32,32]{2,1,0:T(8,128)} %param.22) | copy-start | bytes 36868
  26.4 62.3 %copy-start.25 = (bf16[3,8,16,16]{3,2,1,0:T(8,128)(2,1)S(1)}, bf16[3,8,16,16]{3,2,1,0:T(8,128)(2,1)}, u32[]{:S(2)}) copy-start(bf16[3,8,16,16]{3,2,1,0:T(8,128)(2,1)} %param.39) | copy-start | bytes 36868
  81.9 29.5 %copy-start.1 = (bf16[3,8,128,1536]{3,2,1,0:T(8,128)(2,1)}, bf16[3,8,128,1536]{3,2,1,0:T(8,128)(2,1)S(1)}, u32[]{:S(2)}) copy-start(bf16[3,8,128,1536]{3,2,1,0:T(8,128)(2,1)S(1)} %get-tuple-element.30.all_pairs) | copy-start | bytes 28311556
  81.9 29.5 %copy-start.2 = (bf16[3,128,768]{2,1,0:T(8,128)(2,1)}, bf16[3,128,768]{2,1,0:T(8,128)(2,1)S(1)}, u32[]{:S(2)}) copy-start(bf16[3,128,768]{2,1,0:T(8,128)(2,1)S(1)} %get-tuple-element.28.attended) | copy-start | bytes 1769476
  82.0 29.4 %copy-start.9 = (f32[3,6,1,256]{3,2,1,0:T(1,128)}, f32[3,6,1,256]{3,2,1,0:T(1,128)S(1)}, u32[]{:S(2)}) copy-start(f32[3,6,1,256]{3,2,1,0:T(1,128)S(1)} %get-tuple-element.29.lse) | copy-start | bytes 55300
  86.1 25.3 %copy-start.13 = (f32[384,768]{1,0:T(8,128)}, f32[384,768]{1,0:T(8,128)S(1)}, u32[]{:S(2)}) copy-start(f32[384,768]{1,0:T(8,128)S(1)} %get-tuple-element.154) | copy-start | bytes 3538948
  86.1 25.3 %copy-start.38 = (f32[384]{0:T(512)}, f32[384]{0:T(512)S(1)}, u32[]{:S(2)}) copy-start(f32[384]{0:T(512)S(1)} %broadcast_multiply_fusion) | copy-start | bytes 4612
  86.4 2.2 copy-start.42
  86.5 25.0 %copy-start.53 = (f32[384]{0:T(512)}, f32[384]{0:T(512)S(1)}, u32[]{:S(2)}) copy-start(f32[384]{0:T(512)S(1)} %fusion.89) | copy-start | bytes 4612
  87.2 24.2 %copy-start.32 = (pred[3,8,16]{2,1,0:T(8,128)(4,1)}, pred[3,8,16]{2,1,0:T(8,128)(4,1)S(1)}, u32[]{:S(2)}) copy-start(pred[3,8,16]{2,1,0:T(8,128)(4,1)S(1)} %get-tuple-element.137) | copy-start | bytes 1156
  87.2 24.2 %copy-start.35 = (pred[3,8,16]{2,1,0:T(8,128)(4,1)}, pred[3,8,16]{2,1,0:T(8,128)(4,1)S(1)}, u32[]{:S(2)}) copy-start(pred[3,8,16]{2,1,0:T(8,128)(4,1)S(1)} %get-tuple-element.142) | copy-start | bytes 1156
  87.3 24.2 %copy-start.50 = (f32[3072]{0:T(1024)}, f32[3072]{0:T(1024)S(1)}, u32[]{:S(2)}) copy-start(f32[3072]{0:T(1024)S(1)} %convert_element_type.240) | copy-start | bytes 36868
  88.0 23.5 %copy-start.58 = (f32[768]{0:T(1024)}, f32[768]{0:T(1024)S(1)}, u32[]{:S(2)}) copy-start(f32[768]{0:T(1024)S(1)} %convert_element_type.238) | copy-start | bytes 9220
  88.7 22.8 %copy-start.48 = (f32[768]{0:T(1024)}, f32[768]{0:T(1024)S(1)}, u32[]{:S(2)}) copy-start(f32[768]{0:T(1024)S(1)} %convert_element_type.237) | copy-start | bytes 9220
  91.0 20.5 %copy-start.26 = (bf16[3,10,16,16]{3,2,1,0:T(8,128)(2,1)}, bf16[3,10,16,16]{3,2,1,0:T(8,128)(2,1)S(1)}, u32[]{:S(2)}) copy-start(bf16[3,10,16,16]{3,2,1,0:T(8,128)(2,1)S(1)} %constant_dynamic-update-slice_fusion) | copy-start | bytes 46084
  91.6 26.9 %collective-permute-start.7 = (bf16[3,10,1,16]{3,2,1,0:T(2,128)(2,1)}, bf16[3,10,1,16]{3,2,1,0:T(2,128)(2,1)}, u32[]{:S(2)}, u32[]{:S(2)}) collective-permute-start(bf16[3,10,1,16]{3,2,1,0:T(2,128)(2,1)} %get-tuple-element.128), channel_id=1, source_target_pairs={{0,1},{2,3},{4,5},{6,7},{8,9},{10,11},{12,13},{14,15},{16,17},{18,... | collective-permute-start | bytes 2888 | tf_op jit(solution)/shard_map/ppermute | solution.py:25
  94.6 16.9 %copy-start.60 = (bf16[768]{0:T(1024)(128)(2,1)S(1)}, bf16[768]{0:T(1024)(128)(2,1)}, u32[]{:S(2)}) copy-start(bf16[768]{0:T(1024)(128)(2,1)} %param.37) | copy-start | bytes 4612
  94.6 23.9 %collective-permute-start.6 = (bf16[3,10,1,16]{3,2,1,0:T(2,128)(2,1)}, bf16[3,10,1,16]{3,2,1,0:T(2,128)(2,1)}, u32[]{:S(2)}, u32[]{:S(2)}) collective-permute-start(bf16[3,10,1,16]{3,2,1,0:T(2,128)(2,1)} %get-tuple-element.129), channel_id=1, source_target_pairs={{1,0},{3,2},{5,4},{7,6},{9,8},{11,10},{13,12},{15,14},{17,16},{19,... | collective-permute-start | bytes 2888 | tf_op jit(solution)/shard_map/ppermute | solution.py:26
  111.5 7.0 %copy-start.30 = (pred[3,8,16]{2,1,0:T(8,128)(4,1)S(1)}, pred[3,8,16]{2,1,0:T(8,128)(4,1)}, u32[]{:S(2)}) copy-start(pred[3,8,16]{2,1,0:T(8,128)(4,1)} %get-tuple-element.135) | copy-start | bytes 1156
  111.5 7.0 %copy-start.31 = (pred[3,8,16]{2,1,0:T(8,128)(4,1)S(1)}, pred[3,8,16]{2,1,0:T(8,128)(4,1)}, u32[]{:S(2)}) copy-start(pred[3,8,16]{2,1,0:T(8,128)(4,1)} %get-tuple-element.136) | copy-start | bytes 1156
  111.5 7.0 %copy-start.34 = (pred[3,8,16]{2,1,0:T(8,128)(4,1)S(1)}, pred[3,8,16]{2,1,0:T(8,128)(4,1)}, u32[]{:S(2)}) copy-start(pred[3,8,16]{2,1,0:T(8,128)(4,1)} %get-tuple-element.138) | copy-start | bytes 1156
  123.0 19.6 %slice-start = ((s8[4718592]{0:T(1024)(128)(4,1)}), s8[4194304]{0:T(1024)(128)(4,1)S(1)}, s32[]{:S(2)}) async-start(s8[4718592]{0:T(1024)(128)(4,1)} %bitcast.180), calls=%async_computation | async-start | bytes 8388608
  126.0 16.6 %copy-start.14 = (f32[384,768]{1,0:T(8,128)S(1)}, f32[384,768]{1,0:T(8,128)}, u32[]{:S(2)}) copy-start(f32[384,768]{1,0:T(8,128)} %copy-done.13) | copy-start | bytes 3538948
  126.0 16.6 %copy-start.39 = (f32[384]{0:T(512)S(1)}, f32[384]{0:T(512)}, u32[]{:S(2)}) copy-start(f32[384]{0:T(512)} %copy-done.38) | copy-start | bytes 4612
  126.0 16.6 %copy-start.49 = (f32[768]{0:T(1024)S(1)}, f32[768]{0:T(1024)}, u32[]{:S(2)}) copy-start(f32[768]{0:T(1024)} %copy-done.48) | copy-start | bytes 9220
  126.0 16.6 %copy-start.54 = (f32[384]{0:T(512)S(1)}, f32[384]{0:T(512)}, u32[]{:S(2)}) copy-start(f32[384]{0:T(512)} %copy-done.53) | copy-start | bytes 4612
  126.0 16.6 %slice-start.1 = ((s8[4718592]{0:T(1024)(128)(4,1)}), s8[524288]{0:T(1024)(128)(4,1)S(1)}, s32[]{:S(2)}) async-start(s8[4718592]{0:T(1024)(128)(4,1)} %bitcast.180), calls=%async_computation.1 | async-start | bytes 1048576
  142.6 2.8 copy-start.59
  145.5 4.7 %copy-start.43 = (f32[384]{0:T(512)S(1)}, f32[384]{0:T(512)}, u32[]{:S(2)}) copy-start(f32[384]{0:T(512)} %copy-done.42) | copy-start | bytes 4612
  150.2 2.1 copy-start.3
  150.2 2.1 copy-start.5
  150.2 2.1 copy-start.10
  152.3 59.5 %copy-start.12 = (f32[384,768]{1,0:T(8,128)S(1)}, f32[384,768]{1,0:T(8,128)}, u32[]{:S(2)}) copy-start(f32[384,768]{1,0:T(8,128)} %copy-done.11) | copy-start | bytes 3538948
  152.3 59.5 %copy-start.37 = (f32[384]{0:T(512)S(1)}, f32[384]{0:T(512)}, u32[]{:S(2)}) copy-start(f32[384]{0:T(512)} %copy-done.36) | copy-start | bytes 4612
  152.3 59.5 %copy-start.47 = (f32[768]{0:T(1024)S(1)}, f32[768]{0:T(1024)}, u32[]{:S(2)}) copy-start(f32[768]{0:T(1024)} %copy-done.46) | copy-start | bytes 9220
  152.3 59.5 %copy-start.52 = (f32[384]{0:T(512)S(1)}, f32[384]{0:T(512)}, u32[]{:S(2)}) copy-start(f32[384]{0:T(512)} %copy-done.51) | copy-start | bytes 4612
  211.8 2.4 copy-start.7
  211.9 2.4 copy-start.41
  211.9 2.4 copy-start.45
  214.3 2.2 copy-start.61
  217.6 4.6 %copy-start.17 = (bf16[768,384]{1,0:T(8,128)(2,1)S(1)}, bf16[768,384]{1,0:T(8,128)(2,1)}, u32[]{:S(2)}) copy-start(bf16[768,384]{1,0:T(8,128)(2,1)} %copy.64) | copy-start | bytes 1769476
  220.4 5.8 %copy-start.57 = (f32[768]{0:T(1024)S(1)}, f32[768]{0:T(1024)}, u32[]{:S(2)}) copy-start(f32[768]{0:T(1024)} %convert_element_type.242) | copy-start | bytes 9220
  234.5 18.2 %copy-start.55 = (bf16[768]{0:T(1024)(128)(2,1)S(1)}, bf16[768]{0:T(1024)(128)(2,1)}, u32[]{:S(2)}) copy-start(bf16[768]{0:T(1024)(128)(2,1)} %get-tuple-element.101) | copy-start | bytes 4612
  260.9 6.7 %copy-start.8 = (bf16[3,128,2304]{2,1,0:T(8,128)(2,1)S(1)}, bf16[3,128,2304]{2,1,0:T(8,128)(2,1)}, u32[]{:S(2)}) copy-start(bf16[3,128,2304]{2,1,0:T(8,128)(2,1)} %copy-done.7) | copy-start | bytes 5308420
  260.9 6.7 %copy-start.24 = (bf16[768,384]{1,0:T(8,128)(2,1)S(1)}, bf16[768,384]{1,0:T(8,128)(2,1)}, u32[]{:S(2)}) copy-start(bf16[768,384]{1,0:T(8,128)(2,1)} %copy.66) | copy-start | bytes 1769476
  267.6 3.8 copy-start.18
  267.6 3.8 copy-start.21
  272.4 119.1 %copy-start.16 = (bf16[384,768]{1,0:T(8,128)(2,1)S(1)}, bf16[384,768]{1,0:T(8,128)(2,1)}, u32[]{:S(2)}) copy-start(bf16[384,768]{1,0:T(8,128)(2,1)} %fusion.29) | copy-start | bytes 1769476
  391.4 5.8 %collective-permute-start.1 = (bf16[3,1,16,768]{3,2,1,0:T(8,128)(2,1)S(1)}, bf16[3,1,16,768]{3,2,1,0:T(8,128)(2,1)S(1)}, u32[]{:S(2)}, u32[]{:S(2)}) collective-permute-start(bf16[3,1,16,768]{3,2,1,0:T(8,128)(2,1)S(1)} %get-tuple-element.118), channel_id=1, source_target_pairs={{2,0},{4,2},{6,4},{3,1},{5,3},{7,5},{10,8},{12,10},{14,12},{11,9},... | collective-permute-start | bytes 221192 | tf_op jit(solution)/shard_map/ppermute | solution.py:26
  392.7 4.5 %collective-permute-start = (bf16[3,1,16,768]{3,2,1,0:T(8,128)(2,1)S(1)}, bf16[3,1,16,768]{3,2,1,0:T(8,128)(2,1)S(1)}, u32[]{:S(2)}, u32[]{:S(2)}) collective-permute-start(bf16[3,1,16,768]{3,2,1,0:T(8,128)(2,1)S(1)} %get-tuple-element.117), channel_id=1, source_target_pairs={{0,2},{2,4},{4,6},{1,3},{3,5},{5,7},{8,10},{10,12},{12,14},{9,11},... | collective-permute-start | bytes 221192 | tf_op jit(solution)/shard_map/ppermute | solution.py:25
  398.1 20.9 %collective-permute-start.3 = (bf16[3,10,1,768]{3,2,1,0:T(2,128)(2,1)}, bf16[3,10,1,768]{3,2,1,0:T(2,128)(2,1)}, u32[]{:S(2)}, u32[]{:S(2)}) collective-permute-start(bf16[3,10,1,768]{3,2,1,0:T(2,128)(2,1)} %get-tuple-element.116), channel_id=1, source_target_pairs={{1,0},{3,2},{5,4},{7,6},{9,8},{11,10},{13,12},{15,14},{17,16},{19,... | collective-permute-start | bytes 138248 | tf_op jit(solution)/shard_map/ppermute | solution.py:26
  399.4 19.6 %collective-permute-start.2 = (bf16[3,10,1,768]{3,2,1,0:T(2,128)(2,1)}, bf16[3,10,1,768]{3,2,1,0:T(2,128)(2,1)}, u32[]{:S(2)}, u32[]{:S(2)}) collective-permute-start(bf16[3,10,1,768]{3,2,1,0:T(2,128)(2,1)} %get-tuple-element.115), channel_id=1, source_target_pairs={{0,1},{2,3},{4,5},{6,7},{8,9},{10,11},{12,13},{14,15},{16,17},{18,... | collective-permute-start | bytes 138248 | tf_op jit(solution)/shard_map/ppermute | solution.py:25
  407.4 6.6 %copy-start.20 = (bf16[192,3072]{1,0:T(8,128)(2,1)S(1)}, bf16[192,3072]{1,0:T(8,128)(2,1)}, u32[]{:S(2)}) copy-start(bf16[192,3072]{1,0:T(8,128)(2,1)} %get-tuple-element.36) | copy-start | bytes 3538948
  407.4 8.3 %copy-start.19 = (bf16[768,768]{1,0:T(8,128)(2,1)S(1)}, bf16[768,768]{1,0:T(8,128)(2,1)}, u32[]{:S(2)}) copy-start(bf16[768,768]{1,0:T(8,128)(2,1)} %get-tuple-element.37) | copy-start | bytes 3538948
  415.7 5.3 %copy-start.33 = (pred[3,8,16]{2,1,0:T(8,128)(4,1)S(1)}, pred[3,8,16]{2,1,0:T(8,128)(4,1)}, u32[]{:S(2)}) copy-start(pred[3,8,16]{2,1,0:T(8,128)(4,1)} %copy-done.32) | copy-start | bytes 1156
  (9 other events, 11.6 us)

commit v3 on v1

v3 whole, which is shorter than its diff:
```python
import functools

import jax
import jax.numpy as jnp
from jax import lax
from jax.experimental import pallas as pl
from jax.experimental.pallas import tpu as pltpu
from jax.sharding import PartitionSpec as P

MESH = pl.DeviceIdType.MESH
norm_eps = 1e-05


def cell_of(token, tile, tile_height, tile_width, columns):
    down = tile // columns * tile_height + token // tile_width
    across = tile % columns * tile_width + token % tile_width
    return down, across


def fill_shift(shift_ref, tile_height, tile_width):
    tokens = tile_height * tile_width
    bands, columns = lax.axis_size("ty"), lax.axis_size("tx")
    own = lax.axis_index("ty") * columns + lax.axis_index("tx")
    lane = lax.broadcasted_iota(jnp.int32, (8, tokens), 1)
    down, across = cell_of(lane, own, tile_height, tile_width, columns)
    step = lax.broadcasted_iota(jnp.int32, (shift_ref.shape[0], tokens), 0)
    for p in range(9):
        i, j = down - (p // 3 - 1), across - (p % 3 - 1)
        inside = (i >= 0) & (i < bands * tile_height) & (j >= 0) & (j < columns * tile_width)
        tile = i // tile_height * columns + j // tile_width
        place = tile * tokens + i % tile_height * tile_width + j % tile_width
        place = jnp.where(inside, place, -1)[0:1]
        chosen = jnp.where(step == place, 1.0, 0.0)
        shift_ref[:, p * tokens : (p + 1) * tokens] = chosen.astype(jnp.bfloat16)


def same_image(cuts_ref, row, p, tile_height, tile_width):
    tokens = tile_height * tile_width
    columns = lax.axis_size("tx")
    own = lax.axis_index("ty") * columns + lax.axis_index("tx")
    lane = lax.broadcasted_iota(jnp.int32, (8, tokens), 1)
    down, across = cell_of(lane, own, tile_height, tile_width, columns)
    left_width, top_height = cuts_ref[row, 0], cuts_ref[row, 1]

    def image_of(i, j):
        return jnp.where(j < left_width, 0, jnp.where(i < top_height, 1, 2))

    there = image_of(down - (p // 3 - 1), across - (p % 3 - 1))
    return jnp.where(image_of(down, across) == there, 1.0, 0.0)[0:1]


def mm(former, latter, axis_former, axis_latter):
    return lax.dot_general(
        former,
        latter,
        (((axis_former,), (axis_latter,)), ((), ())),
        preferred_element_type=jnp.float32,
    )


def normalised(values):
    average = jnp.mean(values, axis=1, keepdims=True)
    centred = values - average
    rate = lax.rsqrt(jnp.mean(centred * centred, axis=1, keepdims=True) + norm_eps)
    return centred * rate, rate


def norm_back(incoming, unit, rate, gain):
    scaled = incoming * gain
    first = jnp.mean(scaled, axis=1, keepdims=True)
    second = jnp.mean(scaled * unit, axis=1, keepdims=True)
    return (scaled - first - unit * second) * rate


def down_sum(values):
    return jnp.sum(values, axis=0, keepdims=True)


def front_kernel(latent, skip, embed_weight, skip_weight, qkv_weight, vectors, embedded, stream, normed, query, pairs):
    width = skip.shape[1]
    row_count, tokens = query.shape[0], query.shape[1]
    for row in range(row_count):
        at = slice(row * tokens, (row + 1) * tokens)
        entered = (mm(latent[at, :], embed_weight[...], 1, 1) + vectors[0:1]).astype(jnp.bfloat16)
        embedded[at, :] = entered
        total = mm(entered, skip_weight[:width], 1, 0) + mm(skip[at, :], skip_weight[width:], 1, 0) + vectors[1:2]
        stream[at, :] = total
        unit, rate = normalised(total)
        low = (unit * vectors[2:3] + vectors[3:4]).astype(jnp.bfloat16)
        normed[at, :] = low
        query[row] = mm(low, qkv_weight[:, :width], 1, 0).astype(jnp.bfloat16)
        pairs[row] = mm(low, qkv_weight[:, width:], 1, 0).astype(jnp.bfloat16)


def front(latent, skip, embed_weight, skip_weight, qkv_weight, vectors, row_count):
    token_count, width = skip.shape
    tokens = token_count // row_count
    low = jnp.bfloat16
    return pl.pallas_call(
        front_kernel,
        out_shape=[
            jax.ShapeDtypeStruct((token_count, width), low),
            jax.ShapeDtypeStruct((token_count, width), jnp.float32),
            jax.ShapeDtypeStruct((token_count, width), low),
            jax.ShapeDtypeStruct((row_count, tokens, width), low),
            jax.ShapeDtypeStruct((row_count, tokens, 2 * width), low),
        ],
        compiler_params=pltpu.CompilerParams(vmem_limit_bytes=32 * 1024 * 1024),
        name="front",
    )(latent, skip, embed_weight, skip_weight, qkv_weight, vectors)


def erf_of(values):
    x = jnp.clip(values, -4.0, 4.0)
    square = x * x
    upper = square * -2.72614225801306e-10 + 2.77068142495902e-08
    for term in (-2.10102402082508e-06, -5.69250639462346e-05, -7.34990630326855e-04, -2.95459980854025e-03, -1.60960333262415e-02):
        upper = upper * square + term
    lower = square * -1.45660718464996e-05 + -2.13374055278905e-04
    for term in (-1.68282697438203e-03, -7.37332916720468e-03, -1.42647390514189e-02):
        lower = lower * square + term
    return x * upper / lower


def middle_kernel(
    tile_height, tile_width,
    cuts, attended, stream, cot_tiles, proj_weight, conv_turned, vectors, hidden_bias, fc1_weight, fc2_weight,
    fc1_grad, fc2_grad, hidden_bias_grad, proj_grad, attended_grad, mid_grad, conv_in, spread, vector_grads,
    middle, normed, out_grad, out_low, forward_sum, backward_sum, shift,
):
    step = pl.program_id(0)
    row_count, tokens = cot_tiles.shape[1], cot_tiles.shape[3]
    token_count = row_count * tokens
    low = jnp.bfloat16
    parts = [slice(k * tokens, (k + 1) * tokens) for k in range(row_count)]

    @pl.when(step == 0)
    def _():
        fill_shift(shift, tile_height, tile_width)
        tile_count = cot_tiles.shape[0]
        patch = cot_tiles.shape[2]
        turned = jnp.concatenate(
            [cot_tiles[t].reshape(row_count * patch, tokens) for t in range(tile_count)], axis=1
        )
        moved = mm(turned, shift[...], 1, 0)
        for row in range(row_count):
            for p in range(9):
                piece = moved[row * patch : (row + 1) * patch, p * tokens : (p + 1) * tokens]
                piece = piece * same_image(cuts, row, p, tile_height, tile_width)
                spread[p * patch : (p + 1) * patch, parts[row]] = piece.astype(low)
        total = jnp.zeros((1, stream.shape[1]), jnp.float32)
        for at in parts:
            grad = mm(spread[:, at], conv_turned[...], 0, 0)
            out_grad[at, :] = grad
            out_low[at, :] = grad.astype(low)
            total = total + down_sum(grad)
            value = stream[at, :] + mm(attended[at, :], proj_weight[...], 1, 0) + vectors[4:5]
            middle[at, :] = value
            unit, rate = normalised(value)
            normed[at, :] = (unit * vectors[5:6] + vectors[6:7]).astype(low)
        vector_grads[7:8] = total
        forward_sum[...] = jnp.zeros_like(forward_sum)
        backward_sum[...] = jnp.zeros_like(backward_sum)

    bias_grad = jnp.zeros((1, fc1_weight.shape[1]), jnp.float32)
    actives, hidden_lows = [], []
    for at in parts:
        hidden = mm(normed[at, :], fc1_weight[...], 1, 0) + hidden_bias[0]
        active_grad = mm(out_low[at, :], fc2_weight[...], 1, 1)
        share = 0.5 + 0.5 * erf_of(hidden * 0.7071067811865476)
        density = jnp.exp(hidden * hidden * -0.5) * 0.3989422804014327
        active = (hidden * share).astype(low)
        hidden_grad = active_grad * (share + hidden * density)
        bias_grad = bias_grad + down_sum(hidden_grad)
        hidden_low = hidden_grad.astype(low)
        forward_sum[at, :] = forward_sum[at, :] + mm(active, fc2_weight[...], 1, 0)
        backward_sum[at, :] = backward_sum[at, :] + mm(hidden_low, fc1_weight[...], 1, 1)
        actives.append(active)
        hidden_lows.append(hidden_low)
    hidden_bias_grad[0] = bias_grad
    fc2_grad[...] = mm(jnp.concatenate(actives, axis=0), out_low[...], 0, 0).astype(low)
    fc1_grad[...] = mm(normed[...], jnp.concatenate(hidden_lows, axis=0), 0, 0).astype(low)

    @pl.when(step == pl.num_programs(0) - 1)
    def _():
        width = stream.shape[1]
        gain_sum = jnp.zeros((1, width), jnp.float32)
        bias_sum = jnp.zeros((1, width), jnp.float32)
        mid_sum = jnp.zeros((1, width), jnp.float32)
        lows = []
        for at in parts:
            unit, rate = normalised(middle[at, :])
            conv_in[at, :] = (middle[at, :] + forward_sum[at, :] + vectors[7:8]).astype(low)
            incoming = backward_sum[at, :]
            gain_sum = gain_sum + down_sum(incoming * unit)
            bias_sum = bias_sum + down_sum(incoming)
            grad = out_grad[at, :] + norm_back(incoming, unit, rate, vectors[5:6])
            mid_grad[at, :] = grad
            mid_sum = mid_sum + down_sum(grad)
            mid_low = grad.astype(low)
            lows.append(mid_low)
            attended_grad[at, :] = mm(mid_low, proj_weight[...], 1, 1).astype(low)
        proj_grad[...] = mm(attended[...], jnp.concatenate(lows, axis=0), 0, 0).astype(low)
        vector_grads[4:5] = mid_sum
        vector_grads[5:6] = gain_sum
        vector_grads[6:7] = bias_sum


def middle(cuts, attended, stream, cot_tiles, proj_weight, conv_turned, vectors, hidden_bias, fc1_weight, fc2_weight, tile_height, tile_width):
    token_count, width = stream.shape
    hidden_width = fc1_weight.shape[1]
    block = 512
    steps = hidden_width // block
    low = jnp.bfloat16
    vmem = pl.BlockSpec(memory_space=pltpu.VMEM)
    tile_count, tokens = cot_tiles.shape[0], cot_tiles.shape[3]
    taps = conv_turned.shape[0]
    return pl.pallas_call(
        functools.partial(middle_kernel, tile_height, tile_width),
        grid=(steps,),
        out_shape=[
            jax.ShapeDtypeStruct((width, hidden_width), low),
            jax.ShapeDtypeStruct((hidden_width, width), low),
            jax.ShapeDtypeStruct((steps, 1, block), jnp.float32),
            jax.ShapeDtypeStruct((width, width), low),
            jax.ShapeDtypeStruct((token_count, width), low),
            jax.ShapeDtypeStruct((token_count, width), jnp.float32),
            jax.ShapeDtypeStruct((token_count, width), low),
            jax.ShapeDtypeStruct((taps, token_count), low),
            jax.ShapeDtypeStruct((8, width), jnp.float32),
        ],
        in_specs=[pl.BlockSpec(memory_space=pltpu.SMEM)]
        + [vmem] * 6
        + [
            pl.BlockSpec((1, 1, block), lambda k: (k, 0, 0)),
            pl.BlockSpec((width, block), lambda k: (0, k)),
            pl.BlockSpec((block, width), lambda k: (k, 0)),
        ],
        out_specs=[
            pl.BlockSpec((width, block), lambda k: (0, k)),
            pl.BlockSpec((block, width), lambda k: (k, 0)),
            pl.BlockSpec((1, 1, block), lambda k: (k, 0, 0)),
        ]
        + [vmem] * 6,
        scratch_shapes=[
            pltpu.VMEM((token_count, width), jnp.float32),
            pltpu.VMEM((token_count, width), low),
            pltpu.VMEM((token_count, width), jnp.float32),
            pltpu.VMEM((token_count, width), low),
            pltpu.VMEM((token_count, width), jnp.float32),
            pltpu.VMEM((token_count, width), jnp.float32),
            pltpu.VMEM((tile_count * tokens, 9 * tokens), low),
        ],
        compiler_params=pltpu.CompilerParams(vmem_limit_bytes=40 * 1024 * 1024),
        name="middle",
    )(cuts, attended, stream, cot_tiles, proj_weight, conv_turned, vectors, hidden_bias, fc1_weight, fc2_weight)


def rear_kernel(
    projected_grad, qkv_weight, normed, stream, mid_grad, embedded, skip, latent, skip_weight, vectors,
    middle_grads, hidden_bias_grad, conv_grad, qkv_grad, skip_grad, skip_input_grad, thin, flat, stream_low,
):
    token_count, width = stream.shape
    low = jnp.bfloat16
    tokens = 128
    parts = [slice(k * tokens, (k + 1) * tokens) for k in range(token_count // tokens)]
    zero = jnp.zeros((1, width), jnp.float32)
    gain_sum, bias_sum, stream_sum, embed_sum = zero, zero, zero, zero
    for at in parts:
        incoming = mm(projected_grad[at, :], qkv_weight[...], 1, 1)
        unit, rate = normalised(stream[at, :])
        gain_sum = gain_sum + down_sum(incoming * unit)
        bias_sum = bias_sum + down_sum(incoming)
        grad = mid_grad[at, :] + norm_back(incoming, unit, rate, vectors[2:3])
        stream_sum = stream_sum + down_sum(grad)
        stream_low[at, :] = grad.astype(low)
    embed_lows = []
    for at in parts:
        embed_grad = mm(stream_low[at, :], skip_weight[:width], 1, 1)
        embed_sum = embed_sum + down_sum(embed_grad)
        embed_lows.append(embed_grad.astype(low))
        skip_input_grad[at, :] = mm(stream_low[at, :], skip_weight[width:], 1, 1).astype(low)
    qkv_grad[...] = mm(normed[...], projected_grad[...], 0, 0).astype(low)
    skip_grad[:width] = mm(embedded[...], stream_low[...], 0, 0).astype(low)
    skip_grad[width:] = mm(skip[...], stream_low[...], 0, 0).astype(low)
    embed_weight_grad = mm(jnp.concatenate(embed_lows, axis=0), latent[...], 0, 0)
    thin[:, :128] = conv_grad[:, :128].astype(low)
    rest = jnp.zeros((width, 128 - 2 * 16), jnp.float32)
    thin[:, 128:] = jnp.concatenate([conv_grad[:, 128:144], embed_weight_grad, rest], axis=1).astype(low)
    rows = [embed_sum, stream_sum, gain_sum, bias_sum] + [middle_grads[k : k + 1] for k in range(4, 8)]
    stack = jnp.concatenate(rows, axis=0)
    share = width // 4
    for block in range(4):
        own = stack[:, block * share : (block + 1) * share]
        own = jnp.concatenate([own, jnp.zeros((8, 256 - share), jnp.float32)], axis=1)
        line = hidden_bias_grad[block : block + 1]
        pieces = [line[:, k * 256 : (k + 1) * 256] for k in range(width // 256)]
        body = jnp.concatenate([own] + pieces + [jnp.zeros((8 - len(pieces), 256), jnp.float32)], axis=0)
        flat[block, 0:16] = body.astype(low)
        flat[block, 16:64] = jnp.zeros((48, 256), low)


def rear(projected_grad, qkv_weight, normed, stream, mid_grad, embedded, skip, latent, skip_weight, vectors, middle_grads, hidden_bias_grad, conv_grad):
    token_count, width = stream.shape
    low = jnp.bfloat16
    return pl.pallas_call(
        rear_kernel,
        out_shape=[
            jax.ShapeDtypeStruct((width, 3 * width), low),
            jax.ShapeDtypeStruct((2 * width, width), low),
            jax.ShapeDtypeStruct((token_count, width), low),
            jax.ShapeDtypeStruct((width, 256), low),
            jax.ShapeDtypeStruct((4, 64, 256), low),
        ],
        scratch_shapes=[pltpu.VMEM((token_count, width), low)],
        compiler_params=pltpu.CompilerParams(vmem_limit_bytes=40 * 1024 * 1024),
        name="rear",
    )(projected_grad, qkv_weight, normed, stream, mid_grad, embedded, skip, latent, skip_weight, vectors, middle_grads, hidden_bias_grad, conv_grad)


def plane_peers():
    z, ty, y = lax.axis_index("rows"), lax.axis_index("ty"), lax.axis_index("tx")
    core, x = lax.rem(ty, 2), ty // 2
    here = x * 2 + core
    across = (1 - x) * 2 + core
    tiles = {
        "own": here * 2 + y,
        "x": across * 2 + y,
        "y": here * 2 + 1 - y,
        "xy": across * 2 + 1 - y,
    }
    peers = {
        "core": (z, x * 2 + 1 - core, y),
        "x": (z, across, y),
        "y": (z, here, 1 - y),
    }
    return tiles, peers


def plane_peer(k):
    z, ty, y = lax.axis_index("rows"), lax.axis_index("ty"), lax.axis_index("tx")
    x, core = ty // 2, lax.rem(ty, 2)
    flip_x, flip_core, flip_y = k // 4, k // 2 % 2, k % 2
    x = x + flip_x - 2 * flip_x * x
    core = core + flip_core - 2 * flip_core * core
    y = y + flip_y - 2 * flip_y * y
    return (z, x * 2 + core, y), (x * 2 + core) * 2 + y


def greet(peers):
    barrier = pltpu.get_barrier_semaphore()
    for peer in peers:
        pl.semaphore_signal(barrier, inc=1, device_id=peer, device_id_type=MESH)
    pl.semaphore_wait(barrier, len(peers))


def fill_mask(mask_ref, cuts_ref, row, tile_height, tile_width):
    ty, tx = lax.axis_index("ty"), lax.axis_index("tx")
    columns = lax.axis_size("tx")
    tokens = tile_height * tile_width
    left_width = cuts_ref[row, 0]
    top_height = cuts_ref[row, 1]

    def image_of(down, across):
        return jnp.where(across < left_width, 0, jnp.where(down < top_height, 1, 2))

    lane = lax.broadcasted_iota(jnp.int32, (tokens, tokens), 1)
    step = lax.broadcasted_iota(jnp.int32, (tokens, tokens), 0)
    mine = image_of(
        ty * tile_height + lane // tile_width, tx * tile_width + lane % tile_width
    )
    for tile in range(mask_ref.shape[0] // tokens):
        theirs = image_of(
            tile // columns * tile_height + step // tile_width,
            tile % columns * tile_width + step % tile_width,
        )
        mask_ref[tile * tokens : (tile + 1) * tokens, :] = jnp.where(
            mine == theirs, 0.0, -1e30
        )


def two_heads(pair, scale):
    lane = lax.broadcasted_iota(jnp.int32, pair.shape, 1)
    wide = pair.astype(jnp.float32) * scale
    first = jnp.where(lane < pair.shape[1] // 2, wide, 0.0)
    return jnp.concatenate([first, wide - first], axis=0).astype(jnp.bfloat16)


def own_blocks(both):
    head, tokens = both.shape[0] // 2, both.shape[1] // 2
    return jnp.concatenate([both[:head, :tokens], both[head:, tokens:]], axis=0)


def attend_kernel(
    tile_height, tile_width, cuts, query, pairs, cot, out, lse, all_out, cot_out, held, scores, mask, local_sem, send_sem, recv_sem,
    cot_sem, cot_send_sem, cot_recv_sem
):
    row_count, tokens, width = query.shape
    tile_count = held.shape[1]
    pair_count = width // 128
    tiles, peers = plane_peers()
    own = tiles["own"]
    greet([plane_peer(k)[0] for k in range(1, tile_count)])
    cot_copies = [pltpu.make_async_copy(cot, cot_out.at[own], cot_sem.at[0])]
    for k in range(1, tile_count):
        cot_copies.append(
            pltpu.make_async_remote_copy(
                src_ref=cot,
                dst_ref=cot_out.at[own],
                send_sem=cot_send_sem.at[k],
                recv_sem=cot_recv_sem.at[k],
                device_id=plane_peer(k)[0],
                device_id_type=MESH,
            )
        )

    def send(row, slot, source, target, peer):
        copy = pltpu.make_async_remote_copy(
            src_ref=source,
            dst_ref=target,
            send_sem=send_sem.at[row, slot],
            recv_sem=recv_sem.at[row, slot],
            device_id=peer,
            device_id_type=MESH,
        )
        copy.start()
        return copy

    flights = [{} for _ in range(row_count)]

    def begin(row):
        here = held.at[row, own]
        source = pairs.at[row]
        flights[row]["x"] = send(row, 0, source, here, peers["x"])
        flights[row]["y"] = send(row, 1, source, here, peers["y"])
        flights[row]["core"] = send(row, 2, source, here, peers["core"])
        keep = pltpu.make_async_copy(source, here, local_sem.at[row, 0])
        keep.start()
        flights[row]["keep"] = keep

    def forward(row):
        flights[row]["y"].wait_recv()
        key_half = held.at[row, tiles["y"], :, pl.ds(0, width)]
        flights[row]["far_x"] = send(row, 3, key_half, key_half, peers["x"])
        flights[row]["x"].wait_recv()
        value_half = held.at[row, tiles["x"], :, pl.ds(width, width)]
        flights[row]["far_y"] = send(row, 4, value_half, value_half, peers["y"])
        for slot, name in ((5, "x"), (6, "y")):
            tile = held.at[row, tiles[name]]
            flights[row]["core_" + name] = send(row, slot, tile, tile, peers["core"])

    def finish(row):
        flights[row]["far_x"].wait_recv()
        flights[row]["far_y"].wait_recv()
        tile = held.at[row, tiles["xy"]]
        last = send(row, 7, tile, tile, peers["core"])
        flights[row]["keep"].wait()
        for name in ("core", "core_x", "core_y"):
            flights[row][name].wait_recv()
        last.wait_recv()
        for name in ("x", "y", "core", "far_x", "far_y", "core_x", "core_y"):
            flights[row][name].wait_send()
        last.wait_send()
        keep = pltpu.make_async_copy(held.at[row], all_out.at[row], local_sem.at[row, 1])
        keep.start()
        flights[row]["out"] = keep

    chunk = 2

    def compute(row):
        fill_mask(mask, cuts, row, tile_height, tile_width)

        def one_pair(p, carry):
            at = pl.ds(pl.multiple_of(p * 128, 128), 128)
            at_value = pl.ds(pl.multiple_of(width + p * 128, 128), 128)
            both = two_heads(query[row, :, at], 0.125)
            peak = None
            for c in range(tile_count // chunk):
                span = slice(c * chunk * tokens, (c + 1) * chunk * tokens)
                keys = held[row, c * chunk : (c + 1) * chunk, :, at].reshape(chunk * tokens, 128)
                extra = mask[span, :]
                part = mm(keys, both, 1, 1) + jnp.concatenate([extra, extra], axis=1)
                scores[span, :] = part
                top = jnp.max(part, axis=0, keepdims=True)
                peak = top if peak is None else jnp.maximum(peak, top)
            total = jnp.zeros_like(peak)
            summed = jnp.zeros((128, 2 * tokens), jnp.float32)
            for c in range(tile_count // chunk):
                span = slice(c * chunk * tokens, (c + 1) * chunk * tokens)
                values = held[row, c * chunk : (c + 1) * chunk, :, at_value].reshape(chunk * tokens, 128)
                part = jnp.exp(scores[span, :] - peak)
                total = total + jnp.sum(part, axis=0, keepdims=True)
                summed = summed + mm(values, part.astype(jnp.bfloat16), 0, 0)
            blocks = own_blocks(summed / total)
            out[row, :, at] = jnp.transpose(blocks).astype(jnp.bfloat16)
            lse[row, p] = peak + jnp.log(total)
            return carry

        lax.fori_loop(0, pair_count, one_pair, 0)

    begin(0)
    if row_count > 1:
        begin(1)
    for copy in cot_copies:
        copy.start()
    forward(0)
    for row in range(row_count):
        if row + 2 < row_count:
            begin(row + 2)
        if row + 1 < row_count:
            forward(row + 1)
        finish(row)
        compute(row)
    for row in range(row_count):
        flights[row]["out"].wait()
    for copy in cot_copies:
        copy.wait()


def attend(cuts, query, pairs, cot, tile_height, tile_width):
    row_count, tokens, width = query.shape
    tile_count = lax.axis_size("ty") * lax.axis_size("tx")
    pair_count = width // 128
    low = jnp.bfloat16
    vmem = pl.BlockSpec(memory_space=pltpu.VMEM)
    return pl.pallas_call(
        functools.partial(attend_kernel, tile_height, tile_width),
        out_shape=[
            jax.ShapeDtypeStruct((row_count, tokens, width), low),
            jax.ShapeDtypeStruct((row_count, pair_count, 1, 2 * tokens), jnp.float32),
            jax.ShapeDtypeStruct((row_count, tile_count, tokens, 2 * width), low),
            jax.ShapeDtypeStruct((tile_count,) + cot.shape, low),
        ],
        in_specs=[pl.BlockSpec(memory_space=pltpu.SMEM), vmem] + [pl.BlockSpec(memory_space=pl.ANY)] * 2,
        out_specs=[vmem, vmem] + [pl.BlockSpec(memory_space=pl.ANY)] * 2,
        scratch_shapes=[
            pltpu.VMEM((row_count, tile_count, tokens, 2 * width), low),
            pltpu.VMEM((tile_count * tokens, 2 * tokens), jnp.float32),
            pltpu.VMEM((tile_count * tokens, tokens), jnp.float32),
            pltpu.SemaphoreType.DMA((row_count, 2)),
            pltpu.SemaphoreType.DMA((row_count, 8)),
            pltpu.SemaphoreType.DMA((row_count, 8)),
            pltpu.SemaphoreType.DMA((1,)),
            pltpu.SemaphoreType.DMA((tile_count,)),
            pltpu.SemaphoreType.DMA((tile_count,)),
        ],
        compiler_params=pltpu.CompilerParams(
            collective_id=1, has_side_effects=True, vmem_limit_bytes=40 * 1024 * 1024
        ),
        name="attend",
    )(cuts, query, pairs, cot)


def attend_back_kernel(
    tile_height, tile_width, cuts, query, attended, grad, lse, conv_in, conv_turned, spread, all_pairs,
    out, conv_grad, conv_out, held, terms, core_terms, side_terms, mask, shift, taps, part, part_got,
    load_sem, send_sem, recv_sem, part_send_sem, part_recv_sem
):
    row_count, tokens, width = query.shape
    tile_count = held.shape[1]
    pair_count = width // 128
    tiles, peers = plane_peers()
    low = jnp.bfloat16
    loads = []
    for row in range(row_count):
        load = pltpu.make_async_copy(all_pairs.at[row], held.at[row], load_sem.at[row])
        load.start()
        loads.append(load)
    greet([plane_peer(k)[0] for k in range(1, tile_count)])
    core = lax.rem(lax.axis_index("ty"), 2)
    chunk = 2

    def send(row, slot, source, target, peer):
        copy = pltpu.make_async_remote_copy(
            src_ref=source,
            dst_ref=target,
            send_sem=send_sem.at[row, slot],
            recv_sem=recv_sem.at[row, slot],
            device_id=peer,
            device_id_type=MESH,
        )
        copy.start()
        return copy

    def compute(row):
        loads[row].wait()
        fill_mask(mask, cuts, row, tile_height, tile_width)

        def one_pair(p, carry):
            at = pl.ds(pl.multiple_of(p * 128, 128), 128)
            at_value = pl.ds(pl.multiple_of(width + p * 128, 128), 128)
            grad_pair = grad[row, :, at]
            both = two_heads(query[row, :, at], 0.125)
            both_grad = two_heads(grad_pair, 1.0)
            inner = jnp.transpose(grad_pair.astype(jnp.float32) * attended[row, :, at].astype(jnp.float32))
            half = inner.shape[0] // 2
            delta = jnp.concatenate(
                [jnp.sum(inner[:half], axis=0, keepdims=True), jnp.sum(inner[half:], axis=0, keepdims=True)], axis=1
            )
            level = lse[row, p]
            query_part = jnp.zeros((128, 2 * tokens), jnp.float32)
            for c in range(tile_count // chunk):
                span = slice(c * chunk * tokens, (c + 1) * chunk * tokens)
                some = slice(c * chunk, (c + 1) * chunk)
                keys = held[row, some, :, at].reshape(chunk * tokens, 128)
                values = held[row, some, :, at_value].reshape(chunk * tokens, 128)
                extra = mask[span, :]
                weights = jnp.exp(mm(keys, both, 1, 1) + jnp.concatenate([extra, extra], axis=1) - level)
                score_grad = (weights * (mm(values, both_grad, 1, 1) - delta)).astype(low)
                value_part = mm(weights.astype(low), both_grad, 1, 0)
                key_part = mm(score_grad, both, 1, 0)
                query_part = query_part + mm(keys, score_grad, 0, 0)
                terms[row, some, :, at] = key_part.astype(low).reshape(chunk, tokens, 128)
                terms[row, some, :, at_value] = value_part.astype(low).reshape(chunk, tokens, 128)
            blocks = own_blocks(query_part) * 0.125
            out[row, :, at] = jnp.transpose(blocks).astype(low)
            return carry

        lax.fori_loop(0, pair_count, one_pair, 0)

    flights = [{} for _ in range(row_count)]
    names = ("own", "x", "y", "xy")
    key_at, value_at = pl.ds(0, width), pl.ds(width, width)

    def begin(row):
        copies = []
        other = 2 - 4 * core
        for k, name in enumerate(names):
            copies.append(send(row, k, terms.at[row, tiles[name] + other], core_terms.at[row, k], peers["core"]))
        flights[row]["core"] = copies

    def add(target, source, row_total):
        def body(i, carry):
            at = pl.ds(pl.multiple_of(i * 16, 16), 16)
            target[at, :] = target[at, :] + source[at, :]
            return carry

        lax.fori_loop(0, row_total // 16, body, 0)

    def scatter(row):
        for k in (3, 1, 2, 0):
            flights[row]["core"][k].wait()
            add(terms.at[row, tiles[names[k]]], core_terms.at[row, k], tokens)
            if k == 3:
                far = terms.at[row, tiles["xy"]]
                flights[row]["far_x"] = send(row, 4, far.at[:, key_at], side_terms.at[row, 0], peers["x"])
                flights[row]["far_y"] = send(row, 5, far.at[:, value_at], side_terms.at[row, 1], peers["y"])
            if k == 1:
                near = terms.at[row, tiles["x"]]
                flights[row]["near_x"] = send(row, 6, near.at[:, key_at], side_terms.at[row, 2], peers["x"])
            if k == 2:
                near = terms.at[row, tiles["y"]]
                flights[row]["near_y"] = send(row, 7, near.at[:, value_at], side_terms.at[row, 3], peers["y"])

    def pass_on(row):
        flights[row]["far_x"].wait()
        near = terms.at[row, tiles["y"], :, key_at]
        add(near, side_terms.at[row, 0], tokens)
        flights[row]["last_y"] = send(row, 8, near, side_terms.at[row, 4], peers["y"])
        flights[row]["far_y"].wait()
        near = terms.at[row, tiles["x"], :, value_at]
        add(near, side_terms.at[row, 1], tokens)
        flights[row]["last_x"] = send(row, 9, near, side_terms.at[row, 5], peers["x"])

    def close(row):
        for name in ("near_x", "near_y", "last_x", "last_y"):
            flights[row][name].wait()
        mine = terms.at[row, tiles["own"]]

        def body(i, carry):
            at = pl.ds(pl.multiple_of(i * 16, 16), 16)
            for start, first, second in ((0, 2, 4), (width, 3, 5)):
                total = mine[at, start : start + width].astype(jnp.float32)
                total = total + side_terms[row, first, at, :].astype(jnp.float32)
                total = total + side_terms[row, second, at, :].astype(jnp.float32)
                out[row, at, width + start : 2 * width + start] = total.astype(low)
            return carry

        lax.fori_loop(0, tokens // 16, body, 0)

    part_copies = []

    def convolve():
        fill_shift(shift, tile_height, tile_width)
        patch = part.shape[2]
        taps[...] = mm(conv_turned[...], conv_in[...], 1, 1)
        rows = []
        for row in range(row_count):
            pieces = []
            for p in range(9):
                piece = taps[p * patch : (p + 1) * patch, row * tokens : (row + 1) * tokens]
                pieces.append(piece * same_image(cuts, row, p, tile_height, tile_width))
            rows.append(jnp.concatenate(pieces, axis=1))
        whole = jnp.concatenate(rows, axis=0)
        coarse = whole.astype(low)
        fine = (whole - coarse.astype(jnp.float32)).astype(low)
        moved = mm(coarse, shift[...], 1, 1) + mm(fine, shift[...], 1, 1)
        for tile in range(tile_count):
            part[tile] = moved[:, tile * tokens : (tile + 1) * tokens].reshape(row_count, patch, tokens)
        for k in range(1, tile_count):
            peer, tile = plane_peer(k)
            copy = pltpu.make_async_remote_copy(
                src_ref=part.at[tile],
                dst_ref=part_got.at[k],
                send_sem=part_send_sem.at[k],
                recv_sem=part_recv_sem.at[k],
                device_id=peer,
                device_id_type=MESH,
            )
            copy.start()
            part_copies.append(copy)
        conv_grad[...] = mm(conv_in[...], spread[...], 0, 1)

    def collect():
        total = part[tiles["own"]]
        for k, copy in enumerate(part_copies):
            copy.wait()
            total = total + part_got[k + 1]
        conv_out[...] = total.astype(low)

    for row in range(row_count):
        compute(row)
        begin(row)
        if row > 0:
            scatter(row - 1)
        if row > 1:
            pass_on(row - 2)
    scatter(row_count - 1)
    convolve()
    for row in range(max(row_count - 2, 0), row_count):
        pass_on(row)
    for row in range(row_count):
        close(row)
    collect()


def attend_back(cuts, query, attended, grad, lse, conv_in, conv_turned, spread, all_pairs, tile_height, tile_width):
    row_count, tokens, width = query.shape
    tile_count = all_pairs.shape[1]
    taps = conv_turned.shape[0]
    low = jnp.bfloat16
    vmem = pl.BlockSpec(memory_space=pltpu.VMEM)
    return pl.pallas_call(
        functools.partial(attend_back_kernel, tile_height, tile_width),
        out_shape=[
            jax.ShapeDtypeStruct((row_count, tokens, 3 * width), low),
            jax.ShapeDtypeStruct((width, taps), jnp.float32),
            jax.ShapeDtypeStruct((row_count, taps // 9, tokens), low),
        ],
        in_specs=[pl.BlockSpec(memory_space=pltpu.SMEM)] + [vmem] * 7 + [pl.BlockSpec(memory_space=pl.ANY)],
        out_specs=[vmem] * 3,
        scratch_shapes=[
            pltpu.VMEM((row_count, tile_count, tokens, 2 * width), low),
            pltpu.VMEM((row_count, tile_count, tokens, 2 * width), low),
            pltpu.VMEM((row_count, 4, tokens, 2 * width), low),
            pltpu.VMEM((row_count, 6, tokens, width), low),
            pltpu.VMEM((tile_count * tokens, tokens), jnp.float32),
            pltpu.VMEM((tile_count * tokens, 9 * tokens), low),
            pltpu.VMEM((taps, row_count * tokens), jnp.float32),
            pltpu.VMEM((tile_count, row_count, taps // 9, tokens), jnp.float32),
            pltpu.VMEM((tile_count, row_count, taps // 9, tokens), jnp.float32),
            pltpu.SemaphoreType.DMA((row_count,)),
            pltpu.SemaphoreType.DMA((row_count, 10)),
            pltpu.SemaphoreType.DMA((row_count, 10)),
            pltpu.SemaphoreType.DMA((tile_count,)),
            pltpu.SemaphoreType.DMA((tile_count,)),
        ],
        compiler_params=pltpu.CompilerParams(
            collective_id=2, has_side_effects=True, vmem_limit_bytes=50 * 1024 * 1024
        ),
        name="attend_back",
    )(cuts, query, attended, grad, lse, conv_in, conv_turned, spread, all_pairs)


def add_rows(target, first, second, rows):
    step = 16

    def body(i, carry):
        at = pl.ds(pl.multiple_of(i * step, step), step)
        target[at, :] = first[at, :] + second[at, :]
        return carry

    lax.fori_loop(0, rows // step, body, 0)


def grad_reduce_kernel(shapes, *refs):
    count = len(shapes)
    grads = refs[:count]
    outs = refs[count : 2 * count]
    rest = refs[2 * count :]
    own, got, half, quarter, final = [rest[i * count : (i + 1) * count] for i in range(5)]
    local_sem, send_sem, recv_sem = rest[5 * count :]
    z, ty, y = lax.axis_index("rows"), lax.axis_index("ty"), lax.axis_index("tx")
    core, x = lax.rem(ty, 2), ty // 2
    peer_core = (z, x * 2 + 1 - core, y)
    peer_x = (z, (1 - x) * 2 + core, y)
    peer_y = (z, ty, 1 - y)
    peer_xy = (z, (1 - x) * 2 + core, 1 - y)
    peers_z = [(lax.rem(z + k, 4), ty, y) for k in (1, 2, 3)]
    barrier = pltpu.get_barrier_semaphore()
    everyone = [peer_core, peer_x, peer_y, peer_xy] + peers_z
    for peer in everyone:
        pl.semaphore_signal(barrier, inc=1, device_id=peer, device_id_type=MESH)
    pl.semaphore_wait(barrier, len(everyone))

    def send(w, slot, source, target, peer):
        return pltpu.make_async_remote_copy(
            src_ref=source,
            dst_ref=target,
            send_sem=send_sem.at[w, slot],
            recv_sem=recv_sem.at[w, slot],
            device_id=peer,
            device_id_type=MESH,
        )

    def columns(w, which):
        width = shapes[w][2] // 2
        return pl.ds(pl.multiple_of(which * width, 128), width)

    def rows(start, size):
        return pl.ds(pl.multiple_of(start, 16), size)

    def place(w, block):
        depth = shapes[w][1]
        later = block // 2
        major = x + later * (y - x)
        minor = y + later * (x - y)
        return rows(major * (depth // 2) + minor * (depth // 4), depth // 4)

    pending = [{} for _ in shapes]

    def begin(w):
        swap = send(w, 0, grads[w].at[:, :, columns(w, 1 - core)], got[w], peer_core)
        swap.start()
        mine = pltpu.make_async_copy(grads[w].at[:, :, columns(w, core)], own[w], local_sem.at[w, 0])
        mine.start()
        pending[w].update(swap=swap, mine=mine)

    def stage_core(w):
        depth = shapes[w][1]
        pending[w]["mine"].wait()
        pending[w]["swap"].wait()
        for block in range(4):
            add_rows(own[w].at[block], own[w].at[block], got[w].at[block], depth)
        first = send(w, 1, own[w].at[0:2, rows((1 - x) * (depth // 2), depth // 2)], half[w].at[0:2], peer_x)
        second = send(w, 2, own[w].at[2:4, rows((1 - y) * (depth // 2), depth // 2)], half[w].at[2:4], peer_y)
        first.start()
        second.start()
        pending[w].update(half=(first, second))

    def stage_half(w):
        depth = shapes[w][1]
        for copy in pending[w]["half"]:
            copy.wait()
        for block in range(4):
            side = x if block < 2 else y
            kept = own[w].at[block, rows(side * (depth // 2), depth // 2)]
            add_rows(kept, kept, half[w].at[block], depth // 2)
        first = send(w, 3, own[w].at[0:2, rows(x * (depth // 2) + (1 - y) * (depth // 4), depth // 4)], quarter[w].at[0:2], peer_y)
        second = send(w, 4, own[w].at[2:4, rows(y * (depth // 2) + (1 - x) * (depth // 4), depth // 4)], quarter[w].at[2:4], peer_x)
        first.start()
        second.start()
        pending[w].update(quarter=(first, second))

    def stage_quarter(w):
        depth = shapes[w][1]
        for copy in pending[w]["quarter"]:
            copy.wait()
        for block in range(4):
            kept = own[w].at[block, place(w, block // 2 * 2)]
            add_rows(kept, kept, quarter[w].at[block], depth // 4)
        copies = []
        for k, peer in enumerate(peers_z):
            block = peer[0]
            copy = send(w, 5 + k, own[w].at[block, place(w, block)], final[w].at[k], peer)
            copy.start()
            copies.append(copy)
        pending[w].update(final=copies)

    def stage_final(w):
        depth = shapes[w][1]
        for copy in pending[w]["final"]:
            copy.wait()
        kept = own[w].at[z, place(w, z)]
        total = final[w].at[0]

        def body(i, carry):
            at = pl.ds(pl.multiple_of(i * 16, 16), 16)
            parts = [ref[at, :].astype(jnp.float32) for ref in (kept, total, final[w].at[1], final[w].at[2])]
            total[at, :] = (parts[0] + parts[1] + (parts[2] + parts[3])).astype(jnp.bfloat16)
            return carry

        lax.fori_loop(0, depth // 64, body, 0)
        target = outs[w].at[place(w, z), columns(w, core)]
        copies = []
        for k, peer in enumerate((peer_x, peer_y, peer_xy)):
            copy = send(w, 8 + k, total, target, peer)
            copy.start()
            copies.append(copy)
        keep = pltpu.make_async_copy(total, target, local_sem.at[w, 1])
        keep.start()
        pending[w].update(gather=copies, keep=keep)

    def stage_gather(w):
        for copy in pending[w]["gather"]:
            copy.wait()
        pending[w]["keep"].wait()
        strip = outs[w].at[:, columns(w, core)]
        copy = send(w, 11, strip, strip, peer_core)
        copy.start()
        pending[w].update(strip=copy)

    def stage_strip(w):
        pending[w]["strip"].wait()

    for w in range(count):
        begin(w)
    stages = [stage_core, stage_half, stage_quarter, stage_final, stage_gather, stage_strip]
    for tick in range(count + len(stages) - 1):
        for depth_index in reversed(range(len(stages))):
            w = tick - depth_index
            if 0 <= w < count:
                stages[depth_index](w)


def grad_reduce(grads):
    shapes = tuple(entry.shape for entry in grads)
    count = len(shapes)
    low = jnp.bfloat16
    scratch = (
        [pltpu.VMEM((s[0], s[1], s[2] // 2), low) for s in shapes]
        + [pltpu.VMEM((s[0], s[1], s[2] // 2), low) for s in shapes]
        + [pltpu.VMEM((s[0], s[1] // 2, s[2] // 2), low) for s in shapes]
        + [pltpu.VMEM((s[0], s[1] // 4, s[2] // 2), low) for s in shapes]
        + [pltpu.VMEM((3, s[1] // 4, s[2] // 2), low) for s in shapes]
        + [
            pltpu.SemaphoreType.DMA((count, 2)),
            pltpu.SemaphoreType.DMA((count, 12)),
            pltpu.SemaphoreType.DMA((count, 12)),
        ]
    )
    return pl.pallas_call(
        functools.partial(grad_reduce_kernel, shapes),
        out_shape=[jax.ShapeDtypeStruct(s[1:], low) for s in shapes],
        in_specs=[pl.BlockSpec(memory_space=pl.ANY)] * count,
        out_specs=[pl.BlockSpec(memory_space=pl.ANY)] * count,
        scratch_shapes=scratch,
        compiler_params=pltpu.CompilerParams(collective_id=3, has_side_effects=True, vmem_limit_bytes=56 * 1024 * 1024),
        name="grad_reduce",
    )(*grads)


def sum_by_table(local_grads):
    band_count, column_count = lax.axis_size("ty"), lax.axis_size("tx")
    group_count = lax.axis_size("rows")
    tile_count = band_count * column_count
    table = jnp.concatenate([entry.reshape(group_count, -1) for entry in local_grads], axis=1)
    column_total = table.shape[1]
    padded_columns = -(-column_total // tile_count) * tile_count
    piece_width = padded_columns // tile_count
    table = table.reshape(group_count, tile_count, piece_width)
    shares = lax.psum_scatter(
        table.reshape(group_count * tile_count, piece_width),
        ("rows", "ty", "tx"),
        scatter_dimension=0,
        tiled=True,
    )
    summed = (
        lax.all_gather(shares.astype(jnp.bfloat16), ("ty", "tx"), axis=0, tiled=True)
        .astype(shares.dtype)
        .reshape(-1)
    )
    totals = []
    start_at = 0
    for entry in local_grads:
        length = entry.size // group_count
        shard_shape = (entry.shape[0] // group_count,) + entry.shape[1:]
        totals.append(summed[start_at : start_at + length].reshape(shard_shape))
        start_at = start_at + length
    return tuple(totals)


def shards(
    latent,
    skip_input,
    segment_ids,
    embed_weight,
    embed_bias,
    skip_weight,
    skip_bias,
    norm1_gain,
    norm1_bias,
    qkv_weight,
    proj_weight,
    proj_bias,
    norm2_gain,
    norm2_bias,
    fc1_weight,
    fc1_bias,
    fc2_weight,
    fc2_bias,
    conv_weight,
    cotangent,
):
    row_count, tile_height, tile_width, width = skip_input.shape
    patch = latent.shape[3]
    tokens = tile_height * tile_width
    token_count = row_count * tokens
    low = jnp.bfloat16
    wide = jnp.float32
    cuts = jnp.stack(
        [jnp.sum(segment_ids[:, 0, :] == 0, axis=1), jnp.sum(segment_ids[:, :, -1] == 1, axis=1)],
        axis=1,
    ).astype(jnp.int32)
    vectors = jnp.stack(
        [embed_bias, skip_bias, norm1_gain, norm1_bias, proj_bias, norm2_gain, norm2_bias, fc2_bias]
    ).astype(wide)
    hidden_bias = fc1_bias.astype(wide).reshape(-1, 1, 512)
    conv_turned = conv_weight.T
    cot = cotangent.reshape(row_count, tokens, patch).transpose(0, 2, 1)
    flat_latent = latent.reshape(token_count, patch)
    flat_skip = skip_input.reshape(token_count, width)
    embedded, stream, normed, query, pairs = front(
        flat_latent, flat_skip, embed_weight, skip_weight, qkv_weight, vectors, row_count
    )
    attended, log_total, row_pairs, cot_tiles = attend(cuts, query, pairs, cot, tile_height, tile_width)
    (
        fc1_grad, fc2_grad, hidden_bias_grad, proj_grad, attended_grad, mid_grad, conv_in, spread, middle_grads
    ) = middle(
        cuts, attended.reshape(token_count, width), stream, cot_tiles, proj_weight, conv_turned, vectors,
        hidden_bias, fc1_weight, fc2_weight, tile_height, tile_width,
    )
    projected_grad, conv_grad, conv_out = attend_back(
        cuts, query, attended, attended_grad.reshape(row_count, tokens, width), log_total,
        conv_in, conv_turned, spread, row_pairs, tile_height, tile_width,
    )
    qkv_grad, skip_grad, skip_input_grad, thin, flat = rear(
        projected_grad.reshape(token_count, 3 * width), qkv_weight, normed, stream, mid_grad, embedded, flat_skip,
        flat_latent, skip_weight, vectors, middle_grads, hidden_bias_grad.reshape(4, -1), conv_grad,
    )
    output = conv_out.transpose(0, 2, 1).reshape(row_count, tile_height, tile_width, patch)
    skip_input_grad = skip_input_grad.reshape(row_count, tile_height, tile_width, width)
    taps = 9 * patch
    share = width // 4
    mesh_shape = (lax.axis_size("rows"), lax.axis_size("ty"), lax.axis_size("tx"))
    if mesh_shape == (4, 4, 2):
        local = [proj_grad, fc1_grad, fc2_grad, qkv_grad, skip_grad, thin]
        summed = grad_reduce([entry.reshape(4, -1, entry.shape[1]) for entry in local] + [flat])
        proj_total, fc1_total, fc2_total, qkv_total, skip_total = [entry.astype(wide) for entry in summed[:5]]
        conv_total = summed[5][:, :taps].astype(wide)
        embed_total = summed[5][:, taps : taps + patch].astype(wide)
        line = [summed[6][k, :share].astype(wide) for k in range(8)]
        fc1_line = summed[6][8:11].reshape(-1).astype(wide)
        return (
            output, skip_input_grad, embed_total, line[0], skip_total, line[1], line[2], line[3], qkv_total,
            proj_total, line[4], line[5], line[6], fc1_total, fc1_line, fc2_total, line[7], conv_total,
        )
    line = [flat[:, k, :share].reshape(-1) for k in range(8)]
    fc1_line = flat[:, 8:11].reshape(-1)
    local_grads = [
        thin[:, taps : taps + patch], line[0], skip_grad, line[1], line[2], line[3], qkv_grad, proj_grad, line[4],
        line[5], line[6], fc1_grad, fc1_line, fc2_grad, line[7], thin[:, :taps],
    ]
    return (output, skip_input_grad) + sum_by_table([entry.astype(wide) for entry in local_grads])


def solution(mesh):
    return jax.shard_map(
        shards,
        mesh=mesh,
        in_specs=(
            P("rows", "ty", "tx", None),
            P("rows", "ty", "tx", None),
            P("rows", None, None),
            P(),
            P(),
            P(),
            P(),
            P(),
            P(),
            P(),
            P(),
            P(),
            P(),
            P(),
            P(),
            P(),
            P(),
            P(),
            P(),
            P("rows", "ty", "tx", None),
        ),
        out_specs=(
            P("rows", "ty", "tx", None),
            P("rows", "ty", "tx", None),
            P("rows", None),
            P("rows"),
            P("rows", None),
            P("rows"),
            P("rows"),
            P("rows"),
            P("rows", None),
            P("rows", None),
            P("rows"),
            P("rows"),
            P("rows"),
            P("rows", None),
            P("rows"),
            P("rows", None),
            P("rows"),
            P("rows", None),
        ),
        check_vma=False,
    )
```

time: 503 us -> 334 us (0.66); the launches traced: 496 us -> 332 us
  Pallas kernels: 116 us -> 275 us
  matrix products: 141 us -> 0 us
  other arithmetic: 78.1 us -> 15.1 us
  local copies, waits for them, and re-layouts: 104 us -> 41.2 us
  starting transfers between devices: 22.5 us -> 0 us
  waiting for transfers between devices: 19.9 us -> 0 us
  between operations: 15.3 us -> 0.8 us
    pallas_call x0 -> x5, Pallas kernels: none -> 160 us  [the longest x1 61.5 us: attend_back(): pl.pallas_call(functools.partial(attend_back_kernel, tile_height, tile_wi...]
    dot_general x26 -> x0, matrix products: 141 us -> none  [product(): jnp.einsum(pattern, former, latter, preferred_element_type=jnp.float32)]
    reshape x10 -> x2, local copies, waits for them, and re-layouts: 33.4 us -> 1.68 us  [the longest x1 0.95 us: shards(): cot = cotangent.reshape(row_count, tokens, patch).transpose(0, 2, 1)]
    convert_element_type x20 -> x10, other arithmetic: 39 us -> 11.8 us  [the longest x5 7.66 us: shards(): entry.astype(wide)]
    slice x8 -> x0, local copies, waits for them, and re-layouts: 27.1 us -> none  [the longest x2 14.7 us: shards(): row_pairs[:, :, :model_width]]
    ppermute x8 -> x0, starting transfers between devices: 22.4 us -> none  [the longest x4 17.3 us: with_halo(): before = lax.ppermute(last, axis, up)]
    unnamed x138 -> x70, local copies, waits for them, and re-layouts: 12.1 us -> 33.2 us
    all_gather x1 -> x0, waiting for transfers between devices: 13.8 us -> none  [shards(): row_pairs = lax.all_gather(local_pairs, ('ty', 'tx'), axis=1, tiled=True)]
  transfers between devices with their start and end apart: 10 -> 0, of which waited for: 2 -> 0; matrix products, arithmetic and copies ran while one was open for 19% -> 0% of each run, Pallas kernels for 0% -> 0%
where the time goes in v3:
time: 334 us; the launch traced here: 332 us
  Pallas kernels  275 us (82%)
  local copies, waits for them, and re-layouts  41.2 us (12%)
  other arithmetic  15.1 us (5%)
    pallas_call x1, Pallas kernels, grad_reduce(): pl.pallas_call(functools.partial(grad_reduce_kernel, shapes), out_shape=[...  115 us
    pallas_call x1, Pallas kernels, attend_back(): pl.pallas_call(functools.partial(attend_back_kernel, tile_height, tile_wi...  61.5 us
    pallas_call x1, Pallas kernels, attend(): pl.pallas_call(functools.partial(attend_kernel, tile_height, tile_width),...  54.9 us
    unnamed x70, local copies, waits for them, and re-layouts  33.2 us
    pallas_call x1, Pallas kernels, middle(): pl.pallas_call(functools.partial(middle_kernel, tile_height, tile_width),...  28.2 us
    pallas_call x1, Pallas kernels, rear(): pl.pallas_call(rear_kernel, out_shape=[jax.ShapeDtypeStruct((width, 3 * w...  11.9 us
    convert_element_type x5, other arithmetic, shards(): entry.astype(wide)  7.66 us

profile of v3, /device:TPU:0, one launch (start us, length us, event | category | flops | bytes accessed | tf_op | source)
XLA Modules:
  0.0 332.5 jit_solution(11763782603600458477)
XLA Ops:
  0.7 1.0 convert_reduce_fusion
  1.7 0.9 fusion
  2.5 0.1 copy.38
  2.6 0.1 copy.39
  2.7 0.1 pad_add_fusion.cuts
  2.8 0.7 stack.39
  3.5 0.7 stack.40
  4.2 0.7 stack.41
  4.9 0.7 stack.42
  5.6 0.7 stack.43
  6.3 0.7 stack.44
  6.9 0.7 stack.45
  7.6 0.7 stack.46
  8.4 0.0 copy-start.23
  8.4 0.7 reshape.128
  9.1 1.0 copy.45
  10.0 0.9 copy.40.embed_weight
  11.0 0.0 copy-start
  11.0 2.0 copy-done
  13.0 1.7 copy-done.2
  14.6 1.1 copy-done.5
  15.7 0.9 copy-done.21
  16.6 3.7 %front.1 = (bf16[384,768]{1,0:T(8,128)(2,1)S(1)}, f32[384,768]{1,0:T(8,128)S(1)}, bf16[384,768]{1,0:T(8,128)(2,1)S(1)}, bf16[3,128,768]{2,1,0:T(8,128)(2,1)S(1)}, bf16[3,128,1536]{2,1,0:T(8,128)(2,1)S(1)}) custom-call(bf16[384,16]{1,0:T(8,128)(2,1)S(1)} %bitcast.39, bf16[384,768]{1,0:T(8,128)(2,1)S(1)} %bitcast.29, bf16[768,16]{1,0:T(8,128)(2,1)S(1)} %copy.40.embed_weight, ...), custom_call_target="tpu_custom_call" | custom-call | tf_op jit(solution)/shard_map/front/pallas_call | solution.py:99
  20.3 0.8 copy-done.16
  21.1 0.8 copy-done.18
  21.9 54.9 %attend.1 = (bf16[3,128,768]{2,1,0:T(8,128)(2,1)S(1)}, f32[3,6,1,256]{3,2,1,0:T(1,128)S(1)}, bf16[3,8,128,1536]{3,2,1,0:T(8,128)(2,1)S(1)}, bf16[8,3,16,128]{3,2,1,0:T(8,128)(2,1)S(1)}) custom-call(s32[3,2]{1,0:T(4,128)S(1)} %pad_add_fusion.cuts, bf16[3,128,768]{2,1,0:T(8,128)(2,1)S(1)} %get-tuple-element.51.query, ...), custom_call_target="tpu_custom_call" | custom-call | tf_op jit(solution)/shard_map/attend/pallas_call | solution.py:526
  76.8 3.6 %copy-done.1 = bf16[3,8,128,1536]{3,2,1,0:T(8,128)(2,1)} copy-done((bf16[3,8,128,1536]{3,2,1,0:T(8,128)(2,1)}, bf16[3,8,128,1536]{3,2,1,0:T(8,128)(2,1)S(1)}, u32[]{:S(2)}) %copy-start.1) | copy-done | bytes 9437208
  80.4 28.2 %middle.1 = (bf16[768,3072]{1,0:T(8,128)(2,1)S(1)}, bf16[3072,768]{1,0:T(8,128)(2,1)}, f32[6,1,512]{2,1,0:T(1,128)S(1)}, bf16[768,768]{1,0:T(8,128)(2,1)S(1)}, b...) custom-call(s32[3,2]{1,0:T(4,128)S(1)} %pad_add_fusion.cuts, ...), custom_call_target="tpu_custom_call" | custom-call | tf_op jit(solution)/shard_map/middle/pallas_call | solution.py:218
  108.7 2.1 copy-done.4
  110.8 1.0 copy-done.9
  111.8 1.0 copy-done.10
  112.8 0.6 copy-done.26
  113.4 61.5 %attend_back.1 = (bf16[3,128,2304]{2,1,0:T(8,128)(2,1)}, f32[768,144]{1,0:T(8,128)S(1)}, bf16[3,16,128]{2,1,0:T(8,128)(2,1)S(1)}) custom-call(s32[3,2]{1,0:T(4,128)S(1)} %pad_add_fusion.cuts, bf16[3,128,768]{2,1,0:T(8,128)(2,1)S(1)} %get-tuple-element.51.query, bf16[3,128,768]{2,1,0:T(8,128)(2,1)S(1)} %get-tuple-element.53.attended, ...), custom_call_target="tpu_custom_call" | custom-call | tf_op jit(solution)/shard_map/attend_back/pallas_call | solution.py:743
  175.0 0.9 copy-done.14
  175.9 0.6 copy-done.28
  176.5 0.6 reduce.2
  177.1 0.7 reshape.120.hidden_bias_grad
  177.8 1.5 copy.46
  179.3 1.1 copy-done.6
  180.3 1.5 copy-done.8
  181.8 1.3 copy-done.11
  183.1 1.1 copy-done.15
  184.2 1.1 copy-done.17
  185.3 1.1 copy-done.19
  186.4 0.9 copy-done.22
  187.2 0.7 copy-done.24
  188.0 0.7 copy-done.27
  188.7 11.9 %rear.1 = (bf16[768,2304]{1,0:T(8,128)(2,1)}, bf16[1536,768]{1,0:T(8,128)(2,1)S(1)}, bf16[384,768]{1,0:T(8,128)(2,1)}, bf16[768,256]{1,0:T(8,128)(2,1)S(1)}, bf16[4,64,256]{2,1,0:T(8,128)(2,1)S(1)}) custom-call(bf16[384,2304]{1,0:T(8,128)(2,1)S(1)} %bitcast.33, bf16[768,2304]{1,0:T(8,128)(2,1)} %qkv_weight.3, bf16[384,768]{1,0:T(8,128)(2,1)S(1)} %copy-done.19, ...), custom_call_target="tpu_custom_call" | custom-call | tf_op jit(solution)/shard_map/rear/pallas_call | solution.py:306
  200.6 1.4 copy-done.7
  202.0 0.7 copy-done.20
  202.8 0.7 copy-done.25
  203.4 115.2 %grad_reduce.1 = (bf16[192,768]{1,0:T(8,128)(2,1)}, bf16[192,3072]{1,0:T(8,128)(2,1)}, bf16[768,768]{1,0:T(8,128)(2,1)}, bf16[192,2304]{1,0:T(8,128)(2,1)}, bf16...) custom-call(bf16[4,192,768]{2,1,0:T(8,128)(2,1)} %bitcast.34, ...), custom_call_target="tpu_custom_call" | custom-call | tf_op jit(solution)/shard_map/grad_reduce/pallas_call | solution.py:942
  318.6 0.8 slice_convert_fusion.2
  319.4 1.6 slice_convert_fusion.3
  320.9 0.6 reshape.137
  321.5 0.9 slice_convert_fusion.1
  322.4 0.7 copy.43
  323.1 0.9 slice_convert_fusion
  324.0 0.8 copy.44
  324.8 2.2 convert_element_type.93
  327.0 0.9 convert_element_type.101
  327.9 1.3 convert_element_type.100
  329.2 1.7 convert_element_type.108
  330.9 1.6 convert_element_type.111
  (41 shorter events, 0.1 us)
Async XLA Ops:
  8.4 72.1 %copy-start.23 = (f32[8,768]{1,0:T(8,128)}, f32[8,768]{1,0:T(8,128)S(1)}, u32[]{:S(2)}) copy-start(f32[8,768]{1,0:T(8,128)S(1)} %convert_element_type.89.vectors) | copy-start | bytes 73732
  11.0 2.0 copy-start
  13.0 1.7 copy-start.2
  14.6 1.1 copy-start.5
  15.7 0.9 copy-start.21
  16.6 63.8 %copy-start.13 = (bf16[768,144]{0,1:T(8,128)(2,1)S(1)}, bf16[768,144]{0,1:T(8,128)(2,1)}, u32[]{:S(2)}) copy-start(bf16[768,144]{0,1:T(8,128)(2,1)} %param.38) | copy-start | bytes 663556
  20.3 0.8 copy-start.16
  21.1 0.8 copy-start.18
  21.9 58.5 %copy-start.12 = (bf16[768,768]{1,0:T(8,128)(2,1)S(1)}, bf16[768,768]{1,0:T(8,128)(2,1)}, u32[]{:S(2)}) copy-start(bf16[768,768]{1,0:T(8,128)(2,1)} %proj_weight.1) | copy-start | bytes 3538948
  76.8 3.7 %copy-start.1 = (bf16[3,8,128,1536]{3,2,1,0:T(8,128)(2,1)}, bf16[3,8,128,1536]{3,2,1,0:T(8,128)(2,1)S(1)}, u32[]{:S(2)}) copy-start(bf16[3,8,128,1536]{3,2,1,0:T(8,128)(2,1)S(1)} %get-tuple-element.60.all_pairs) | copy-start | bytes 28311556
  108.7 2.1 copy-start.4
  110.8 1.0 copy-start.9
  111.8 1.0 copy-start.10
  112.8 0.6 copy-start.26
  113.4 65.8 %copy-start.3 = (bf16[1536,768]{1,0:T(8,128)(2,1)S(1)}, bf16[1536,768]{1,0:T(8,128)(2,1)}, u32[]{:S(2)}) copy-start(bf16[1536,768]{1,0:T(8,128)(2,1)} %skip_weight.3) | copy-start | bytes 7077892
  175.0 0.9 copy-start.14
  175.9 0.6 copy-start.28
  179.3 1.1 copy-start.6
  180.3 1.5 copy-start.8
  181.8 1.3 copy-start.11
  183.1 1.1 copy-start.15
  184.2 1.1 copy-start.17
  185.3 1.1 copy-start.19
  186.4 0.9 copy-start.22
  187.2 0.7 copy-start.24
  188.0 0.7 copy-start.27
  200.6 1.4 copy-start.7
  202.0 0.7 copy-start.20
  202.8 0.7 copy-start.25
  318.6 8.4 %copy-start.32 = (bf16[192,768]{1,0:T(8,128)(2,1)S(1)}, bf16[192,768]{1,0:T(8,128)(2,1)}, u32[]{:S(2)}) copy-start(bf16[192,768]{1,0:T(8,128)(2,1)} %get-tuple-element.81) | copy-start | bytes 884740
  318.6 9.3 %copy-start.31 = (bf16[192,2304]{1,0:T(8,128)(2,1)S(1)}, bf16[192,2304]{1,0:T(8,128)(2,1)}, u32[]{:S(2)}) copy-start(bf16[192,2304]{1,0:T(8,128)(2,1)} %get-tuple-element.80) | copy-start | bytes 2654212
  324.8 4.4 %copy-start.30 = (bf16[192,3072]{1,0:T(8,128)(2,1)S(1)}, bf16[192,3072]{1,0:T(8,128)(2,1)}, u32[]{:S(2)}) copy-start(bf16[192,3072]{1,0:T(8,128)(2,1)} %get-tuple-element.82) | copy-start | bytes 3538948
  329.2 1.7 copy-start.29

commit v4 on v3

--- a/solution.py
+++ b/solution.py
@@ -257,15 +257,60 @@
 
 
 def rear_kernel(
-    projected_grad, qkv_weight, normed, stream, mid_grad, embedded, skip, latent, skip_weight, vectors,
-    middle_grads, hidden_bias_grad, conv_grad, qkv_grad, skip_grad, skip_input_grad, thin, flat, stream_low,
+    starts, reduces, projected_in, qkv_in, normed_in, stream_in, mid_in, embedded_in, skip_in, skip_weight_in,
+    latent, vectors, middle_grads, hidden_bias_grad, conv_grad, *refs
 ):
+    count = len(starts)
+    resumed, refs = refs[:count], refs[count:]
+    skip_input_grad, refs = refs[0], refs[1:]
+    if reduces:
+        sums, refs = refs[: count + 4], refs[count + 4 :]
+        peers = chip_peers()
+    qkv_grad, skip_grad, thin, flat, refs = *refs[:4], refs[4:]
+    projected_grad, qkv_weight, normed, stream, mid_grad, embedded, skip, skip_weight, stream_low, load_sem = refs[:10]
+    sources = (projected_in, normed_in, qkv_in, stream_in, mid_in, embedded_in, skip_in, skip_weight_in)
+    targets = (projected_grad, normed, qkv_weight, stream, mid_grad, embedded, skip, skip_weight)
+    loads = [pltpu.make_async_copy(a, b, load_sem.at[k]) for k, (a, b) in enumerate(zip(sources, targets))]
+    for load in loads[:3]:
+        load.start()
+    later, news = [], []
+    if reduces:
+        items = make_reducers(
+            starts + ("plane",) * 4, resumed + (qkv_grad, skip_grad, thin, flat), sums, refs[10:]
+        )
+        later, news = items[:count], items[count:]
+        greet([peers[name] for name in ("core", "x", "y", "xy")] + peers["z"])
+    for item in later:
+        item.begin()
+    for load in loads[3:]:
+        load.start()
+    for item in later:
+        item.stages.pop(0)()
     token_count, width = stream.shape
     low = jnp.bfloat16
     tokens = 128
     parts = [slice(k * tokens, (k + 1) * tokens) for k in range(token_count // tokens)]
     zero = jnp.zeros((1, width), jnp.float32)
     gain_sum, bias_sum, stream_sum, embed_sum = zero, zero, zero, zero
+    loads[0].wait()
+    loads[1].wait()
+    blocks, depth = qkv_grad.shape[0], qkv_grad.shape[1]
+    for k in range(3):
+        at = slice(k * width, (k + 1) * width)
+        qkv_grad[:, :, at] = mm(normed[...], projected_grad[:, at], 0, 0).astype(low).reshape(blocks, depth, width)
+
+    def open_up(which):
+        for item in news[which]:
+            item.begin()
+
+    def step_on(group):
+        for item in group:
+            if item.stages:
+                item.stages.pop(0)()
+
+    open_up(slice(0, 1))
+    for load in loads[2:5]:
+        load.wait()
     for at in parts:
         incoming = mm(projected_grad[at, :], qkv_weight[...], 1, 1)
         unit, rate = normalised(stream[at, :])
@@ -274,19 +319,24 @@
         grad = mid_grad[at, :] + norm_back(incoming, unit, rate, vectors[2:3])
         stream_sum = stream_sum + down_sum(grad)
         stream_low[at, :] = grad.astype(low)
+    step_on(news[0:1])
+    loads[5].wait()
+    loads[6].wait()
+    skip_grad[0:2] = mm(embedded[...], stream_low[...], 0, 0).astype(low).reshape(2, width // 2, width)
+    skip_grad[2:4] = mm(skip[...], stream_low[...], 0, 0).astype(low).reshape(2, width // 2, width)
+    open_up(slice(1, 2))
+    loads[7].wait()
     embed_lows = []
     for at in parts:
         embed_grad = mm(stream_low[at, :], skip_weight[:width], 1, 1)
         embed_sum = embed_sum + down_sum(embed_grad)
         embed_lows.append(embed_grad.astype(low))
-        skip_input_grad[at, :] = mm(stream_low[at, :], skip_weight[width:], 1, 1).astype(low)
-    qkv_grad[...] = mm(normed[...], projected_grad[...], 0, 0).astype(low)
-    skip_grad[:width] = mm(embedded[...], stream_low[...], 0, 0).astype(low)
-    skip_grad[width:] = mm(skip[...], stream_low[...], 0, 0).astype(low)
     embed_weight_grad = mm(jnp.concatenate(embed_lows, axis=0), latent[...], 0, 0)
-    thin[:, :128] = conv_grad[:, :128].astype(low)
+    step_on(news[1:2])
     rest = jnp.zeros((width, 128 - 2 * 16), jnp.float32)
-    thin[:, 128:] = jnp.concatenate([conv_grad[:, 128:144], embed_weight_grad, rest], axis=1).astype(low)
+    thin[:, :, :128] = conv_grad[:, :128].astype(low).reshape(4, width // 4, 128)
+    edge = jnp.concatenate([conv_grad[:, 128:144], embed_weight_grad, rest], axis=1)
+    thin[:, :, 128:] = edge.astype(low).reshape(4, width // 4, 128)
     rows = [embed_sum, stream_sum, gain_sum, bias_sum] + [middle_grads[k : k + 1] for k in range(4, 8)]
     stack = jnp.concatenate(rows, axis=0)
     share = width // 4
@@ -298,24 +348,50 @@
         body = jnp.concatenate([own] + pieces + [jnp.zeros((8 - len(pieces), 256), jnp.float32)], axis=0)
         flat[block, 0:16] = body.astype(low)
         flat[block, 16:64] = jnp.zeros((48, 256), low)
-
-
-def rear(projected_grad, qkv_weight, normed, stream, mid_grad, embedded, skip, latent, skip_weight, vectors, middle_grads, hidden_bias_grad, conv_grad):
+    open_up(slice(2, 4))
+    step_on(later)
+    step_on(news[0:1])
+    for at in parts:
+        skip_input_grad[at, :] = mm(stream_low[at, :], skip_weight[width:], 1, 1).astype(low)
+    step_on(news[2:4])
+    while any(item.stages for item in later + news):
+        step_on(later)
+        step_on(news)
+
+
+def rear(projected_grad, qkv_weight, normed, stream, mid_grad, embedded, skip, skip_weight, latent, vectors, middle_grads, hidden_bias_grad, conv_grad, resumed, reduces):
     token_count, width = stream.shape
     low = jnp.bfloat16
+    starts = tuple(start for start, _, _ in resumed)
+    sizes = [(width // 4, 3 * width), (width // 2, width), (width // 4, 256), (64, 256)]
+    totals = [shape for _, _, shape in resumed] + sizes
+    vmem, anywhere = pl.BlockSpec(memory_space=pltpu.VMEM), pl.BlockSpec(memory_space=pl.ANY)
+    big = [projected_grad, qkv_weight, normed, stream, mid_grad, embedded, skip, skip_weight]
+    out_shape = [jax.ShapeDtypeStruct((token_count, width), low)]
+    out_specs = [vmem]
+    scratch = []
+    if reduces:
+        out_shape += [jax.ShapeDtypeStruct(shape, low) for shape in totals]
+        out_specs += [anywhere] * len(totals)
+        scratch += [pltpu.VMEM((4,) + shape, low) for shape in sizes]
+        params = pltpu.CompilerParams(collective_id=3, has_side_effects=True, vmem_limit_bytes=56 * 1024 * 1024)
+    else:
+        out_shape += [jax.ShapeDtypeStruct((4,) + shape, low) for shape in sizes]
+        out_specs += [vmem] * len(sizes)
+        params = pltpu.CompilerParams(vmem_limit_bytes=48 * 1024 * 1024)
+    scratch += [pltpu.VMEM(entry.shape, entry.dtype) for entry in big]
+    scratch += [pltpu.VMEM((token_count, width), low), pltpu.SemaphoreType.DMA((len(big),))]
+    if reduces:
+        scratch += reducer_scratch(starts + ("plane",) * 4, totals)
     return pl.pallas_call(
-        rear_kernel,
-        out_shape=[
-            jax.ShapeDtypeStruct((width, 3 * width), low),
-            jax.ShapeDtypeStruct((2 * width, width), low),
-            jax.ShapeDtypeStruct((token_count, width), low),
-            jax.ShapeDtypeStruct((width, 256), low),
-            jax.ShapeDtypeStruct((4, 64, 256), low),
-        ],
-        scratch_shapes=[pltpu.VMEM((token_count, width), low)],
-        compiler_params=pltpu.CompilerParams(vmem_limit_bytes=40 * 1024 * 1024),
+        functools.partial(rear_kernel, starts, reduces),
+        out_shape=out_shape,
+        in_specs=[anywhere] * len(big) + [vmem] * 5 + [anywhere] * len(starts),
+        out_specs=out_specs,
+        scratch_shapes=scratch,
+        compiler_params=params,
         name="rear",
-    )(projected_grad, qkv_weight, normed, stream, mid_grad, embedded, skip, latent, skip_weight, vectors, middle_grads, hidden_bias_grad, conv_grad)
+    )(*big, latent, vectors, middle_grads, hidden_bias_grad, conv_grad, *[entry for _, entry, _ in resumed])
 
 
 def plane_peers():
@@ -496,7 +572,7 @@
             lse[row, p] = peak + jnp.log(total)
             return carry
 
-        lax.fori_loop(0, pair_count, one_pair, 0)
+        lax.fori_loop(0, pair_count, one_pair, 0, unroll=3)
 
     begin(0)
     if row_count > 1:
@@ -552,10 +628,19 @@
 
 
 def attend_back_kernel(
-    tile_height, tile_width, cuts, query, attended, grad, lse, conv_in, conv_turned, spread, all_pairs,
-    out, conv_grad, conv_out, held, terms, core_terms, side_terms, mask, shift, taps, part, part_got,
-    load_sem, send_sem, recv_sem, part_send_sem, part_recv_sem
+    tile_height, tile_width, starts, cuts, query_in, attended_in, grad_in, lse_in, conv_in, conv_turned, spread, all_pairs, *refs
 ):
+    count = len(starts)
+    grads, refs = refs[:count], refs[count:]
+    (out, conv_grad, conv_out), saved, refs = refs[:3], refs[3 : 3 + count], refs[3 + count :]
+    query, attended, grad, lse, row_sem = refs[:5]
+    refs = refs[5:]
+    held, terms, core_terms, side_terms, mask, shift, taps, part, part_got = refs[:9]
+    load_sem, send_sem, recv_sem, part_send_sem, part_recv_sem = refs[9:14]
+    items = make_reducers(starts, grads, saved, refs[14:]) if count else []
+    firsts = [item for item in items if item.start == "z"]
+    planes = [item for item in items if item.start == "plane"]
+
     row_count, tokens, width = query.shape
     tile_count = held.shape[1]
     pair_count = width // 128
@@ -565,8 +650,12 @@
     for row in range(row_count):
         load = pltpu.make_async_copy(all_pairs.at[row], held.at[row], load_sem.at[row])
         load.start()
-        loads.append(load)
-    greet([plane_peer(k)[0] for k in range(1, tile_count)])
+        loads.append([load])
+        for k, (source, target) in enumerate(((query_in, query), (attended_in, attended), (grad_in, grad), (lse_in, lse))):
+            load = pltpu.make_async_copy(source.at[row], target.at[row], row_sem.at[row, k])
+            load.start()
+            loads[-1].append(load)
+    greet([plane_peer(k)[0] for k in range(1, tile_count)] + (chip_peers()["z"] if count else []))
     core = lax.rem(lax.axis_index("ty"), 2)
     chunk = 2
 
@@ -583,7 +672,8 @@
         return copy
 
     def compute(row):
-        loads[row].wait()
+        for load in loads[row]:
+            load.wait()
         fill_mask(mask, cuts, row, tile_height, tile_width)
 
         def one_pair(p, carry):
@@ -616,7 +706,7 @@
             out[row, :, at] = jnp.transpose(blocks).astype(low)
             return carry
 
-        lax.fori_loop(0, pair_count, one_pair, 0)
+        lax.fori_loop(0, pair_count, one_pair, 0, unroll=3)
 
     flights = [{} for _ in range(row_count)]
     names = ("own", "x", "y", "xy")
@@ -718,38 +808,72 @@
             total = total + part_got[k + 1]
         conv_out[...] = total.astype(low)
 
+    def advance(group, stage):
+        for item in group:
+            item.stages[stage]()
+
+    for item in items:
+        item.begin()
+    advance(items[:2], 0)
     for row in range(row_count):
         compute(row)
         begin(row)
+        if row == 0:
+            advance(items[2:], 0)
+        if row > 1:
+            pass_on(row - 2)
         if row > 0:
             scatter(row - 1)
-        if row > 1:
-            pass_on(row - 2)
+            if row < 3:
+                advance(planes, row)
     scatter(row_count - 1)
+    if row_count > 1:
+        pass_on(row_count - 2)
     convolve()
-    for row in range(max(row_count - 2, 0), row_count):
-        pass_on(row)
+    pass_on(row_count - 1)
+    for stage in range(min(row_count, 3), 3):
+        advance(planes, stage)
     for row in range(row_count):
         close(row)
     collect()
-
-
-def attend_back(cuts, query, attended, grad, lse, conv_in, conv_turned, spread, all_pairs, tile_height, tile_width):
+    advance(planes, 3)
+    advance(firsts, 1)
+    for item in items:
+        item.save()
+    for item in items:
+        item.land("save")
+
+
+def attend_back(cuts, query, attended, grad, lse, conv_in, conv_turned, spread, all_pairs, grads, tile_height, tile_width):
     row_count, tokens, width = query.shape
+    starts = tuple(start for start, _ in grads)
+    grads = [entry for _, entry in grads]
+    count = len(starts)
+    shapes = [entry.shape[1:] for entry in grads]
+    saves = [(r if start == "z" else r // 4, c // 2) for start, (r, c) in zip(starts, shapes)]
     tile_count = all_pairs.shape[1]
     taps = conv_turned.shape[0]
     low = jnp.bfloat16
     vmem = pl.BlockSpec(memory_space=pltpu.VMEM)
     return pl.pallas_call(
-        functools.partial(attend_back_kernel, tile_height, tile_width),
+        functools.partial(attend_back_kernel, tile_height, tile_width, starts),
         out_shape=[
             jax.ShapeDtypeStruct((row_count, tokens, 3 * width), low),
             jax.ShapeDtypeStruct((width, taps), jnp.float32),
             jax.ShapeDtypeStruct((row_count, taps // 9, tokens), low),
-        ],
-        in_specs=[pl.BlockSpec(memory_space=pltpu.SMEM)] + [vmem] * 7 + [pl.BlockSpec(memory_space=pl.ANY)],
-        out_specs=[vmem] * 3,
+        ]
+        + [jax.ShapeDtypeStruct(s, low) for s in saves],
+        in_specs=[pl.BlockSpec(memory_space=pltpu.SMEM)]
+        + [pl.BlockSpec(memory_space=pl.ANY)] * 4
+        + [vmem] * 3
+        + [pl.BlockSpec(memory_space=pl.ANY)] * (1 + count),
+        out_specs=[vmem] * 3 + [pl.BlockSpec(memory_space=pl.ANY)] * count,
         scratch_shapes=[
+            pltpu.VMEM(query.shape, low),
+            pltpu.VMEM(attended.shape, low),
+            pltpu.VMEM(grad.shape, low),
+            pltpu.VMEM(lse.shape, jnp.float32),
+            pltpu.SemaphoreType.DMA((row_count, 4)),
             pltpu.VMEM((row_count, tile_count, tokens, 2 * width), low),
             pltpu.VMEM((row_count, tile_count, tokens, 2 * width), low),
             pltpu.VMEM((row_count, 4, tokens, 2 * width), low),
@@ -764,190 +888,249 @@
             pltpu.SemaphoreType.DMA((row_count, 10)),
             pltpu.SemaphoreType.DMA((tile_count,)),
             pltpu.SemaphoreType.DMA((tile_count,)),
-        ],
+        ]
+        + (reducer_scratch(starts, shapes) if count else []),
         compiler_params=pltpu.CompilerParams(
-            collective_id=2, has_side_effects=True, vmem_limit_bytes=50 * 1024 * 1024
+            collective_id=2, has_side_effects=True, vmem_limit_bytes=60 * 1024 * 1024
         ),
         name="attend_back",
-    )(cuts, query, attended, grad, lse, conv_in, conv_turned, spread, all_pairs)
+    )(cuts, query, attended, grad, lse, conv_in, conv_turned, spread, all_pairs, *grads)
 
 
 def add_rows(target, first, second, rows):
-    step = 16
-
     def body(i, carry):
-        at = pl.ds(pl.multiple_of(i * step, step), step)
+        at = pl.ds(pl.multiple_of(i * 16, 16), 16)
         target[at, :] = first[at, :] + second[at, :]
         return carry
 
-    lax.fori_loop(0, rows // step, body, 0)
-
-
-def grad_reduce_kernel(shapes, *refs):
-    count = len(shapes)
-    grads = refs[:count]
-    outs = refs[count : 2 * count]
-    rest = refs[2 * count :]
-    own, got, half, quarter, final = [rest[i * count : (i + 1) * count] for i in range(5)]
-    local_sem, send_sem, recv_sem = rest[5 * count :]
+    lax.fori_loop(0, rows // 16, body, 0)
+
+
+def add_four(target, others, rows):
+    def body(i, carry):
+        at = pl.ds(pl.multiple_of(i * 16, 16), 16)
+        total = target[at, :].astype(jnp.float32) + others[0, at, :].astype(jnp.float32)
+        total = total + (others[1, at, :].astype(jnp.float32) + others[2, at, :].astype(jnp.float32))
+        target[at, :] = total.astype(jnp.bfloat16)
+        return carry
+
+    lax.fori_loop(0, rows // 16, body, 0)
+
+
+def chip_peers():
     z, ty, y = lax.axis_index("rows"), lax.axis_index("ty"), lax.axis_index("tx")
     core, x = lax.rem(ty, 2), ty // 2
-    peer_core = (z, x * 2 + 1 - core, y)
-    peer_x = (z, (1 - x) * 2 + core, y)
-    peer_y = (z, ty, 1 - y)
-    peer_xy = (z, (1 - x) * 2 + core, 1 - y)
-    peers_z = [(lax.rem(z + k, 4), ty, y) for k in (1, 2, 3)]
-    barrier = pltpu.get_barrier_semaphore()
-    everyone = [peer_core, peer_x, peer_y, peer_xy] + peers_z
-    for peer in everyone:
-        pl.semaphore_signal(barrier, inc=1, device_id=peer, device_id_type=MESH)
-    pl.semaphore_wait(barrier, len(everyone))
-
-    def send(w, slot, source, target, peer):
-        return pltpu.make_async_remote_copy(
+    across = (1 - x) * 2 + core
+    return {
+        "core": (z, x * 2 + 1 - core, y),
+        "x": (z, across, y),
+        "y": (z, ty, 1 - y),
+        "xy": (z, across, 1 - y),
+        "z": [(lax.rem(z + k, 4), ty, y) for k in (1, 2, 3)],
+    }
+
+
+class Reducer:
+    def __init__(self, start, grad, out, buffers, sems, w):
+        self.start, self.grad, self.out, self.buffers, self.w = start, grad, out, buffers, w
+        self.local_sem, self.send_sem, self.recv_sem = sems
+        self.z, ty, self.y = lax.axis_index("rows"), lax.axis_index("ty"), lax.axis_index("tx")
+        self.core, self.x = lax.rem(ty, 2), ty // 2
+        self.peers = chip_peers()
+        self.flying = {}
+        self.own = buffers[0]
+        if start in ("plane", "z"):
+            self.got, self.half, self.quarter, self.final = buffers[1:]
+            self.depth, self.width = grad.shape[1], grad.shape[2] // 2
+        else:
+            self.depth, self.width = out.shape[0], out.shape[1] // 2
+        if start == "block":
+            self.half, self.quarter = buffers[1:]
+        late = [self.begin_late, self.add_half_late, self.add_quarter_late, self.pass_strip, self.end]
+        self.stages = {
+            "plane": [self.add_core, self.add_half, self.add_quarter, self.sum_z, self.gather_piece, self.pass_strip, self.end],
+            "z": [self.add_core, self.sum_z_first] + late,
+            "block": late,
+            "piece": [self.gather_piece, self.pass_strip, self.end],
+        }[start]
+
+    def part(self, at):
+        if self.start == "block":
+            return self.own.at[at]
+        return self.own.at[self.z, at]
+
+    def send(self, slot, source, target, peer):
+        copy = pltpu.make_async_remote_copy(
             src_ref=source,
             dst_ref=target,
-            send_sem=send_sem.at[w, slot],
-            recv_sem=recv_sem.at[w, slot],
+            send_sem=self.send_sem.at[self.w, slot],
+            recv_sem=self.recv_sem.at[self.w, slot],
             device_id=peer,
             device_id_type=MESH,
         )
-
-    def columns(w, which):
-        width = shapes[w][2] // 2
-        return pl.ds(pl.multiple_of(which * width, 128), width)
-
-    def rows(start, size):
+        copy.start()
+        return copy
+
+    def keep(self, slot, source, target):
+        copy = pltpu.make_async_copy(source, target, self.local_sem.at[self.w, slot])
+        copy.start()
+        return copy
+
+    def land(self, name):
+        for copy in self.flying.pop(name):
+            copy.wait()
+
+    def columns(self, which):
+        return pl.ds(pl.multiple_of(which * self.width, 128), self.width)
+
+    def rows(self, start, size):
         return pl.ds(pl.multiple_of(start, 16), size)
 
-    def place(w, block):
-        depth = shapes[w][1]
+    def place(self, block):
         later = block // 2
-        major = x + later * (y - x)
-        minor = y + later * (x - y)
-        return rows(major * (depth // 2) + minor * (depth // 4), depth // 4)
-
-    pending = [{} for _ in shapes]
-
-    def begin(w):
-        swap = send(w, 0, grads[w].at[:, :, columns(w, 1 - core)], got[w], peer_core)
-        swap.start()
-        mine = pltpu.make_async_copy(grads[w].at[:, :, columns(w, core)], own[w], local_sem.at[w, 0])
-        mine.start()
-        pending[w].update(swap=swap, mine=mine)
-
-    def stage_core(w):
-        depth = shapes[w][1]
-        pending[w]["mine"].wait()
-        pending[w]["swap"].wait()
+        major = self.x + later * (self.y - self.x)
+        minor = self.y + later * (self.x - self.y)
+        return self.rows(major * (self.depth // 2) + minor * (self.depth // 4), self.depth // 4)
+
+    def begin(self):
+        if self.start in ("block", "piece"):
+            self.flying["load"] = [self.keep(0, self.grad, self.own)]
+            return
+        swap = self.send(0, self.grad.at[:, :, self.columns(1 - self.core)], self.got, self.peers["core"])
+        mine = self.keep(0, self.grad.at[:, :, self.columns(self.core)], self.own)
+        self.flying["core"] = [swap, mine]
+
+    def add_core(self):
+        self.land("core")
         for block in range(4):
-            add_rows(own[w].at[block], own[w].at[block], got[w].at[block], depth)
-        first = send(w, 1, own[w].at[0:2, rows((1 - x) * (depth // 2), depth // 2)], half[w].at[0:2], peer_x)
-        second = send(w, 2, own[w].at[2:4, rows((1 - y) * (depth // 2), depth // 2)], half[w].at[2:4], peer_y)
-        first.start()
-        second.start()
-        pending[w].update(half=(first, second))
-
-    def stage_half(w):
-        depth = shapes[w][1]
-        for copy in pending[w]["half"]:
-            copy.wait()
+            add_rows(self.own.at[block], self.own.at[block], self.got.at[block], self.depth)
+        if self.start == "z":
+            self.flying["z"] = [
+                self.send(5 + k, self.own.at[peer[0]], self.final.at[k], peer) for k, peer in enumerate(self.peers["z"])
+            ]
+            return
+        part = self.depth // 2
+        first = self.send(1, self.own.at[0:2, self.rows((1 - self.x) * part, part)], self.half.at[0:2], self.peers["x"])
+        second = self.send(2, self.own.at[2:4, self.rows((1 - self.y) * part, part)], self.half.at[2:4], self.peers["y"])
+        self.flying["half"] = [first, second]
+
+    def add_half(self):
+        self.land("half")
+        part, less = self.depth // 2, self.depth // 4
         for block in range(4):
-            side = x if block < 2 else y
-            kept = own[w].at[block, rows(side * (depth // 2), depth // 2)]
-            add_rows(kept, kept, half[w].at[block], depth // 2)
-        first = send(w, 3, own[w].at[0:2, rows(x * (depth // 2) + (1 - y) * (depth // 4), depth // 4)], quarter[w].at[0:2], peer_y)
-        second = send(w, 4, own[w].at[2:4, rows(y * (depth // 2) + (1 - x) * (depth // 4), depth // 4)], quarter[w].at[2:4], peer_x)
-        first.start()
-        second.start()
-        pending[w].update(quarter=(first, second))
-
-    def stage_quarter(w):
-        depth = shapes[w][1]
-        for copy in pending[w]["quarter"]:
-            copy.wait()
+            side = self.x if block < 2 else self.y
+            kept = self.own.at[block, self.rows(side * part, part)]
+            add_rows(kept, kept, self.half.at[block], part)
+        first = self.own.at[0:2, self.rows(self.x * part + (1 - self.y) * less, less)]
+        second = self.own.at[2:4, self.rows(self.y * part + (1 - self.x) * less, less)]
+        self.flying["quarter"] = [
+            self.send(3, first, self.quarter.at[0:2], self.peers["y"]),
+            self.send(4, second, self.quarter.at[2:4], self.peers["x"]),
+        ]
+
+    def add_quarter(self):
+        self.land("quarter")
         for block in range(4):
-            kept = own[w].at[block, place(w, block // 2 * 2)]
-            add_rows(kept, kept, quarter[w].at[block], depth // 4)
+            kept = self.own.at[block, self.place(block // 2 * 2)]
+            add_rows(kept, kept, self.quarter.at[block], self.depth // 4)
+        self.flying["z"] = [
+            self.send(5 + k, self.own.at[peer[0], self.place(peer[0])], self.final.at[k], peer)
+            for k, peer in enumerate(self.peers["z"])
+        ]
+
+    def gather(self, pieces, sources):
         copies = []
-        for k, peer in enumerate(peers_z):
-            block = peer[0]
-            copy = send(w, 5 + k, own[w].at[block, place(w, block)], final[w].at[k], peer)
-            copy.start()
-            copies.append(copy)
-        pending[w].update(final=copies)
-
-    def stage_final(w):
-        depth = shapes[w][1]
-        for copy in pending[w]["final"]:
-            copy.wait()
-        kept = own[w].at[z, place(w, z)]
-        total = final[w].at[0]
-
-        def body(i, carry):
-            at = pl.ds(pl.multiple_of(i * 16, 16), 16)
-            parts = [ref[at, :].astype(jnp.float32) for ref in (kept, total, final[w].at[1], final[w].at[2])]
-            total[at, :] = (parts[0] + parts[1] + (parts[2] + parts[3])).astype(jnp.bfloat16)
-            return carry
-
-        lax.fori_loop(0, depth // 64, body, 0)
-        target = outs[w].at[place(w, z), columns(w, core)]
-        copies = []
-        for k, peer in enumerate((peer_x, peer_y, peer_xy)):
-            copy = send(w, 8 + k, total, target, peer)
-            copy.start()
-            copies.append(copy)
-        keep = pltpu.make_async_copy(total, target, local_sem.at[w, 1])
-        keep.start()
-        pending[w].update(gather=copies, keep=keep)
-
-    def stage_gather(w):
-        for copy in pending[w]["gather"]:
-            copy.wait()
-        pending[w]["keep"].wait()
-        strip = outs[w].at[:, columns(w, core)]
-        copy = send(w, 11, strip, strip, peer_core)
-        copy.start()
-        pending[w].update(strip=copy)
-
-    def stage_strip(w):
-        pending[w]["strip"].wait()
-
-    for w in range(count):
-        begin(w)
-    stages = [stage_core, stage_half, stage_quarter, stage_final, stage_gather, stage_strip]
-    for tick in range(count + len(stages) - 1):
-        for depth_index in reversed(range(len(stages))):
-            w = tick - depth_index
-            if 0 <= w < count:
-                stages[depth_index](w)
-
-
-def grad_reduce(grads):
-    shapes = tuple(entry.shape for entry in grads)
-    count = len(shapes)
-    low = jnp.bfloat16
-    scratch = (
-        [pltpu.VMEM((s[0], s[1], s[2] // 2), low) for s in shapes]
-        + [pltpu.VMEM((s[0], s[1], s[2] // 2), low) for s in shapes]
-        + [pltpu.VMEM((s[0], s[1] // 2, s[2] // 2), low) for s in shapes]
-        + [pltpu.VMEM((s[0], s[1] // 4, s[2] // 2), low) for s in shapes]
-        + [pltpu.VMEM((3, s[1] // 4, s[2] // 2), low) for s in shapes]
-        + [
-            pltpu.SemaphoreType.DMA((count, 2)),
-            pltpu.SemaphoreType.DMA((count, 12)),
-            pltpu.SemaphoreType.DMA((count, 12)),
+        for n, (at, source) in enumerate(zip(pieces, sources)):
+            target = self.out.at[at, self.columns(self.core)]
+            for k, name in enumerate(("x", "y", "xy")):
+                copies.append(self.send(8 + 3 * n + k, source, target, self.peers[name]))
+            copies.append(self.keep(1 + n, source, target))
+        self.flying["gather"] = copies
+
+    def sum_z(self):
+        self.land("z")
+        add_four(self.own.at[self.z, self.place(self.z)], self.final, self.depth // 4)
+
+    def gather_piece(self):
+        if self.start == "piece":
+            self.land("load")
+            self.gather([self.place(self.z)], [self.own])
+        else:
+            self.gather([self.place(self.z)], [self.own.at[self.z, self.place(self.z)]])
+
+    def sum_z_first(self):
+        self.land("z")
+        add_four(self.own.at[self.z], self.final, self.depth)
+
+    def save(self):
+        source = self.own.at[self.z] if self.start == "z" else self.own.at[self.z, self.place(self.z)]
+        self.flying["save"] = [self.keep(1, source, self.out)]
+
+    def begin_late(self):
+        if self.start == "block":
+            self.land("load")
+        half, less = self.depth // 2, self.depth // 4
+        self.flying["half"] = [
+            self.send(1, self.part(self.rows((1 - self.x) * less, less)), self.half.at[0], self.peers["x"]),
+            self.send(2, self.part(self.rows(half + (1 - self.y) * less, less)), self.half.at[1], self.peers["y"]),
         ]
-    )
-    return pl.pallas_call(
-        functools.partial(grad_reduce_kernel, shapes),
-        out_shape=[jax.ShapeDtypeStruct(s[1:], low) for s in shapes],
-        in_specs=[pl.BlockSpec(memory_space=pl.ANY)] * count,
-        out_specs=[pl.BlockSpec(memory_space=pl.ANY)] * count,
-        scratch_shapes=scratch,
-        compiler_params=pltpu.CompilerParams(collective_id=3, has_side_effects=True, vmem_limit_bytes=56 * 1024 * 1024),
-        name="grad_reduce",
-    )(*grads)
+
+    def add_half_late(self):
+        self.land("half")
+        half, less, least = self.depth // 2, self.depth // 4, self.depth // 8
+        for n, start in enumerate((self.x * less, half + self.y * less)):
+            kept = self.part(self.rows(start, less))
+            add_rows(kept, kept, self.half.at[n], less)
+        first = self.part(self.rows(self.x * less + (1 - self.y) * least, least))
+        second = self.part(self.rows(half + self.y * less + (1 - self.x) * least, least))
+        self.flying["quarter"] = [
+            self.send(3, first, self.quarter.at[0], self.peers["y"]),
+            self.send(4, second, self.quarter.at[1], self.peers["x"]),
+        ]
+
+    def add_quarter_late(self):
+        self.land("quarter")
+        half, less, least = self.depth // 2, self.depth // 4, self.depth // 8
+        pieces = [self.rows(self.x * less + self.y * least, least), self.rows(half + self.y * less + self.x * least, least)]
+        for n, at in enumerate(pieces):
+            add_rows(self.part(at), self.part(at), self.quarter.at[n], least)
+        self.gather(pieces, [self.part(at) for at in pieces])
+
+    def pass_strip(self):
+        self.land("gather")
+        strip = self.out.at[:, self.columns(self.core)]
+        self.flying["strip"] = [self.send(14, strip, strip, self.peers["core"])]
+
+    def end(self):
+        self.land("strip")
+
+
+def reducer_scratch(starts, shapes):
+    buffers = []
+    for start, (depth, width) in zip(starts, shapes):
+        half = width // 2
+        sizes = {
+            "plane": [(4, depth, half)] * 2 + [(4, depth // 2, half), (4, depth // 4, half), (3, depth // 4, half)],
+            "z": [(4, depth, half)] * 2 + [(2, depth // 4, half), (2, depth // 8, half), (3, depth, half)],
+            "block": [(depth, half), (2, depth // 4, half), (2, depth // 8, half)],
+            "piece": [(depth // 4, half)],
+        }[start]
+        buffers += [pltpu.VMEM(size, jnp.bfloat16) for size in sizes]
+    count = len(starts)
+    return buffers + [
+        pltpu.SemaphoreType.DMA((count, 3)),
+        pltpu.SemaphoreType.DMA((count, 15)),
+        pltpu.SemaphoreType.DMA((count, 15)),
+    ]
+
+
+def make_reducers(starts, grads, outs, scratch):
+    items, at = [], 0
+    for w, (start, grad, out) in enumerate(zip(starts, grads, outs)):
+        size = {"plane": 5, "z": 5, "block": 3, "piece": 1}[start]
+        items.append(Reducer(start, grad, out, scratch[at : at + size], scratch[-3:], w))
+        at = at + size
+    return items
 
 
 def sum_by_table(local_grads):
@@ -1030,31 +1213,41 @@
         cuts, attended.reshape(token_count, width), stream, cot_tiles, proj_weight, conv_turned, vectors,
         hidden_bias, fc1_weight, fc2_weight, tile_height, tile_width,
     )
-    projected_grad, conv_grad, conv_out = attend_back(
+    here = (lax.axis_size("rows"), lax.axis_size("ty"), lax.axis_size("tx")) == (4, 4, 2)
+
+    def in_blocks(grads):
+        return [entry.reshape(4, -1, entry.shape[1]) for entry in grads]
+
+    early = [("plane", fc1_grad), ("z", fc2_grad), ("plane", proj_grad)] if here else []
+    projected_grad, conv_grad, conv_out, *saved = attend_back(
         cuts, query, attended, attended_grad.reshape(row_count, tokens, width), log_total,
-        conv_in, conv_turned, spread, row_pairs, tile_height, tile_width,
+        conv_in, conv_turned, spread, row_pairs, list(zip([start for start, _ in early], in_blocks([g for _, g in early]))),
+        tile_height, tile_width,
     )
-    qkv_grad, skip_grad, skip_input_grad, thin, flat = rear(
+    follow = {"plane": "piece", "z": "block"}
+    resumed = [
+        (follow[start], entry, (grad.shape[0] // 4, grad.shape[1])) for (start, grad), entry in zip(early, saved)
+    ]
+    skip_input_grad, *rest = rear(
         projected_grad.reshape(token_count, 3 * width), qkv_weight, normed, stream, mid_grad, embedded, flat_skip,
-        flat_latent, skip_weight, vectors, middle_grads, hidden_bias_grad.reshape(4, -1), conv_grad,
+        skip_weight, flat_latent, vectors, middle_grads, hidden_bias_grad.reshape(4, -1), conv_grad, resumed, here,
     )
     output = conv_out.transpose(0, 2, 1).reshape(row_count, tile_height, tile_width, patch)
     skip_input_grad = skip_input_grad.reshape(row_count, tile_height, tile_width, width)
     taps = 9 * patch
     share = width // 4
-    mesh_shape = (lax.axis_size("rows"), lax.axis_size("ty"), lax.axis_size("tx"))
-    if mesh_shape == (4, 4, 2):
-        local = [proj_grad, fc1_grad, fc2_grad, qkv_grad, skip_grad, thin]
-        summed = grad_reduce([entry.reshape(4, -1, entry.shape[1]) for entry in local] + [flat])
-        proj_total, fc1_total, fc2_total, qkv_total, skip_total = [entry.astype(wide) for entry in summed[:5]]
-        conv_total = summed[5][:, :taps].astype(wide)
-        embed_total = summed[5][:, taps : taps + patch].astype(wide)
-        line = [summed[6][k, :share].astype(wide) for k in range(8)]
-        fc1_line = summed[6][8:11].reshape(-1).astype(wide)
+    if here:
+        fc1_total, fc2_total, proj_total, qkv_total, skip_total = [entry.astype(wide) for entry in rest[:5]]
+        conv_total = rest[5][:, :taps].astype(wide)
+        embed_total = rest[5][:, taps : taps + patch].astype(wide)
+        line = [rest[6][k, :share].astype(wide) for k in range(8)]
+        fc1_line = rest[6][8:11].reshape(-1).astype(wide)
         return (
             output, skip_input_grad, embed_total, line[0], skip_total, line[1], line[2], line[3], qkv_total,
             proj_total, line[4], line[5], line[6], fc1_total, fc1_line, fc2_total, line[7], conv_total,
         )
+    qkv_grad, skip_grad, thin = [entry.reshape(-1, entry.shape[2]) for entry in rest[:3]]
+    flat = rest[3]
     line = [flat[:, k, :share].reshape(-1) for k in range(8)]
     fc1_line = flat[:, 8:11].reshape(-1)
     local_grads = [

time: 334 us -> 290 us (0.87)
  Pallas kernels: 275 us -> 240 us
  local copies, waits for them, and re-layouts: 41.2 us -> 30.5 us
    pallas_call x2 -> x1, Pallas kernels: 127 us -> 69.1 us  [rear(): pl.pallas_call(functools.partial(rear_kernel, starts, reduces), out_shape...]
    pallas_call x1, Pallas kernels: 61.5 us -> 86.6 us  [attend_back(): pl.pallas_call(functools.partial(attend_back_kernel, tile_height, tile_wi...]
    unnamed x70 -> x61, local copies, waits for them, and re-layouts: 33.2 us -> 22.6 us
where the time goes in v4:
time: 290 us; the launch traced here: 286 us
  Pallas kernels  240 us (83%)
  local copies, waits for them, and re-layouts  30.5 us (11%)
  other arithmetic  14.3 us (5%)
    pallas_call x1, Pallas kernels, attend_back(): pl.pallas_call(functools.partial(attend_back_kernel, tile_height, tile_wi...  86.6 us
    pallas_call x1, Pallas kernels, rear(): pl.pallas_call(functools.partial(rear_kernel, starts, reduces), out_shape...  69.1 us
    pallas_call x1, Pallas kernels, attend(): pl.pallas_call(functools.partial(attend_kernel, tile_height, tile_width),...  52.3 us
    pallas_call x1, Pallas kernels, middle(): pl.pallas_call(functools.partial(middle_kernel, tile_height, tile_width),...  28.5 us
    unnamed x61, local copies, waits for them, and re-layouts  22.6 us
    convert_element_type x5, other arithmetic, shards(): entry.astype(wide)  7.47 us

profile of v4, /device:TPU:0, one launch (start us, length us, event | category | flops | bytes accessed | tf_op | source)
XLA Modules:
  0.0 286.2 jit_solution(9273569219608033314)
XLA Ops:
  0.7 1.0 convert_reduce_fusion
  1.7 0.9 fusion
  2.5 0.1 copy.38
  2.6 0.1 copy.39
  2.7 0.1 pad_add_fusion.cuts
  2.8 0.7 stack.39
  3.5 0.7 stack.40
  4.2 0.7 stack.41
  4.9 0.7 stack.42
  5.6 0.7 stack.43
  6.3 0.7 stack.44
  6.9 0.7 stack.45
  7.6 0.7 stack.46
  8.4 0.0 copy-start.17
  8.4 0.7 reshape.116
  9.1 1.0 copy.45
  10.0 0.9 copy.40.embed_weight
  11.0 0.0 copy-start
  11.0 2.0 copy-done
  13.0 1.7 copy-done.2
  14.6 1.1 copy-done.6
  15.7 0.9 copy-done.16
  16.6 3.6 %front.1 = (bf16[384,768]{1,0:T(8,128)(2,1)S(1)}, f32[384,768]{1,0:T(8,128)S(1)}, bf16[384,768]{1,0:T(8,128)(2,1)S(1)}, bf16[3,128,768]{2,1,0:T(8,128)(2,1)S(1)}, bf16[3,128,1536]{2,1,0:T(8,128)(2,1)S(1)}) custom-call(bf16[384,16]{1,0:T(8,128)(2,1)S(1)} %bitcast.34, bf16[384,768]{1,0:T(8,128)(2,1)S(1)} %bitcast.28, bf16[768,16]{1,0:T(8,128)(2,1)S(1)} %copy.40.embed_weight, ...), custom_call_target="tpu_custom_call" | custom-call | tf_op jit(solution)/shard_map/front/pallas_call | solution.py:99
  20.2 0.0 copy-start.12
  20.2 0.8 copy-done.12
  21.1 0.8 copy-done.13
  21.9 52.3 %attend.1 = (bf16[3,128,768]{2,1,0:T(8,128)(2,1)S(1)}, f32[3,6,1,256]{3,2,1,0:T(1,128)S(1)}, bf16[3,8,128,1536]{3,2,1,0:T(8,128)(2,1)S(1)}, bf16[8,3,16,128]{3,2,1,0:T(8,128)(2,1)S(1)}) custom-call(s32[3,2]{1,0:T(4,128)S(1)} %pad_add_fusion.cuts, bf16[3,128,768]{2,1,0:T(8,128)(2,1)S(1)} %get-tuple-element.50.query.query_in, ...), custom_call_target="tpu_custom_call" | custom-call | tf_op jit(solution)/shard_map/attend/pallas_call | solution.py:602
  74.2 0.0 copy-start.1
  74.2 3.6 %copy-done.1 = bf16[3,8,128,1536]{3,2,1,0:T(8,128)(2,1)} copy-done((bf16[3,8,128,1536]{3,2,1,0:T(8,128)(2,1)}, bf16[3,8,128,1536]{3,2,1,0:T(8,128)(2,1)S(1)}, u32[]{:S(2)}) %copy-start.1) | copy-done | bytes 9437208
  77.9 0.6 copy-done.21
  78.5 0.0 copy-done.19
  78.5 0.0 copy-done.17
  78.5 0.0 copy-done.10
  78.5 0.0 copy-done.11
  78.5 28.5 %middle.1 = (bf16[768,3072]{1,0:T(8,128)(2,1)S(1)}, bf16[3072,768]{1,0:T(8,128)(2,1)}, f32[6,1,512]{2,1,0:T(1,128)S(1)}, bf16[768,768]{1,0:T(8,128)(2,1)S(1)}, b...) custom-call(s32[3,2]{1,0:T(4,128)S(1)} %pad_add_fusion.cuts, ...), custom_call_target="tpu_custom_call" | custom-call | tf_op jit(solution)/shard_map/middle/pallas_call | solution.py:218
  107.0 0.0 copy-done.3
  107.0 0.0 copy-done.7
  107.0 0.0 copy-done.5
  107.0 0.0 copy-start.4
  107.0 2.2 copy-done.4
  109.2 1.0 copy-done.8
  110.2 1.0 copy-done.9
  111.2 0.8 copy-done.14
  112.0 0.8 copy-done.15
  112.9 0.6 copy-done.18
  113.5 0.6 copy-done.20
  114.1 86.6 %attend_back.1 = (bf16[3,128,2304]{2,1,0:T(8,128)(2,1)}, f32[768,144]{1,0:T(8,128)}, bf16[3,16,128]{2,1,0:T(8,128)(2,1)}, bf16[48,1536]{1,0:T(8,128)(2,1)}, bf16...) custom-call(s32[3,2]{1,0:T(4,128)} %copy-done.19, bf16[3,128,768]{2,1,0:T(8,128)(2,1)} %copy-done.7, ...), custom_call_target="tpu_custom_call" | custom-call | tf_op jit(solution)/shard_map/attend_back/pallas_call | solution.py:858
  200.8 0.6 reshape.114.hidden_bias_grad
  201.4 69.1 %rear.1 = (bf16[384,768]{1,0:T(8,128)(2,1)}, bf16[192,3072]{1,0:T(8,128)(2,1)}, bf16[768,768]{1,0:T(8,128)(2,1)}, bf16[192,768]{1,0:T(8,128)(2,1)}, bf16[192,230...) custom-call(bf16[384,2304]{1,0:T(8,128)(2,1)} %bitcast.38, ...), custom_call_target="tpu_custom_call" | custom-call | tf_op jit(solution)/shard_map/rear/pallas_call | solution.py:386
  270.5 0.7 slice_convert_fusion.2
  271.3 1.6 slice_convert_fusion.3
  272.8 0.6 reshape.125
  273.4 0.8 copy.46
  274.2 1.0 slice_convert_fusion.1
  275.1 0.7 copy.43
  275.8 0.9 slice_convert_fusion
  276.7 0.8 copy.44
  277.5 1.8 convert_element_type.101
  279.3 1.1 convert_element_type.93
  280.4 0.0 copy-done.24
  280.4 1.3 convert_element_type.100
  281.7 1.7 convert_element_type.108
  283.4 1.6 convert_element_type.111
  285.0 0.8 copy.48
  (31 shorter events, 0.1 us)
Async XLA Ops:
  2.8 75.6 %copy-start.19 = (s32[3,2]{1,0:T(4,128)}, s32[3,2]{1,0:T(4,128)S(1)}, u32[]{:S(2)}) copy-start(s32[3,2]{1,0:T(4,128)S(1)} %pad_add_fusion.cuts) | copy-start | bytes 76
  8.4 70.1 %copy-start.17 = (f32[8,768]{1,0:T(8,128)}, f32[8,768]{1,0:T(8,128)S(1)}, u32[]{:S(2)}) copy-start(f32[8,768]{1,0:T(8,128)S(1)} %convert_element_type.89.vectors) | copy-start | bytes 73732
  11.0 2.0 copy-start
  13.0 1.7 copy-start.2
  14.6 1.1 copy-start.6
  15.7 0.9 copy-start.16
  20.2 0.8 copy-start.12
  21.1 0.8 copy-start.13
  21.9 85.1 %copy-start.3 = (f32[384,768]{1,0:T(8,128)}, f32[384,768]{1,0:T(8,128)S(1)}, u32[]{:S(2)}) copy-start(f32[384,768]{1,0:T(8,128)S(1)} %get-tuple-element.53.stream.stream_in) | copy-start | bytes 3538948
  21.9 85.1 %copy-start.7 = (bf16[3,128,768]{2,1,0:T(8,128)(2,1)}, bf16[3,128,768]{2,1,0:T(8,128)(2,1)S(1)}, u32[]{:S(2)}) copy-start(bf16[3,128,768]{2,1,0:T(8,128)(2,1)S(1)} %get-tuple-element.50.query.query_in) | copy-start | bytes 1769476
  21.9 56.5 %copy-start.10 = (bf16[768,768]{1,0:T(8,128)(2,1)S(1)}, bf16[768,768]{1,0:T(8,128)(2,1)}, u32[]{:S(2)}) copy-start(bf16[768,768]{1,0:T(8,128)(2,1)} %proj_weight.1) | copy-start | bytes 3538948
  21.9 56.5 %copy-start.11 = (bf16[768,144]{0,1:T(8,128)(2,1)S(1)}, bf16[768,144]{0,1:T(8,128)(2,1)}, u32[]{:S(2)}) copy-start(bf16[768,144]{0,1:T(8,128)(2,1)} %param.38) | copy-start | bytes 663556
  74.2 3.7 %copy-start.1 = (bf16[3,8,128,1536]{3,2,1,0:T(8,128)(2,1)}, bf16[3,8,128,1536]{3,2,1,0:T(8,128)(2,1)S(1)}, u32[]{:S(2)}) copy-start(bf16[3,8,128,1536]{3,2,1,0:T(8,128)(2,1)S(1)} %get-tuple-element.59.all_pairs) | copy-start | bytes 28311556
  77.9 0.6 copy-start.21
  78.5 28.5 %copy-start.5 = (bf16[3,128,768]{2,1,0:T(8,128)(2,1)}, bf16[3,128,768]{2,1,0:T(8,128)(2,1)S(1)}, u32[]{:S(2)}) copy-start(bf16[3,128,768]{2,1,0:T(8,128)(2,1)S(1)} %get-tuple-element.52.attended_in) | copy-start | bytes 1769476
  107.0 2.2 copy-start.4
  109.2 1.0 copy-start.8
  110.2 1.0 copy-start.9
  111.2 0.8 copy-start.14
  112.0 0.8 copy-start.15
  112.9 0.6 copy-start.18
  113.5 0.6 copy-start.20
  201.4 72.0 %copy-start.27 = (bf16[3,16,128]{2,1,0:T(8,128)(2,1)S(1)}, bf16[3,16,128]{2,1,0:T(8,128)(2,1)}, u32[]{:S(2)}) copy-start(bf16[3,16,128]{2,1,0:T(8,128)(2,1)} %get-tuple-element.63) | copy-start | bytes 36868
  270.5 8.8 %copy-start.25 = (bf16[384,768]{1,0:T(8,128)(2,1)S(1)}, bf16[384,768]{1,0:T(8,128)(2,1)}, u32[]{:S(2)}) copy-start(bf16[384,768]{1,0:T(8,128)(2,1)} %get-tuple-element.77) | copy-start | bytes 1769476
  274.2 6.2 %copy-start.24 = (bf16[192,2304]{1,0:T(8,128)(2,1)S(1)}, bf16[192,2304]{1,0:T(8,128)(2,1)}, u32[]{:S(2)}) copy-start(bf16[192,2304]{1,0:T(8,128)(2,1)} %get-tuple-element.78) | copy-start | bytes 2654212
  279.3 2.4 copy-start.23
  281.7 1.7 copy-start.22
  283.4 1.6 copy-start.26
